TPU v7x, 512 devices: a whole 4x8x8 slice. The times are simulated.
512 devices in a mesh: row: 16 (over x, y_hi, core), col: 32 (over y_lo, z).
Axes of the slice: x: 4, y: 8 (y_hi: 2, y_lo: 4; y = y_hi * 4 + y_lo), z: 8, core: 2. Of those that a mesh axis runs over, the one named last changes fastest.
Arguments:
- resident: float32 [12288, 12288], P('row', 'col')
- factor: float32 [1, 12288, 512], P(None, 'col', 'row'), may hold values from -0.078125 to 0.078125
- dinv: float32 [1, 512, 512], P(None, 'col')
- panel_cols: int32 [1, 512], replicated, may hold values from 0 to 12287, as said below
- row_lists: int32 [1, 6144], replicated, may hold values from 0 to 12287, as said below
Outputs:
- inverse_out: float32 [12288, 12288], P('row', 'col')
Inputs may be any that keep to these rules, and one draw needn't show every extreme that they name: The entries of panel_cols are distinct positions. The resident array and every dinv[k] are symmetric. Each row_lists[k] holds distinct positions, none of them in panel_cols[j] for any j <= k.
All inputs are finite; a program needn't handle non-finite values.
Results may differ from a plain program's by a relative error of at most 0.0001.
Values sent between devices are 32-bit elements; how exact they have to be, the bound alone decides.
No kernel may reach another device: no remote copies, remote signals or barrier semaphores. Data moves between devices by JAX's collectives and lax.ppermute only.
A program may use at most 64 MiB of HBM per device.

v0:
```python
import jax
import jax.numpy as jnp
from jax import lax
from jax.sharding import Mesh
from jax.sharding import PartitionSpec as P

ROW = ("row_0", "row_1", "row_2")


def split_up(shard, dim, count):
    shape = shard.shape
    blocks = shard.reshape(*shape[:dim], count, shape[dim] // count, *shape[dim + 1 :])
    return jnp.moveaxis(blocks, dim, 0)


def sum_at_owner(shard, axis, dim):
    count = lax.axis_size(axis)
    blocks = lax.all_to_all(split_up(shard, dim, count), axis, 0, 0, tiled=True)
    return jnp.sum(blocks, axis=0)


def in_order(blocks, dim):
    shape = list(blocks.shape[1:])
    shape[dim] *= blocks.shape[0]
    return jnp.moveaxis(blocks, 0, dim).reshape(shape)


def sent_to_all(shard, axis):
    copies = jnp.broadcast_to(shard, (lax.axis_size(axis), *shard.shape))
    return lax.all_to_all(copies, axis, split_axis=0, concat_axis=0, tiled=True)


def gathered_copies(shard, axis, dim):
    return in_order(sent_to_all(shard, axis), dim)


def padded_to(lines, count):
    spare = -len(lines) % count
    return jnp.pad(lines, [(0, spare)] + [(0, 0)] * (lines.ndim - 1))


def gather_axes(shard, axes, dim):
    far, near = axes
    initial = sent_to_all(shard, far)
    blocks = jnp.swapaxes(sent_to_all(initial, near), 0, 1)
    return in_order(blocks.reshape(-1, *shard.shape), dim)


def summed_rows(shard, axes, dim):
    far, near = axes
    blocks = split_up(shard, dim, lax.axis_size(far))
    nearer = sum_at_owner(blocks, near, dim + 1)
    arrived = lax.all_to_all(nearer, far, split_axis=0, concat_axis=0, tiled=True)
    return arrived.sum(axis=0)


def sum_by_parts(shard, axes):
    lines = shard.reshape(-1, shard.shape[-1])
    padded = padded_to(lines, lax.axis_size(axes[0]) * lax.axis_size(axes[1]))
    whole = gather_axes(summed_rows(padded, axes, 0), axes, 0)
    return lax.slice_in_dim(whole, 0, len(lines)).reshape(shard.shape)


def sum_by_parts_2(shard, axes):
    lines = shard.reshape(-1, shard.shape[-1])
    own = sum_at_owner(padded_to(lines, lax.axis_size(axes)), axes, 0)
    whole = gathered_copies(own, axes, 0)
    return whole[: len(lines)].reshape(shard.shape)


def on_device(resident, factor, dinv, panel_cols, row_lists):
    highest = lax.Precision.HIGHEST
    row_count = lax.axis_size(ROW)
    col_count = lax.axis_size("col")
    ratio = col_count // row_count
    row_block, col_block = resident.shape
    total = row_block * row_count
    width = panel_cols.shape[1]
    dinv_rows = dinv.shape[1]
    row_pos = lax.axis_index(ROW)
    col_pos = lax.axis_index("col")
    row_ids = row_pos * row_block + jnp.arange(row_block, dtype=jnp.int32)
    col_ids = col_pos * col_block + jnp.arange(col_block, dtype=jnp.int32)
    matrix = resident
    for panel in reversed(range(factor.shape[0])):
        in_rows = jnp.zeros((total,), jnp.float32).at[row_lists[panel]].set(1.0)
        panel_map = (
            jnp.full((total,), -1, jnp.int32)
            .at[panel_cols[panel]]
            .set(jnp.arange(width, dtype=jnp.int32))
        )
        col_mask = in_rows[col_ids]
        gathered = lax.all_gather(factor[panel], ROW, axis=1, tiled=True)
        lower_cols = gathered * col_mask[:, None]
        partial_value = jnp.dot(matrix, lower_cols, precision=highest)
        shares = sum_at_owner(-partial_value, "col", 0)
        product_rows = gathered_copies(shares, "col", 0)
        owner = col_pos // ratio
        offset = col_pos % ratio * col_block
        mine = lax.dynamic_slice_in_dim(product_rows, offset, col_block, 0)
        masked = jnp.where(row_pos == owner, mine, jnp.zeros_like(mine))
        product_cols = sum_by_parts(masked, (("row_0", "row_1"), "row_2"))
        placed = lax.dynamic_update_slice(
            jnp.zeros((width, width), jnp.float32), dinv[panel], (col_pos * dinv_rows, 0)
        )
        gram_term = jnp.dot(lower_cols.T, product_cols, precision=highest)
        diagonal = sum_by_parts_2(placed - gram_term, "col")
        row_slot = panel_map[row_ids]
        col_slot = panel_map[col_ids]
        row_safe = jnp.maximum(row_slot, 0)
        col_safe = jnp.maximum(col_slot, 0)
        row_in = in_rows[row_ids] > 0.5
        col_in = col_mask > 0.5
        row_panel = row_slot >= 0
        col_panel = col_slot >= 0
        below = jnp.take(product_rows, col_safe, axis=1)
        beside = jnp.take(product_cols, row_safe, axis=1).T
        corner = jnp.take(jnp.take(diagonal, row_safe, axis=0), col_safe, axis=1)
        matrix = jnp.where(
            row_panel[:, None] & col_panel[None, :],
            corner,
            jnp.where(
                row_panel[:, None] & col_in[None, :],
                beside,
                jnp.where(row_in[:, None] & col_panel[None, :], below, matrix),
            ),
        )
    return matrix


def solution(mesh):
    finer = Mesh(
        mesh.devices.reshape(4, 2, 2, mesh.shape["col"]), ("row_0", "row_1", "row_2", "col")
    )
    return jax.shard_map(
        on_device,
        mesh=finer,
        in_specs=(P(ROW, "col"), P(None, "col", ROW), P(None, "col", None), P(), P()),
        out_specs=P(ROW, "col"),
        check_vma=False,
    )
```

profile of v0, /device:TPU:16, one launch (start us, length us, event | category | flops | bytes accessed | tf_op | source)
XLA Modules:
  0.0 302.5 jit_solution(6073321219527905925)
XLA Ops:
  0.0 0.8 compare_select_fusion
  0.8 33.7 %all-gather = f32[1,384,512]{1,2,0:T(8,128)S(1)} all-gather(f32[1,384,32]{1,2,0:T(8,128)} %param.8), channel_id=2, replica_groups=mesh['row_0'=4,'row_1'=2,'row_2'=2,'col'=32] {'row_0','row_1','row_2'}, dimensions={2}, use_global_device_ids=true | all-gather | bytes 835584 | tf_op jit(solution)/shard_map/all_gather | solution.py:93
  34.5 23.0 %scatter_custom_fusion.1 = f32[12288]{0:T(1024)S(1)} fusion(s32[6144]{0:T(1024)S(1)} %bitcast.42, f32[6144]{0:T(1024)S(1)} %broadcast.138, f32[]{:T(128)} %constant.105.clone.1), kind=kCustom, calls=%fused_computation.22 | custom fusion | bytes 49156 | tf_op jit(solution)/shard_map/scatter | solution.py:86
  57.5 2.5 gather_fusion.2
  60.1 3.9 %negate_bitcast_fusion = f32[768,512]{0,1:T(8,128)} fusion(f32[768,384]{1,0:T(8,128)S(1)} %copy-done.1, f32[1,384,512]{1,2,0:T(8,128)S(1)} %all-gather, f32[384]{0:T(512)S(1)} %gather_fusion.2), kind=kOutput, calls=%fused_computation.10 | convolution fusion | flops 1812529152 | bytes 3540480 | tf_op jit(solution)/shard_map/dot_general | solution.py:95
  63.9 1.9 copy.26
  65.8 58.1 %all_to_all.40 = f32[32,24,512]{2,1,0:T(8,128)} all-to-all(f32[32,24,512]{2,1,0:T(8,128)S(1)} %bitcast.39), channel_id=1, replica_groups=mesh['row_0'=4,'row_1'=2,'row_2'=2,'col'=32] {'col'}, dimensions={0} | all-to-all | bytes 3145728 | tf_op jit(solution)/shard_map/all_to_all | solution.py:18
  123.9 1.5 reduce_sum.36
  125.4 1.3 broadcast_in_dim.74
  126.8 6.6 %all-to-all-start.1 = ((f32[32,24,512]{2,1,0:T(8,128)}), f32[32,24,512]{2,1,0:T(8,128)S(1)}, u32[]{:S(2)}, u32[]{:S(2)}) async-start(f32[32,24,512]{2,1,0:T(8,128)} %broadcast_in_dim.74), calls=%async_computation.1 | async-start | bytes 3145728 | tf_op jit(solution)/shard_map/all_to_all | solution.py:30
  133.4 39.3 %all-to-all-done.1 = f32[32,24,512]{2,1,0:T(8,128)S(1)} async-done(((f32[32,24,512]{2,1,0:T(8,128)}), f32[32,24,512]{2,1,0:T(8,128)S(1)}, u32[]{:S(2)}, u32[]{:S(2)}) %all-to-all-start.1) | async-done | bytes 1572896 | tf_op jit(solution)/shard_map/all_to_all | solution.py:30
  172.7 0.1 dynamic-slice_select_fusion
  172.8 0.1 copy.27
  172.9 1.0 copy-done
  173.9 4.4 %all_to_all.41 = f32[2,8,24,512]{3,2,1,0:T(8,128)S(1)} all-to-all(f32[2,8,24,512]{3,2,1,0:T(8,128)S(1)} %copy.27), channel_id=1, replica_groups=mesh['row_0'=4,'row_1'=2,'row_2'=2,'col'=32] {'row_2'}, dimensions={0} | all-to-all | bytes 1572864 | tf_op jit(solution)/shard_map/all_to_all | solution.py:18
  178.2 0.1 reduce_sum.37
  178.3 20.3 %all_to_all.42 = f32[8,24,512]{2,1,0:T(8,128)S(1)} all-to-all(f32[8,24,512]{2,1,0:T(8,128)S(1)} %reduce_sum.37), channel_id=1, replica_groups=mesh['row_0'=4,'row_1'=2,'row_2'=2,'col'=32] {'row_0','row_1'}, dimensions={0} | all-to-all | bytes 786432 | tf_op jit(solution)/shard_map/all_to_all | solution.py:53
  198.6 0.0 copy-start.4
  198.6 0.8 broadcast_in_dim.76
  199.4 3.5 %all-to-all-start.4 = ((f32[8,24,512]{2,1,0:T(8,128)}), f32[8,24,512]{2,1,0:T(8,128)S(1)}, u32[]{:S(2)}, u32[]{:S(2)}) async-start(f32[8,24,512]{2,1,0:T(8,128)} %broadcast_in_dim.76), calls=%async_computation.4 | async-start | bytes 786432 | tf_op jit(solution)/shard_map/all_to_all | solution.py:30
  202.9 0.1 broadcast_in_dim.71
  203.0 14.7 %all-to-all-done.4 = f32[8,24,512]{2,1,0:T(8,128)S(1)} async-done(((f32[8,24,512]{2,1,0:T(8,128)}), f32[8,24,512]{2,1,0:T(8,128)S(1)}, u32[]{:S(2)}, u32[]{:S(2)}) %all-to-all-start.4) | async-done | bytes 393248 | tf_op jit(solution)/shard_map/all_to_all | solution.py:30
  217.7 0.1 broadcast_in_dim.77
  217.8 4.4 %all_to_all.43 = f32[2,8,24,512]{3,2,1,0:T(8,128)S(1)} all-to-all(f32[2,8,24,512]{3,2,1,0:T(8,128)S(1)} %broadcast_in_dim.77), channel_id=1, replica_groups=mesh['row_0'=4,'row_1'=2,'row_2'=2,'col'=32] {'row_2'}, dimensions={0} | all-to-all | bytes 1572864 | tf_op jit(solution)/shard_map/all_to_all | solution.py:30
  222.2 0.1 copy.28
  222.2 1.8 convolution_subtract_fusion
  224.1 31.9 %all_to_all.44 = f32[32,16,512]{2,1,0:T(8,128)S(1)} all-to-all(f32[32,16,512]{2,1,0:T(8,128)S(1)} %bitcast.40), channel_id=1, replica_groups=mesh['row_0'=4,'row_1'=2,'row_2'=2,'col'=32] {'col'}, dimensions={0} | all-to-all | bytes 2097152 | tf_op jit(solution)/shard_map/all_to_all | solution.py:18
  256.0 0.1 reduce_sum.39
  256.1 1.1 broadcast_in_dim.78
  257.2 6.0 %all-to-all-start.7 = ((f32[32,16,512]{2,1,0:T(8,128)}), f32[32,16,512]{2,1,0:T(8,128)S(1)}, u32[]{:S(2)}, u32[]{:S(2)}) async-start(f32[32,16,512]{2,1,0:T(8,128)} %broadcast_in_dim.78), calls=%async_computation.7 | async-start | bytes 2097152 | tf_op jit(solution)/shard_map/all_to_all | solution.py:30
  263.3 2.6 scatter_custom_fusion
  265.9 2.5 gather_fusion.1
  268.5 4.5 %gather_fusion = s32[768]{0:T(1024)S(1)} fusion(s32[12288]{0:T(1024)S(1)} %scatter_custom_fusion, s32[1024]{0:T(1024)S(1)} %pad_clamp_fusion.3), kind=kCustom, calls=%fused_computation.2 | custom fusion | bytes 9216 | tf_op jit(solution)/shard_map/gather | solution.py:108
  273.0 0.0 copy-start.2
  273.0 4.5 %gather_fusion.5 = f32[768]{0:T(1024)S(1)} fusion(f32[12288]{0:T(1024)S(1)} %scatter_custom_fusion.1, s32[1024]{0:T(1024)S(1)} %pad_clamp_fusion.3), kind=kCustom, calls=%fused_computation.7 | custom fusion | bytes 9216 | tf_op jit(solution)/shard_map/gather | solution.py:112
  277.5 1.4 copy.33
  278.9 1.9 copy.32
  280.8 2.5 gather_fusion.7
  283.3 0.3 copy.30
  283.6 2.1 gather_fusion.4
  285.7 1.4 copy.31
  287.1 3.7 %all-to-all-done.7 = f32[32,16,512]{2,1,0:T(8,128)S(1)} async-done(((f32[32,16,512]{2,1,0:T(8,128)}), f32[32,16,512]{2,1,0:T(8,128)S(1)}, u32[]{:S(2)}, u32[]{:S(2)}) %all-to-all-start.7) | async-done | bytes 1048608 | tf_op jit(solution)/shard_map/all_to_all | solution.py:30
  290.8 3.1 %gather_fusion.3 = f32[768,512]{1,0:T(8,128)} fusion(f32[512,512]{1,0:T(8,128)S(1)} %bitcast.34, s32[1024]{0:T(1024)S(1)} %pad_clamp_fusion.1), kind=kCustom, calls=%fused_computation.5 | custom fusion | bytes 3148800 | tf_op jit(solution)/shard_map/jit(_take)/gather | solution.py:118
  294.0 1.6 broadcast_select_fusion
  295.6 0.5 copy.29
  296.0 2.5 gather_fusion.6
  298.5 2.6 fusion.1
  301.1 1.4 copy.34
  (26 shorter events, 0.2 us)
Async XLA Ops:
  34.5 25.6 %copy-start.1 = (f32[768,384]{1,0:T(8,128)S(1)}, f32[768,384]{1,0:T(8,128)}, u32[]{:S(2)}) copy-start(f32[768,384]{1,0:T(8,128)} %param.7) | copy-start | bytes 3538948
  126.8 46.0 %all-to-all-start.1 = ((f32[32,24,512]{2,1,0:T(8,128)}), f32[32,24,512]{2,1,0:T(8,128)S(1)}, u32[]{:S(2)}, u32[]{:S(2)}) async-start(f32[32,24,512]{2,1,0:T(8,128)} %broadcast_in_dim.74), calls=%async_computation.1 | async-start | bytes 3145728 | tf_op jit(solution)/shard_map/all_to_all | solution.py:30
  172.7 1.2 copy-start
  198.6 4.4 %copy-start.4 = (f32[1,16,512]{2,1,0:T(8,128)S(1)}, f32[1,16,512]{2,1,0:T(8,128)}, u32[]{:S(2)}) copy-start(f32[1,16,512]{2,1,0:T(8,128)} %param.9) | copy-start | bytes 98308
  199.4 18.3 %all-to-all-start.4 = ((f32[8,24,512]{2,1,0:T(8,128)}), f32[8,24,512]{2,1,0:T(8,128)S(1)}, u32[]{:S(2)}, u32[]{:S(2)}) async-start(f32[8,24,512]{2,1,0:T(8,128)} %broadcast_in_dim.76), calls=%async_computation.4 | async-start | bytes 786432 | tf_op jit(solution)/shard_map/all_to_all | solution.py:30
  257.2 6.1 %copy-start.5 = (s32[1,512]{1,0:T(1,128)S(1)}, s32[1,512]{1,0:T(1,128)}, u32[]{:S(2)}) copy-start(s32[1,512]{1,0:T(1,128)} %param.10) | copy-start | bytes 6148
  257.2 33.7 %all-to-all-start.7 = ((f32[32,16,512]{2,1,0:T(8,128)}), f32[32,16,512]{2,1,0:T(8,128)S(1)}, u32[]{:S(2)}, u32[]{:S(2)}) async-start(f32[32,16,512]{2,1,0:T(8,128)} %broadcast_in_dim.78), calls=%async_computation.7 | async-start | bytes 2097152 | tf_op jit(solution)/shard_map/all_to_all | solution.py:30
  273.0 4.5 %copy-start.2 = (f32[768,384]{1,0:T(8,128)S(1)}, f32[768,384]{1,0:T(8,128)}, u32[]{:S(2)}) copy-start(f32[768,384]{1,0:T(8,128)} %param.7) | copy-start | bytes 3538948
  296.0 2.5 copy-start.3
where the time goes:
time: 303 us
  blocking collectives  153 us (50%)
  local copies, waits for them, and re-layouts  63.1 us (21%)
  waiting for transfers between devices  57.8 us (19%)
  starting transfers between devices  16.1 us (5%)
  other arithmetic  6.79 us (2%)
  matrix products  5.68 us (2%)
    all_to_all x3, blocking collectives, sum_at_owner(): blocks = lax.all_to_all(split_up(shard, dim, count), axis, 0, 0, tiled=True)  94.4 us
    all_to_all x3, waiting for transfers between devices, sent_to_all(): return lax.all_to_all(copies, axis, split_axis=0, concat_axis=0, tiled=True)  57.8 us
    all_gather x1, blocking collectives, on_device(): gathered = lax.all_gather(factor[panel], ROW, axis=1, tiled=True)  33.7 us
    scatter x1, local copies, waits for them, and re-layouts, on_device(): in_rows = jnp.zeros((total,), jnp.float32).at[row_lists[panel]].set(1.0)  23 us
    all_to_all x1, blocking collectives, summed_rows(): lax.all_to_all(nearer, far, split_axis=0, concat_axis=0, tiled=True)  20.3 us
    all_to_all x3, starting transfers between devices, sent_to_all(): return lax.all_to_all(copies, axis, split_axis=0, concat_axis=0, tiled=True)  16.1 us
  transfers between devices with their start and end apart: 3, of which 3 were waited for; matrix products, arithmetic and copies ran while one was open for 8% of the time, Pallas kernels for 0%

commit v1 on v0

v1 whole, which is shorter than its diff:
```python
import functools

import jax
import jax.numpy as jnp
from jax import lax
from jax.experimental import pallas as pl
from jax.experimental.pallas import tpu as pltpu
from jax.sharding import Mesh
from jax.sharding import PartitionSpec as P

ROW = ("row_0", "row_1", "row_2")
HIGHEST = lax.Precision.HIGHEST
LANES = 128
LINES = 16
BY_LAST = ((1,), (1,))
BY_FIRST = ((0,), (0,))


def dot(a, b, dims=((1,), (0,))):
    return lax.dot_general(
        a, b, (dims, ((), ())), precision=HIGHEST, preferred_element_type=jnp.float32
    )


def sum_at_owner(blocks, axis):
    return jnp.sum(lax.all_to_all(blocks, axis, 0, 0, tiled=True), axis=0)


def sent_to_all(shard, axis):
    copies = jnp.broadcast_to(shard, (lax.axis_size(axis), *shard.shape))
    return lax.all_to_all(copies, axis, split_axis=0, concat_axis=0, tiled=True)


def ring_sum(shard, axis):
    count = lax.axis_size(axis)
    ring = [(place, (place + 1) % count) for place in range(count)]

    def step(_, carried):
        moving, total = carried
        moving = lax.ppermute(moving, axis, ring)
        return moving, total + moving

    return lax.fori_loop(0, count - 1, step, (shard, shard))[1]


def general_panel(matrix, factor, dinv, panel_cols, row_in, col_in):
    row_count = lax.axis_size(ROW)
    ratio = lax.axis_size("col") // row_count
    row_block, col_block = matrix.shape
    width = panel_cols.shape[0]
    group = factor.shape[1]
    row_pos = lax.axis_index(ROW)
    col_pos = lax.axis_index("col")
    row_ids = row_pos * row_block + jnp.arange(row_block, dtype=jnp.int32)
    col_ids = col_pos * col_block + jnp.arange(col_block, dtype=jnp.int32)
    masked = factor * col_in[:, None].astype(jnp.float32)

    def column_places(turn):
        cols = lax.dynamic_slice_in_dim(panel_cols, turn * group, group)
        return cols, (cols[:, None] == col_ids).astype(jnp.float32)

    def products(turn, carried):
        out, gram = carried
        lower = ring_sum(jnp.where(row_pos == turn, masked, jnp.zeros_like(masked)), ROW)
        by_row = ring_sum(-dot(matrix, lower), "col")
        mine = lax.dynamic_slice_in_dim(by_row, col_pos % ratio * col_block, col_block, 0)
        mine = jnp.where(row_pos == col_pos // ratio, mine, jnp.zeros_like(mine))
        by_col = ring_sum(mine, ROW)
        gram = lax.dynamic_update_slice(
            gram, dot(masked, by_col, BY_FIRST), (row_pos * group, turn * group)
        )
        cols, put_cols = column_places(turn)
        put_rows = (row_ids[:, None] == cols).astype(jnp.float32)
        here = jnp.sum(put_cols, axis=0) > 0.5
        there = jnp.sum(put_rows, axis=1) > 0.5
        out = jnp.where(
            row_in[:, None] & here[None, :],
            dot(by_row, put_cols),
            jnp.where(there[:, None] & col_in[None, :], dot(put_rows, by_col, BY_LAST), out),
        )
        return out, gram

    none = jnp.zeros((width, width), jnp.float32)
    out, gram = lax.fori_loop(0, row_count, products, (matrix, none))
    placed = lax.dynamic_update_slice(none, dinv, (col_pos * dinv.shape[0], 0))
    placed = jnp.where(row_pos == 0, placed, none)
    diagonal = ring_sum(ring_sum(placed - gram, ROW), "col")
    put_rows = (row_ids[:, None] == panel_cols).astype(jnp.float32)
    there = jnp.sum(put_rows, axis=1) > 0.5

    def corners(turn, out):
        _, put_cols = column_places(turn)
        here = jnp.sum(put_cols, axis=0) > 0.5
        part = lax.dynamic_slice_in_dim(diagonal, turn * group, group, 1)
        corner = dot(dot(put_rows, part), put_cols)
        return jnp.where(there[:, None] & here[None, :], corner, out)

    return lax.fori_loop(0, row_count, corners, out)


def slots_kernel(lines, lanes, device_ref, rows_ref, cols_ref, row_slots_ref, col_slots_ref):
    line = lax.broadcasted_iota(jnp.int32, (LINES, 1), 0)
    own = jnp.where(
        line < lines, device_ref[0] * lines + line, device_ref[1] * lines + line - lines
    )
    lower = lax.broadcasted_iota(jnp.int32, (lanes, lanes), 0)
    upper = lax.broadcasted_iota(jnp.int32, (lanes, lanes), 1)
    earlier = (lower < upper).astype(jnp.float32)
    for listed_ref, out_ref in ((rows_ref, row_slots_ref), (cols_ref, col_slots_ref)):
        count = listed_ref.shape[1]
        step = min(count, 1024)
        found = jnp.zeros((LINES, lanes), jnp.float32)
        for start in range(0, count, step):
            size = min(step, count - start)
            listed = listed_ref[:, start : start + size]
            high = lax.div(listed, jnp.int32(lanes))
            low = listed - high * lanes
            line_hit = (own == high).astype(jnp.float32)
            lane_hit = lax.broadcasted_iota(jnp.int32, (lanes, size), 0) == low
            found += lax.dot_general(
                line_hit.astype(jnp.bfloat16),
                lane_hit.astype(jnp.float32).astype(jnp.bfloat16),
                (BY_LAST, ((), ())),
                preferred_element_type=jnp.float32,
            )
        before = jnp.dot(
            found.astype(jnp.bfloat16),
            earlier.astype(jnp.bfloat16),
            preferred_element_type=jnp.float32,
        )
        held = jnp.sum(found, axis=1, keepdims=True)
        for other in range(LINES):
            if (other + 1) % lines:
                later = (line > other) & (line < (other // lines + 1) * lines)
                before += jnp.where(later, held[other : other + 1], 0.0)
        out_ref[...] = jnp.where(found > 0.5, before, -1.0).astype(jnp.int32)


def block_slots(col_block, ratio, panel_cols, row_lists):
    lanes = LANES if col_block % LANES == 0 else col_block
    lines = col_block // lanes
    device = jnp.stack([lax.axis_index("col"), lax.axis_index(ROW) * ratio]).astype(jnp.int32)
    shape = jax.ShapeDtypeStruct((LINES, lanes), jnp.int32)
    whole = pl.BlockSpec(memory_space=pltpu.VMEM)
    found = pl.pallas_call(
        functools.partial(slots_kernel, lines, lanes),
        out_shape=(shape, shape),
        in_specs=[pl.BlockSpec(memory_space=pltpu.SMEM), whole, whole],
        out_specs=(whole, whole),
        name="block_slots",
    )(device, row_lists[None], panel_cols[None])
    used = (1 + ratio) * lines
    return [slots[:used].reshape(used * lanes) for slots in found]


def one_hot(slot, count):
    return (slot[:, None] == jnp.arange(count, dtype=jnp.int32)).astype(jnp.float32)


def fullest(listed, col_block, col_count):
    home = listed // col_block
    counts = jnp.sum((jnp.arange(col_count)[:, None] == home).astype(jnp.int32), axis=1)
    return jnp.max(counts)


def panel_step(matrix, factor, dinv, panel_cols, row_lists):
    row_count = lax.axis_size(ROW)
    col_count = lax.axis_size("col")
    ratio = col_count // row_count
    row_block, col_block = matrix.shape
    width = panel_cols.shape[0]
    dinv_rows = dinv.shape[0]
    row_slots = col_block * 2 // 3
    col_slots = 2 * (width // col_count)
    row_k = ratio * col_slots
    row_pos = lax.axis_index(ROW)
    col_pos = lax.axis_index("col")
    side = col_pos % ratio

    list_slot, panel_slot = block_slots(col_block, ratio, panel_cols, row_lists)
    in_list, in_panel = list_slot >= 0, panel_slot >= 0
    col_in, row_in = in_list[:col_block], in_list[col_block:]
    col_panel, row_panel = in_panel[:col_block], in_panel[col_block:]
    pick = one_hot(list_slot, row_slots)
    pick_cols = pick[:col_block]
    pick_rows = pick[col_block:].reshape(ratio, col_block, row_slots)
    put = one_hot(panel_slot, col_slots)
    put_cols = put[:col_block]
    put_rows = put[col_block:].reshape(ratio, col_block, col_slots)

    packed = dot(factor, pick_cols, BY_FIRST)
    own_half = sent_to_all(packed, ROW[:2]).reshape(width // 2, row_slots)
    other_half = lax.ppermute(own_half, ROW[2], [(0, 1), (1, 0)])
    lower = jnp.concatenate([own_half, other_half])

    narrow = dot(matrix, pick_cols).reshape(ratio, col_block, row_slots)
    dense = jnp.stack([dot(pick_rows[part], narrow[part], BY_FIRST) for part in range(ratio)])
    share = row_slots // col_count
    dense = jnp.moveaxis(dense.reshape(ratio, col_count, share, row_slots), 0, 1)
    dense = dense.reshape(ratio * row_slots, row_slots)

    partial_value = -dot(dense, lower, BY_LAST)
    summed = sum_at_owner(partial_value.reshape(col_count, ratio * share, width), "col")

    home = panel_cols // col_block
    earlier = (panel_cols[None, :] < panel_cols[:, None]) & (home[None, :] == home[:, None])
    rank = jnp.sum(earlier.astype(jnp.int32), axis=1)
    slot = home * col_slots + rank
    wide = max(row_k, LANES)
    spread = home // ratio * wide + home % ratio * col_slots + rank
    half_slots = col_slots // 2

    def this_core_first(values):
        by_core = jnp.moveaxis(values.reshape(-1, 2, factor.shape[1]), 1, 0)
        by_core = by_core.reshape(2, width // 2)
        return jnp.where(lax.axis_index(ROW[2]) == 0, by_core, by_core[::-1]).reshape(width)

    route = one_hot(this_core_first(spread), row_count * wide)

    chosen = dot(summed, route).reshape(ratio, share, row_count, wide)
    chosen = jnp.transpose(chosen, (2, 0, 1, 3)).reshape(col_count, share, wide)
    arrived = lax.all_to_all(chosen, "col", 0, 0, tiled=True).reshape(row_slots, wide)
    arrived = arrived.T[:row_k]

    pairs = [
        (r * col_count + c, (c // ratio) * col_count + ratio * r + c % ratio)
        for r in range(row_count)
        for c in range(col_count)
    ]
    beside = lax.ppermute(arrived, ROW + ("col",), pairs)

    def halves(values):
        blocks = values.reshape(col_count, 2, half_slots, values.shape[1])
        return [blocks[:, part].reshape(col_count * half_slots, -1) for part in range(2)]

    slots = col_count * col_slots
    lower_slots = dot(one_hot(this_core_first(slot), slots), lower, BY_FIRST)
    mine = lax.dynamic_slice_in_dim(slot, col_pos * dinv_rows, dinv_rows)
    placed = dot(
        one_hot(mine, slots), dot(dinv, one_hot(slot - row_pos * row_k, row_k)), BY_FIRST
    )
    lower_pair = jnp.concatenate(halves(lower_slots), axis=1)
    placed_pair = jnp.concatenate(halves(placed), axis=1)
    empty = jnp.zeros_like(beside)
    beside_pair = jnp.concatenate(
        [jnp.concatenate([beside, empty], axis=1), jnp.concatenate([empty, beside], axis=1)]
    )
    terms = placed_pair - dot(lower_pair, beside_pair, BY_LAST)
    corner = sum_at_owner(terms.reshape(col_count, half_slots, 2 * row_k), "col")

    swap = [(c, c + 1 - 2 * (c % ratio)) for c in range(col_count)]
    kept = lax.dynamic_slice_in_dim(arrived, side * col_slots, col_slots, 0)
    given = lax.dynamic_slice_in_dim(arrived, (1 - side) * col_slots, col_slots, 0)
    taken = lax.ppermute(given, "col", swap)
    below = [jnp.where(side == 0, kept, taken), jnp.where(side == 0, taken, kept)]

    below_rows = [dot(pick_rows[part], below[part], BY_LAST) for part in range(ratio)]
    spread_out = dot(beside, pick_cols, BY_LAST)
    at_rows = jnp.concatenate(
        [
            dot(put_rows[part], spread_out[part * col_slots : (part + 1) * col_slots])
            for part in range(ratio)
        ]
    )
    with_rows = jnp.where(row_panel[:, None] & col_in[None, :], at_rows, matrix)
    at_cols = jnp.concatenate(
        [
            below_rows[part]
            + jnp.concatenate(
                [
                    dot(
                        put_rows[part],
                        corner[:, (half * ratio + part) * col_slots :][:, :col_slots],
                        BY_LAST,
                    )
                    for half in range(2)
                ],
                axis=1,
            )
            for part in range(ratio)
        ]
    )
    taken_over = (row_panel | row_in)[:, None] & col_panel[None, :]
    result = jnp.where(taken_over, dot(at_cols, put_cols, BY_LAST), with_rows)

    fits = (fullest(row_lists, col_block, col_count) <= row_slots) & (
        fullest(panel_cols, col_block, col_count) <= col_slots
    )

    def again(carried):
        general = general_panel(matrix, factor, dinv, panel_cols, row_in, col_in)
        return jnp.zeros((), jnp.bool_), general

    return lax.while_loop(lambda carried: carried[0], again, (~fits, result))[1]


def on_device(resident, factor, dinv, panel_cols, row_lists):
    matrix = resident
    for panel in reversed(range(factor.shape[0])):
        matrix = panel_step(
            matrix, factor[panel], dinv[panel], panel_cols[panel], row_lists[panel]
        )
    return matrix


def solution(mesh):
    finer = Mesh(
        mesh.devices.reshape(-1, 2, 2, mesh.shape["col"]), ("row_0", "row_1", "row_2", "col")
    )
    return jax.shard_map(
        on_device,
        mesh=finer,
        in_specs=(P(ROW, "col"), P(None, "col", ROW), P(None, "col", None), P(), P()),
        out_specs=P(ROW, "col"),
        check_vma=False,
    )
```

time: 303 us -> 149 us (0.49)
  the two profiles are of different devices: /device:TPU:16 before, /device:TPU:2 now
where the time goes in v1:
time: 149 us; the launch traced here: 148 us
  waiting for transfers between devices  61.5 us (41%)
  starting transfers between devices  50.7 us (34%)
  matrix products  19.2 us (13%)
  local copies, waits for them, and re-layouts  8.35 us (6%)
  other arithmetic  4.66 us (3%)
  Pallas kernels  2.24 us (2%)
  between operations  1.66 us (1%)
    all_to_all x2, waiting for transfers between devices, sum_at_owner(): return jnp.sum(lax.all_to_all(blocks, axis, 0, 0, tiled=True), axis=0)  28.9 us
    all_to_all x2, starting transfers between devices, sum_at_owner(): return jnp.sum(lax.all_to_all(blocks, axis, 0, 0, tiled=True), axis=0)  26.6 us
    dot_general x20, matrix products, dot(): lax.dot_general(a, b, (dims, ((), ())), precision=HIGHEST, preferred_elem...  19.2 us
    ppermute x1, waiting for transfers between devices, panel_step(): beside = lax.ppermute(arrived, ROW + ('col',), pairs)  18.1 us
    all_to_all x1, starting transfers between devices, sent_to_all(): return lax.all_to_all(copies, axis, split_axis=0, concat_axis=0, tiled=True)  10.1 us
    all_to_all x1, waiting for transfers between devices, panel_step(): lax.all_to_all(chosen, 'col', 0, 0, tiled=True).reshape(row_slots, wide)  9.16 us
    all_to_all x1, starting transfers between devices, panel_step(): lax.all_to_all(chosen, 'col', 0, 0, tiled=True).reshape(row_slots, wide)  5.41 us
    all_to_all x1, waiting for transfers between devices, sent_to_all(): return lax.all_to_all(copies, axis, split_axis=0, concat_axis=0, tiled=True)  5.35 us
  transfers between devices with their start and end apart: 7, of which 5 were waited for; matrix products, arithmetic and copies ran while one was open for 14% of the time, Pallas kernels for 0%

profile of v1, /device:TPU:2, one launch (start us, length us, event | category | flops | bytes accessed | tf_op | source)
XLA Modules:
  0.0 148.3 jit_solution(18226263449383672273)
XLA Ops:
  0.0 0.6 pad_add_fusion.device_ref
  0.6 2.2 %block_slots.1 = (s32[16,128]{1,0:T(8,128)}, s32[16,128]{1,0:T(8,128)}) custom-call(s32[2]{0:T(128)} %pad_add_fusion.device_ref, s32[1,6144]{1,0:T(1,128)} %rows_ref.1, s32[1,512]{1,0:T(1,128)} %cols_ref.1), custom_call_target="tpu_custom_call" | custom-call | tf_op jit(solution)/shard_map/block_slots/pallas_call | solution.py:145
  2.9 0.7 slice_bitcast_fusion
  3.8 1.0 convolution_bitcast_fusion.4
  4.8 0.7 broadcast_in_dim.26
  5.6 10.1 %all-to-all-start = ((f32[8,32,256]{2,1,0:T(8,128)}), f32[8,32,256]{2,1,0:T(8,128)S(1)}, u32[]{:S(2)}, u32[]{:S(2)}) async-start(f32[8,32,256]{2,1,0:T(8,128)} %broadcast_in_dim.26), calls=%async_computation | async-start | bytes 524288 | tf_op jit(solution)/shard_map/all_to_all | solution.py:31
  15.7 0.9 convolution_bitcast_fusion.1
  16.6 0.5 convolution_bitcast_fusion.3
  17.1 0.5 convolution_bitcast_fusion.2
  17.8 0.5 broadcast.265
  18.3 0.7 fusion.100
  19.0 0.3 convert_reduce_fusion.1
  20.1 5.3 %all-to-all-done = f32[8,32,256]{2,1,0:T(8,128)S(1)} async-done(((f32[8,32,256]{2,1,0:T(8,128)}), f32[8,32,256]{2,1,0:T(8,128)S(1)}, u32[]{:S(2)}, u32[]{:S(2)}) %all-to-all-start) | async-done | bytes 262176 | tf_op jit(solution)/shard_map/all_to_all | solution.py:31
  25.4 1.9 %collective-permute-start.5 = (f32[256,256]{1,0:T(8,128)S(1)}, f32[256,256]{1,0:T(8,128)S(1)}, u32[]{:S(2)}, u32[]{:S(2)}) collective-permute-start(f32[256,256]{1,0:T(8,128)S(1)} %bitcast.120), channel_id=1, source_target_pairs={{0,32},{32,0},{1,33},{33,1},{2,34},{34,2},{3,35},{35,3},{4,36},{36... | collective-permute-start | bytes 786440 | tf_op jit(solution)/shard_map/ppermute | solution.py:193
  27.5 0.8 copy.44
  28.3 0.6 slice.124
  29.0 2.0 %convolution_negate_fusion.1 = f32[512,512]{1,0:T(8,128)} fusion(f32[512,256]{1,0:T(8,128)S(1)} %bitcast.114, f32[256,256]{1,0:T(8,128)S(1)} %collective-permute-done.5, f32[256,256]{1,0:T(8,128)S(1)} %bitcast.121), kind=kOutput, calls=%fused_computation.53 | convolution fusion | flops 805699584 | bytes 2097152 | tf_op jit(solution)/shard_map/dot_general | solution.py:20
  31.0 13.5 %all-to-all-start.1 = ((f32[32,16,512]{2,1,0:T(8,128)}), f32[32,16,512]{2,1,0:T(8,128)S(1)}, u32[]{:S(2)}, u32[]{:S(2)}) async-start(f32[32,16,512]{2,1,0:T(8,128)} %bitcast.17), calls=%async_computation.1 | async-start | bytes 2097152 | tf_op jit(solution)/shard_map/all_to_all | solution.py:26
  44.6 0.7 reduce_max.19
  45.9 0.7 reduce_max.18
  47.2 0.9 copy.47
  48.2 0.5 fusion.104
  48.7 0.3 fusion.47
  49.0 0.7 fusion.74
  49.7 0.7 fusion.103
  50.7 2.9 %fusion.32 = f32[1024,256]{1,0:T(8,128)} fusion(s32[512]{0:T(512)S(1)} %bitcast.133, f32[256,256]{1,0:T(8,128)S(1)} %copy-done.11, f32[256,256]{1,0:T(8,128)S(1)} %bitcast.122), kind=kOutput, calls=%fused_computation.51 | convolution fusion | flops 1611268096 | bytes 1574912 | tf_op jit(solution)/shard_map/dot_general | solution.py:20
  53.6 19.8 %all-to-all-done.1 = f32[32,16,512]{2,1,0:T(8,128)S(1)} async-done(((f32[32,16,512]{2,1,0:T(8,128)}), f32[32,16,512]{2,1,0:T(8,128)S(1)}, u32[]{:S(2)}, u32[]{:S(2)}) %all-to-all-start.1) | async-done | bytes 1048608 | tf_op jit(solution)/shard_map/all_to_all | solution.py:26
  73.4 1.9 %fusion.33 = f32[16,2,8,128]{3,2,0,1:T(8,128)S(1)} fusion(s32[16,128]{1,0:T(8,128)S(1)} %multiply_add_fusion, s32[512]{0:T(512)S(1)} %bitcast.132, f32[16,512]{1,0:T(8,128)S(1)} %reduce_sum.105), kind=kOutput, calls=%fused_computation.60 | convolution fusion | flops 202375168 | bytes 174080 | tf_op jit(solution)/shard_map/dot_general | solution.py:20
  75.3 0.7 copy.46
  75.9 5.4 %all-to-all-start.2 = ((f32[32,8,128]{2,1,0:T(8,128)}), f32[32,8,128]{2,1,0:T(8,128)S(1)}, u32[]{:S(2)}, u32[]{:S(2)}) async-start(f32[32,8,128]{2,1,0:T(8,128)} %bitcast.25), calls=%async_computation.2 | async-start | bytes 262144 | tf_op jit(solution)/shard_map/all_to_all | solution.py:222
  81.4 1.3 fusion.102
  82.7 9.2 %all-to-all-done.2 = f32[32,8,128]{2,1,0:T(8,128)S(1)} async-done(((f32[32,8,128]{2,1,0:T(8,128)}), f32[32,8,128]{2,1,0:T(8,128)S(1)}, u32[]{:S(2)}, u32[]{:S(2)}) %all-to-all-start.2) | async-done | bytes 131104 | tf_op jit(solution)/shard_map/all_to_all | solution.py:222
  91.9 3.8 %collective-permute-start.7 = (f32[64,256]{0,1:T(8,128)S(1)}, f32[64,256]{0,1:T(8,128)S(1)}, u32[]{:S(2)}, u32[]{:S(2)}) collective-permute-start(f32[64,256]{0,1:T(8,128)S(1)} %bitcast.109), channel_id=1, source_target_pairs={{0,0},{1,1},{2,32},{3,33},{4,64},{5,65},{6,96},{7,97},{8,128},{9,1... | collective-permute-start | bytes 196616 | tf_op jit(solution)/shard_map/ppermute | solution.py:230
  95.6 0.8 constant_dynamic-slice_fusion
  96.4 2.9 %collective-permute-start.6 = (f32[32,256]{0,1:T(8,128)}, f32[32,256]{0,1:T(8,128)}, u32[]{:S(2)}, u32[]{:S(2)}) collective-permute-start(f32[32,256]{0,1:T(8,128)} %constant_dynamic-slice_fusion), channel_id=1, source_target_pairs={{0,1},{1,0},{2,3},{3,2},{4,5},{5,4},{6,7},{7,6},{8,9},{9,8},{10,11... | collective-permute-start | bytes 98312 | tf_op jit(solution)/shard_map/ppermute | solution.py:254
  99.3 18.1 %collective-permute-done.7 = f32[64,256]{0,1:T(8,128)S(1)} collective-permute-done((f32[64,256]{0,1:T(8,128)S(1)}, f32[64,256]{0,1:T(8,128)S(1)}, u32[]{:S(2)}, u32[]{:S(2)}) %collective-permute-start.7) | collective-permute-done | bytes 65568 | tf_op jit(solution)/shard_map/ppermute | solution.py:230
  117.4 1.7 %convolution_subtract_fusion = f32[512,128]{1,0:T(8,128)} fusion(f32[512,256]{1,0:T(8,128)S(1)} %bitcast.116, f32[512,256]{1,0:T(8,128)S(1)} %bitcast.115, f32[64,256]{0,1:T(8,128)S(1)} %collective-permute-done.7, f32[512,64]{1,0:T(8,128)S(1)} %bitcast.119, f32[512,64]{1,0:T(8,128)S(1)} %bitcast.118), kind=kOutput, calls=%fused_computation.59 | convolution fusion | flops 403374080 | bytes 1638400 | tf_op jit(solution)/shard_map/dot_general | solution.py:20
  119.1 13.1 %all-to-all-start.3 = ((f32[32,16,128]{2,1,0:T(8,128)}), f32[32,16,128]{2,1,0:T(8,128)S(1)}, u32[]{:S(2)}, u32[]{:S(2)}) async-start(f32[32,16,128]{2,1,0:T(8,128)} %bitcast.36), calls=%async_computation.3 | async-start | bytes 524288 | tf_op jit(solution)/shard_map/all_to_all | solution.py:26
  132.2 1.3 fusion.48
  133.4 0.4 fusion.65
  133.9 0.4 fusion.59
  134.2 9.2 %all-to-all-done.3 = f32[32,16,128]{2,1,0:T(8,128)S(1)} async-done(((f32[32,16,128]{2,1,0:T(8,128)}), f32[32,16,128]{2,1,0:T(8,128)S(1)}, u32[]{:S(2)}, u32[]{:S(2)}) %all-to-all-start.3) | async-done | bytes 262176 | tf_op jit(solution)/shard_map/all_to_all | solution.py:26
  143.6 0.3 fusion.67
  143.9 0.3 fusion.63
  144.2 0.3 fusion.61
  144.4 0.5 convolution_add_fusion.1
  144.9 1.3 convolution_add_fusion
  146.3 2.1 %convolution_select_fusion.3 = f32[768,384]{1,0:T(8,128)} fusion(f32[768,384]{1,0:T(8,128)S(1)} %copy-done.1, f32[384,384]{1,0:T(8,128)S(1)} %fusion.59, f32[384,384]{1,0:T(8,128)S(1)} %fusion.65, pred[384]{0:T(512)(128)(4,1)S(1)} %slice.142, pred[384]{0:T(512)(128)(4,1)S(1)} %copy-done.18, pred[768]{0:T(1024)(128)(4,1)S(1)} %copy-done.17, ...), kind=kOutput, calls=%fused_computation.52 | convolution fusion | flops 114745344 | bytes 3689472 | tf_op jit(solution)/shard_map/dot_general | solution.py:20
  (63 shorter events, 2.1 us)
Async XLA Ops:
  0.0 15.7 %copy-start.1 = (f32[768,384]{1,0:T(8,128)S(1)}, f32[768,384]{1,0:T(8,128)}, u32[]{:S(2)}) copy-start(f32[768,384]{1,0:T(8,128)} %param.21) | copy-start | bytes 3538948
  5.6 19.8 %all-to-all-start = ((f32[8,32,256]{2,1,0:T(8,128)}), f32[8,32,256]{2,1,0:T(8,128)S(1)}, u32[]{:S(2)}, u32[]{:S(2)}) async-start(f32[8,32,256]{2,1,0:T(8,128)} %broadcast_in_dim.26), calls=%async_computation | async-start | bytes 524288 | tf_op jit(solution)/shard_map/all_to_all | solution.py:31
  16.6 1.0 copy-start.8
  16.6 1.0 copy-start.12
  17.1 2.9 %copy-start.15 = (s32[16,128]{1,0:T(8,128)S(1)}, s32[16,128]{1,0:T(8,128)}, u32[]{:S(2)}) copy-start(s32[16,128]{1,0:T(8,128)} %get-tuple-element.853) | copy-start | bytes 24580
  17.1 2.9 %copy-start.16 = (s32[16,128]{1,0:T(8,128)S(1)}, s32[16,128]{1,0:T(8,128)}, u32[]{:S(2)}) copy-start(s32[16,128]{1,0:T(8,128)} %get-tuple-element.854) | copy-start | bytes 24580
  17.1 10.4 %copy-start.13 = (f32[1,384,32]{1,2,0:T(8,128)S(1)}, f32[1,384,32]{1,2,0:T(8,128)}, u32[]{:S(2)}) copy-start(f32[1,384,32]{1,2,0:T(8,128)} %param.22) | copy-start | bytes 147460
  25.4 3.5 %collective-permute-start.5 = (f32[256,256]{1,0:T(8,128)S(1)}, f32[256,256]{1,0:T(8,128)S(1)}, u32[]{:S(2)}, u32[]{:S(2)}) collective-permute-start(f32[256,256]{1,0:T(8,128)S(1)} %bitcast.120), channel_id=1, source_target_pairs={{0,32},{32,0},{1,33},{33,1},{2,34},{34,2},{3,35},{35,3},{4,36},{36... | collective-permute-start | bytes 786440 | tf_op jit(solution)/shard_map/ppermute | solution.py:193
  29.0 2.0 %copy-start.10 = (f32[256,256]{1,0:T(8,128)}, f32[256,256]{1,0:T(8,128)S(1)}, u32[]{:S(2)}) copy-start(f32[256,256]{1,0:T(8,128)S(1)} %collective-permute-done.5) | copy-start | bytes 786436
  31.0 16.3 %copy-start.14 = (f32[1,16,512]{2,1,0:T(8,128)S(1)}, f32[1,16,512]{2,1,0:T(8,128)}, u32[]{:S(2)}) copy-start(f32[1,16,512]{2,1,0:T(8,128)} %param.23) | copy-start | bytes 98308
  31.0 42.3 %all-to-all-start.1 = ((f32[32,16,512]{2,1,0:T(8,128)}), f32[32,16,512]{2,1,0:T(8,128)S(1)}, u32[]{:S(2)}, u32[]{:S(2)}) async-start(f32[32,16,512]{2,1,0:T(8,128)} %bitcast.17), calls=%async_computation.1 | async-start | bytes 2097152 | tf_op jit(solution)/shard_map/all_to_all | solution.py:26
  44.5 6.1 %copy-start.11 = (f32[256,256]{1,0:T(8,128)S(1)}, f32[256,256]{1,0:T(8,128)}, u32[]{:S(2)}) copy-start(f32[256,256]{1,0:T(8,128)} %copy-done.10) | copy-start | bytes 786436
  75.9 15.9 %all-to-all-start.2 = ((f32[32,8,128]{2,1,0:T(8,128)}), f32[32,8,128]{2,1,0:T(8,128)S(1)}, u32[]{:S(2)}, u32[]{:S(2)}) async-start(f32[32,8,128]{2,1,0:T(8,128)} %bitcast.25), calls=%async_computation.2 | async-start | bytes 262144 | tf_op jit(solution)/shard_map/all_to_all | solution.py:222
  81.4 36.0 %copy-start.6 = (f32[32,1,16,64]{3,2,1,0:T(8,128)S(1)}, f32[32,1,16,64]{3,2,1,0:T(8,128)}, u32[]{:S(2)}) copy-start(f32[32,1,16,64]{3,2,1,0:T(8,128)} %get-tuple-element.1039) | copy-start | bytes 393220
  91.9 25.5 %collective-permute-start.7 = (f32[64,256]{0,1:T(8,128)S(1)}, f32[64,256]{0,1:T(8,128)S(1)}, u32[]{:S(2)}, u32[]{:S(2)}) collective-permute-start(f32[64,256]{0,1:T(8,128)S(1)} %bitcast.109), channel_id=1, source_target_pairs={{0,0},{1,1},{2,32},{3,33},{4,64},{5,65},{6,96},{7,97},{8,128},{9,1... | collective-permute-start | bytes 196616 | tf_op jit(solution)/shard_map/ppermute | solution.py:230
  96.4 48.1 %collective-permute-start.6 = (f32[32,256]{0,1:T(8,128)}, f32[32,256]{0,1:T(8,128)}, u32[]{:S(2)}, u32[]{:S(2)}) collective-permute-start(f32[32,256]{0,1:T(8,128)} %constant_dynamic-slice_fusion), channel_id=1, source_target_pairs={{0,1},{1,0},{2,3},{3,2},{4,5},{5,4},{6,7},{7,6},{8,9},{9,8},{10,11... | collective-permute-start | bytes 98312 | tf_op jit(solution)/shard_map/ppermute | solution.py:254
  117.4 1.7 %copy-start.7 = (f32[64,256]{0,1:T(8,128)}, f32[64,256]{0,1:T(8,128)S(1)}, u32[]{:S(2)}) copy-start(f32[64,256]{0,1:T(8,128)S(1)} %collective-permute-done.7) | copy-start | bytes 196612
  119.1 24.3 %all-to-all-start.3 = ((f32[32,16,128]{2,1,0:T(8,128)}), f32[32,16,128]{2,1,0:T(8,128)S(1)}, u32[]{:S(2)}, u32[]{:S(2)}) async-start(f32[32,16,128]{2,1,0:T(8,128)} %bitcast.36), calls=%async_computation.3 | async-start | bytes 524288 | tf_op jit(solution)/shard_map/all_to_all | solution.py:26
  133.8 12.4 %copy-start.17 = (pred[768]{0:T(1024)(128)(4,1)S(1)}, pred[768]{0:T(1024)(128)(4,1)}, u32[]{:S(2)}) copy-start(pred[768]{0:T(1024)(128)(4,1)} %get-tuple-element.1044) | copy-start | bytes 2308
  133.8 12.4 %copy-start.18 = (pred[384]{0:T(512)(128)(4,1)S(1)}, pred[384]{0:T(512)(128)(4,1)}, u32[]{:S(2)}) copy-start(pred[384]{0:T(512)(128)(4,1)} %slice.124) | copy-start | bytes 1156
  146.2 2.1 %copy-start.9 = (s32[1,512]{1,0:T(1,128)S(1)}, s32[1,512]{1,0:T(1,128)}, u32[]{:S(2)}) copy-start(s32[1,512]{1,0:T(1,128)} %cols_ref.1) | copy-start | bytes 6148

commit v2 on v1

--- a/solution.py
+++ b/solution.py
@@ -20,6 +20,22 @@
     return lax.dot_general(
         a, b, (dims, ((), ())), precision=HIGHEST, preferred_element_type=jnp.float32
     )
+
+
+def thirds(values, axis):
+    high = lax.reduce_precision(values, 8, 7)
+    rest = values - high
+    middle = lax.reduce_precision(rest, 8, 7)
+    parts = [part.astype(jnp.bfloat16) for part in (high, middle, rest - middle)]
+    return jnp.concatenate(parts, axis=axis)
+
+
+def selected(parts, hot, dims=((1,), (0,))):
+    out = lax.dot_general(
+        parts, hot, (dims, ((), ())), preferred_element_type=jnp.float32
+    )
+    size = out.shape[0] // 3
+    return out[:size] + out[size : 2 * size] + out[2 * size :]
 
 
 def sum_at_owner(blocks, axis):
@@ -153,8 +169,9 @@
     return [slots[:used].reshape(used * lanes) for slots in found]
 
 
-def one_hot(slot, count):
-    return (slot[:, None] == jnp.arange(count, dtype=jnp.int32)).astype(jnp.float32)
+def one_hot(slot, count, dtype=jnp.float32):
+    hot = slot[:, None] == jnp.arange(count, dtype=jnp.int32)
+    return hot.astype(jnp.float32).astype(dtype)
 
 
 def fullest(listed, col_block, col_count):
@@ -188,7 +205,8 @@
     put_cols = put[:col_block]
     put_rows = put[col_block:].reshape(ratio, col_block, col_slots)
 
-    packed = dot(factor, pick_cols, BY_FIRST)
+    narrow_pick = one_hot(list_slot[:col_block], row_slots, jnp.bfloat16)
+    packed = selected(thirds(factor, 1), narrow_pick, BY_FIRST)
     own_half = sent_to_all(packed, ROW[:2]).reshape(width // 2, row_slots)
     other_half = lax.ppermute(own_half, ROW[2], [(0, 1), (1, 0)])
     lower = jnp.concatenate([own_half, other_half])
@@ -206,8 +224,9 @@
     earlier = (panel_cols[None, :] < panel_cols[:, None]) & (home[None, :] == home[:, None])
     rank = jnp.sum(earlier.astype(jnp.int32), axis=1)
     slot = home * col_slots + rank
-    wide = max(row_k, LANES)
-    spread = home // ratio * wide + home % ratio * col_slots + rank
+    wide = ratio * row_k
+    pair = home // ratio * wide
+    place = home % ratio
     half_slots = col_slots // 2
 
     def this_core_first(values):
@@ -215,19 +234,28 @@
         by_core = by_core.reshape(2, width // 2)
         return jnp.where(lax.axis_index(ROW[2]) == 0, by_core, by_core[::-1]).reshape(width)
 
-    route = one_hot(this_core_first(spread), row_count * wide)
-
-    chosen = dot(summed, route).reshape(ratio, share, row_count, wide)
-    chosen = jnp.transpose(chosen, (2, 0, 1, 3)).reshape(col_count, share, wide)
-    arrived = lax.all_to_all(chosen, "col", 0, 0, tiled=True).reshape(row_slots, wide)
-    arrived = arrived.T[:row_k]
-
-    pairs = [
-        (r * col_count + c, (c // ratio) * col_count + ratio * r + c % ratio)
-        for r in range(row_count)
-        for c in range(col_count)
-    ]
-    beside = lax.ppermute(arrived, ROW + ("col",), pairs)
+    def route(first):
+        places = [this_core_first(first(part)) for part in range(ratio)]
+        return one_hot(jnp.concatenate(places), row_count * wide, jnp.bfloat16)
+
+    to_rows = route(lambda part: pair + part * row_k + place * col_slots + rank)
+    to_cols = route(lambda part: pair + (1 - place) * row_k + part * col_slots + rank)
+
+    halves_beside = jnp.concatenate([summed[:share], summed[share:]], axis=1)
+    parts = thirds(halves_beside, 0)
+    chosen = selected(parts, to_rows).reshape(share, row_count, wide)
+    received = lax.all_to_all(jnp.moveaxis(chosen, 1, 0), ROW, 0, 0, tiled=True)
+
+    own = jnp.moveaxis(selected(parts, to_cols).reshape(share, row_count, wide), 1, 0)
+    lane = jnp.arange(wide, dtype=jnp.int32) // row_k
+    sent = jnp.stack([jnp.where(lane == part, received, own) for part in range(ratio)], axis=1)
+    arrived = lax.all_to_all(
+        sent.reshape(col_count, share, wide), "col", 0, 0, tiled=True
+    )
+    arrived = arrived.reshape(row_slots, wide).T
+    upper, under = arrived[:row_k], arrived[row_k:]
+    beside = jnp.where(side == 0, upper, under)
+    below = jnp.where(side == 0, under, upper)
 
     def halves(values):
         blocks = values.reshape(col_count, 2, half_slots, values.shape[1])
@@ -248,13 +276,7 @@
     terms = placed_pair - dot(lower_pair, beside_pair, BY_LAST)
     corner = sum_at_owner(terms.reshape(col_count, half_slots, 2 * row_k), "col")
 
-    swap = [(c, c + 1 - 2 * (c % ratio)) for c in range(col_count)]
-    kept = lax.dynamic_slice_in_dim(arrived, side * col_slots, col_slots, 0)
-    given = lax.dynamic_slice_in_dim(arrived, (1 - side) * col_slots, col_slots, 0)
-    taken = lax.ppermute(given, "col", swap)
-    below = [jnp.where(side == 0, kept, taken), jnp.where(side == 0, taken, kept)]
-
-    below_rows = [dot(pick_rows[part], below[part], BY_LAST) for part in range(ratio)]
+    below_rows = [dot(pick_rows[part], below[part * col_slots : (part + 1) * col_slots], BY_LAST) for part in range(ratio)]
     spread_out = dot(beside, pick_cols, BY_LAST)
     at_rows = jnp.concatenate(
         [

time: 149 us -> 130 us (0.87)
  the two profiles are of different devices: /device:TPU:2 before, /device:TPU:8 now
where the time goes in v2:
time: 130 us; the launch traced here: 129 us
  waiting for transfers between devices  54.4 us (42%)
  starting transfers between devices  40.1 us (31%)
  matrix products  16.2 us (12%)
  other arithmetic  7.64 us (6%)
  local copies, waits for them, and re-layouts  6.51 us (5%)
  Pallas kernels  2.25 us (2%)
  between operations  1.81 us (1%)
    all_to_all x2, waiting for transfers between devices, sum_at_owner(): return jnp.sum(lax.all_to_all(blocks, axis, 0, 0, tiled=True), axis=0)  31.8 us
    all_to_all x2, starting transfers between devices, sum_at_owner(): return jnp.sum(lax.all_to_all(blocks, axis, 0, 0, tiled=True), axis=0)  17 us
    dot_general x18, matrix products, dot(): lax.dot_general(a, b, (dims, ((), ())), precision=HIGHEST, preferred_elem...  14.4 us
    all_to_all x1, waiting for transfers between devices, panel_step(): received = lax.all_to_all(jnp.moveaxis(chosen, 1, 0), ROW, 0, 0, tiled=True)  9.3 us
    all_to_all x1, starting transfers between devices, sent_to_all(): return lax.all_to_all(copies, axis, split_axis=0, concat_axis=0, tiled=True)  8.66 us
    all_to_all x1, waiting for transfers between devices, panel_step(): lax.all_to_all(sent.reshape(col_count, share, wide), 'col', 0, 0, tiled=T...  8.07 us
    all_to_all x1, starting transfers between devices, panel_step(): lax.all_to_all(sent.reshape(col_count, share, wide), 'col', 0, 0, tiled=T...  6.83 us
    all_to_all x1, starting transfers between devices, panel_step(): received = lax.all_to_all(jnp.moveaxis(chosen, 1, 0), ROW, 0, 0, tiled=True)  5.74 us
  transfers between devices with their start and end apart: 6, of which 6 were waited for; matrix products, arithmetic and copies ran while one was open for 13% of the time, Pallas kernels for 0%

profile of v2, /device:TPU:8, one launch (start us, length us, event | category | flops | bytes accessed | tf_op | source)
XLA Modules:
  0.0 129.0 jit_solution(1334032337623977436)
XLA Ops:
  0.0 0.6 pad_add_fusion.2.device_ref
  0.6 2.2 %block_slots.1 = (s32[16,128]{1,0:T(8,128)}, s32[16,128]{1,0:T(8,128)}) custom-call(s32[2]{0:T(128)} %pad_add_fusion.2.device_ref, s32[1,6144]{1,0:T(1,128)} %rows_ref.1, s32[1,512]{1,0:T(1,128)} %cols_ref.1), custom_call_target="tpu_custom_call" | custom-call | tf_op jit(solution)/shard_map/block_slots/pallas_call | solution.py:161
  2.9 0.7 slice_bitcast_fusion.2
  3.6 0.8 reduce-precision_convert_fusion.1
  4.4 0.3 fusion.46
  4.7 0.7 broadcast_in_dim.34
  5.4 8.7 %all-to-all-start = ((f32[8,32,256]{2,1,0:T(8,128)}), f32[8,32,256]{2,1,0:T(8,128)S(1)}, u32[]{:S(2)}, u32[]{:S(2)}) async-start(f32[8,32,256]{2,1,0:T(8,128)} %broadcast_in_dim.34), calls=%async_computation | async-start | bytes 524288 | tf_op jit(solution)/shard_map/all_to_all | solution.py:47
  14.6 0.5 broadcast.335
  15.1 0.6 fusion.99
  15.9 0.3 convert_reduce_fusion.1
  17.7 0.5 slice.186
  18.1 0.6 reduce_max.19
  18.8 0.7 reduce_max.18
  20.7 0.8 copy.70
  21.6 0.8 copy.73
  22.5 0.9 convolution_bitcast_fusion.1
  23.4 0.5 convolution_bitcast_fusion.3
  23.9 4.2 %all-to-all-done = f32[8,32,256]{2,1,0:T(8,128)S(1)} async-done(((f32[8,32,256]{2,1,0:T(8,128)}), f32[8,32,256]{2,1,0:T(8,128)S(1)}, u32[]{:S(2)}, u32[]{:S(2)}) %all-to-all-start) | async-done | bytes 262176 | tf_op jit(solution)/shard_map/all_to_all | solution.py:47
  28.1 1.9 %collective-permute-start.5 = (f32[256,256]{1,0:T(8,128)S(1)}, f32[256,256]{1,0:T(8,128)S(1)}, u32[]{:S(2)}, u32[]{:S(2)}) collective-permute-start(f32[256,256]{1,0:T(8,128)S(1)} %bitcast.135), channel_id=1, source_target_pairs={{0,32},{32,0},{1,33},{33,1},{2,34},{34,2},{3,35},{35,3},{4,36},{36... | collective-permute-start | bytes 786440 | tf_op jit(solution)/shard_map/ppermute | solution.py:211
  30.0 0.5 convolution_bitcast_fusion.2
  30.5 1.0 collective-permute-done.5
  31.5 2.0 %convolution_negate_fusion.1 = f32[512,512]{1,0:T(8,128)} fusion(f32[512,256]{1,0:T(8,128)S(1)} %bitcast.128, f32[256,256]{1,0:T(8,128)S(1)} %collective-permute-done.5, f32[256,256]{1,0:T(8,128)S(1)} %bitcast.136), kind=kOutput, calls=%fused_computation.56 | convolution fusion | flops 805699584 | bytes 2097152 | tf_op jit(solution)/shard_map/dot_general | solution.py:20
  33.5 12.1 %all-to-all-start.1 = ((f32[32,16,512]{2,1,0:T(8,128)}), f32[32,16,512]{2,1,0:T(8,128)S(1)}, u32[]{:S(2)}, u32[]{:S(2)}) async-start(f32[32,16,512]{2,1,0:T(8,128)} %bitcast.17), calls=%async_computation.1 | async-start | bytes 2097152 | tf_op jit(solution)/shard_map/all_to_all | solution.py:42
  45.7 0.6 fusion.104
  46.2 0.3 fusion.45
  46.5 0.7 fusion.76
  47.5 2.9 %fusion.31 = f32[1024,256]{1,0:T(8,128)} fusion(s32[512]{0:T(512)S(1)} %bitcast.152, f32[256,256]{1,0:T(8,128)S(1)} %copy-done.11, f32[256,256]{1,0:T(8,128)S(1)} %bitcast.137), kind=kOutput, calls=%fused_computation.54 | convolution fusion | flops 1611268096 | bytes 1574912 | tf_op jit(solution)/shard_map/dot_general | solution.py:20
  50.4 22.0 %all-to-all-done.1 = f32[32,16,512]{2,1,0:T(8,128)S(1)} async-done(((f32[32,16,512]{2,1,0:T(8,128)}), f32[32,16,512]{2,1,0:T(8,128)S(1)}, u32[]{:S(2)}, u32[]{:S(2)}) %all-to-all-start.1) | async-done | bytes 1048608 | tf_op jit(solution)/shard_map/all_to_all | solution.py:42
  72.5 0.8 fusion.27
  73.3 0.6 fusion.75
  73.9 5.7 %all-to-all-start.2 = ((f32[16,8,128]{2,1,0:T(8,128)}), f32[16,8,128]{2,1,0:T(8,128)S(1)}, u32[]{:S(2)}, u32[]{:S(2)}) async-start(f32[16,8,128]{2,1,0:T(8,128)} %fusion.75), calls=%async_computation.2 | async-start | bytes 131072 | tf_op jit(solution)/shard_map/all_to_all | solution.py:247
  79.7 0.8 fusion.28
  80.5 9.3 %all-to-all-done.2 = f32[16,8,128]{2,1,0:T(8,128)S(1)} async-done(((f32[16,8,128]{2,1,0:T(8,128)}), f32[16,8,128]{2,1,0:T(8,128)S(1)}, u32[]{:S(2)}, u32[]{:S(2)}) %all-to-all-start.2) | async-done | bytes 65568 | tf_op jit(solution)/shard_map/all_to_all | solution.py:247
  89.8 0.7 pad_maximum_fusion.4
  90.4 6.8 %all-to-all-start.3 = ((f32[32,8,128]{2,1,0:T(8,128)}), f32[32,8,128]{2,1,0:T(8,128)S(1)}, u32[]{:S(2)}, u32[]{:S(2)}) async-start(f32[32,8,128]{2,1,0:T(8,128)} %bitcast.31), calls=%async_computation.3 | async-start | bytes 262144 | tf_op jit(solution)/shard_map/all_to_all | solution.py:252
  97.3 1.3 fusion.101
  98.6 8.1 %all-to-all-done.3 = f32[32,8,128]{2,1,0:T(8,128)S(1)} async-done(((f32[32,8,128]{2,1,0:T(8,128)}), f32[32,8,128]{2,1,0:T(8,128)S(1)}, u32[]{:S(2)}, u32[]{:S(2)}) %all-to-all-start.3) | async-done | bytes 131104 | tf_op jit(solution)/shard_map/all_to_all | solution.py:252
  106.6 0.8 slice_select_fusion.1
  107.4 1.7 %convolution_subtract_fusion = f32[512,128]{1,0:T(8,128)} fusion(f32[512,256]{1,0:T(8,128)S(1)} %bitcast.130, f32[512,256]{1,0:T(8,128)S(1)} %bitcast.129, f32[64,256]{0,1:T(8,128)S(1)} %get-tuple-element.1061, f32[512,64]{1,0:T(8,128)S(1)} %bitcast.134, f32[512,64]{1,0:T(8,128)S(1)} %bitcast.133), kind=kOutput, calls=%fused_computation.62 | convolution fusion | flops 403374080 | bytes 1638400 | tf_op jit(solution)/shard_map/dot_general | solution.py:20
  109.1 4.9 %all-to-all-start.4 = ((f32[32,16,128]{2,1,0:T(8,128)}), f32[32,16,128]{2,1,0:T(8,128)S(1)}, u32[]{:S(2)}, u32[]{:S(2)}) async-start(f32[32,16,128]{2,1,0:T(8,128)} %bitcast.43), calls=%async_computation.4 | async-start | bytes 524288 | tf_op jit(solution)/shard_map/all_to_all | solution.py:42
  114.0 0.4 fusion.39
  114.4 0.4 fusion.60
  114.8 0.4 fusion.54
  115.2 9.8 %all-to-all-done.4 = f32[32,16,128]{2,1,0:T(8,128)S(1)} async-done(((f32[32,16,128]{2,1,0:T(8,128)}), f32[32,16,128]{2,1,0:T(8,128)S(1)}, u32[]{:S(2)}, u32[]{:S(2)}) %all-to-all-start.4) | async-done | bytes 262176 | tf_op jit(solution)/shard_map/all_to_all | solution.py:42
  125.3 0.3 fusion.62
  126.1 0.4 convolution_add_fusion.1
  126.4 0.4 convolution_add_fusion
  126.9 2.1 %convolution_select_fusion.3 = f32[768,384]{1,0:T(8,128)} fusion(f32[768,384]{1,0:T(8,128)S(1)} %copy-done.1, f32[384,384]{1,0:T(8,128)S(1)} %fusion.54, f32[384,384]{1,0:T(8,128)S(1)} %fusion.60, pred[384]{0:T(512)(128)(4,1)S(1)} %slice.218, pred[384]{0:T(512)(128)(4,1)S(1)} %copy-done.19, pred[768]{0:T(1024)(128)(4,1)S(1)} %copy-done.18, ...), kind=kOutput, calls=%fused_computation.55 | convolution fusion | flops 114745344 | bytes 3689472 | tf_op jit(solution)/shard_map/dot_general | solution.py:20
  (87 shorter events, 3.1 us)
Async XLA Ops:
  0.0 14.1 %copy-start.8 = (s32[1,512]{1,0:T(1,128)S(1)}, s32[1,512]{1,0:T(1,128)}, u32[]{:S(2)}) copy-start(s32[1,512]{1,0:T(1,128)} %cols_ref.1) | copy-start | bytes 6148
  0.0 14.2 %copy-start.14 = (s32[1,6144]{1,0:T(1,128)S(1)}, s32[1,6144]{1,0:T(1,128)}, u32[]{:S(2)}) copy-start(s32[1,6144]{1,0:T(1,128)} %rows_ref.1) | copy-start | bytes 73732
  0.0 20.7 %copy-start.16 = (f32[1,16,512]{2,1,0:T(8,128)S(1)}, f32[1,16,512]{2,1,0:T(8,128)}, u32[]{:S(2)}) copy-start(f32[1,16,512]{2,1,0:T(8,128)} %param.23) | copy-start | bytes 98308
  2.8 11.3 %copy-start.15 = (s32[16,128]{1,0:T(8,128)S(1)}, s32[16,128]{1,0:T(8,128)}, u32[]{:S(2)}) copy-start(s32[16,128]{1,0:T(8,128)} %get-tuple-element.854) | copy-start | bytes 24580
  2.9 14.5 %copy-start.17 = (s32[16,128]{1,0:T(8,128)S(1)}, s32[16,128]{1,0:T(8,128)}, u32[]{:S(2)}) copy-start(s32[16,128]{1,0:T(8,128)} %get-tuple-element.853) | copy-start | bytes 24580
  4.4 17.2 %copy-start.12 = (f32[1,384,32]{1,2,0:T(8,128)S(1)}, f32[1,384,32]{1,2,0:T(8,128)}, u32[]{:S(2)}) copy-start(f32[1,384,32]{1,2,0:T(8,128)} %param.22) | copy-start | bytes 147460
  4.7 17.8 %copy-start.1 = (f32[768,384]{1,0:T(8,128)S(1)}, f32[768,384]{1,0:T(8,128)}, u32[]{:S(2)}) copy-start(f32[768,384]{1,0:T(8,128)} %param.21) | copy-start | bytes 3538948
  5.4 22.7 %all-to-all-start = ((f32[8,32,256]{2,1,0:T(8,128)}), f32[8,32,256]{2,1,0:T(8,128)S(1)}, u32[]{:S(2)}, u32[]{:S(2)}) async-start(f32[8,32,256]{2,1,0:T(8,128)} %broadcast_in_dim.34), calls=%async_computation | async-start | bytes 524288 | tf_op jit(solution)/shard_map/all_to_all | solution.py:47
  28.1 5.4 %copy-start.6 = (f32[8,32,256]{2,1,0:T(8,128)}, f32[8,32,256]{2,1,0:T(8,128)S(1)}, u32[]{:S(2)}) copy-start(f32[8,32,256]{2,1,0:T(8,128)S(1)} %all-to-all-done) | copy-start | bytes 786436
  28.1 3.4 %collective-permute-start.5 = (f32[256,256]{1,0:T(8,128)S(1)}, f32[256,256]{1,0:T(8,128)S(1)}, u32[]{:S(2)}, u32[]{:S(2)}) collective-permute-start(f32[256,256]{1,0:T(8,128)S(1)} %bitcast.135), channel_id=1, source_target_pairs={{0,32},{32,0},{1,33},{33,1},{2,34},{34,2},{3,35},{35,3},{4,36},{36... | collective-permute-start | bytes 786440 | tf_op jit(solution)/shard_map/ppermute | solution.py:211
  31.5 2.0 %copy-start.10 = (f32[256,256]{1,0:T(8,128)}, f32[256,256]{1,0:T(8,128)S(1)}, u32[]{:S(2)}) copy-start(f32[256,256]{1,0:T(8,128)S(1)} %collective-permute-done.5) | copy-start | bytes 786436
  33.5 38.9 %all-to-all-start.1 = ((f32[32,16,512]{2,1,0:T(8,128)}), f32[32,16,512]{2,1,0:T(8,128)S(1)}, u32[]{:S(2)}, u32[]{:S(2)}) async-start(f32[32,16,512]{2,1,0:T(8,128)} %bitcast.17), calls=%async_computation.1 | async-start | bytes 2097152 | tf_op jit(solution)/shard_map/all_to_all | solution.py:42
  45.6 1.9 %copy-start.7 = (f32[8,32,256]{2,1,0:T(8,128)S(1)}, f32[8,32,256]{2,1,0:T(8,128)}, u32[]{:S(2)}) copy-start(f32[8,32,256]{2,1,0:T(8,128)} %copy-done.6) | copy-start | bytes 786436
  45.6 1.9 %copy-start.11 = (f32[256,256]{1,0:T(8,128)S(1)}, f32[256,256]{1,0:T(8,128)}, u32[]{:S(2)}) copy-start(f32[256,256]{1,0:T(8,128)} %copy-done.10) | copy-start | bytes 786436
  73.9 15.8 %all-to-all-start.2 = ((f32[16,8,128]{2,1,0:T(8,128)}), f32[16,8,128]{2,1,0:T(8,128)S(1)}, u32[]{:S(2)}, u32[]{:S(2)}) async-start(f32[16,8,128]{2,1,0:T(8,128)} %fusion.75), calls=%async_computation.2 | async-start | bytes 131072 | tf_op jit(solution)/shard_map/all_to_all | solution.py:247
  90.4 16.2 %all-to-all-start.3 = ((f32[32,8,128]{2,1,0:T(8,128)}), f32[32,8,128]{2,1,0:T(8,128)S(1)}, u32[]{:S(2)}, u32[]{:S(2)}) async-start(f32[32,8,128]{2,1,0:T(8,128)} %bitcast.31), calls=%async_computation.3 | async-start | bytes 262144 | tf_op jit(solution)/shard_map/all_to_all | solution.py:252
  109.1 15.9 %all-to-all-start.4 = ((f32[32,16,128]{2,1,0:T(8,128)}), f32[32,16,128]{2,1,0:T(8,128)S(1)}, u32[]{:S(2)}, u32[]{:S(2)}) async-start(f32[32,16,128]{2,1,0:T(8,128)} %bitcast.43), calls=%async_computation.4 | async-start | bytes 524288 | tf_op jit(solution)/shard_map/all_to_all | solution.py:42
  114.4 11.7 %copy-start.13 = (f32[64,256]{0,1:T(8,128)S(1)}, f32[64,256]{0,1:T(8,128)}, u32[]{:S(2)}) copy-start(f32[64,256]{0,1:T(8,128)} %get-tuple-element.1060) | copy-start | bytes 196612
  114.8 12.0 %copy-start.18 = (pred[768]{0:T(1024)(128)(4,1)S(1)}, pred[768]{0:T(1024)(128)(4,1)}, u32[]{:S(2)}) copy-start(pred[768]{0:T(1024)(128)(4,1)} %get-tuple-element.1076) | copy-start | bytes 2308
  114.8 12.0 %copy-start.19 = (pred[384]{0:T(512)(128)(4,1)S(1)}, pred[384]{0:T(512)(128)(4,1)}, u32[]{:S(2)}) copy-start(pred[384]{0:T(512)(128)(4,1)} %slice.186) | copy-start | bytes 1156
  126.9 2.1 %copy-start.9 = (s32[1,512]{1,0:T(1,128)S(1)}, s32[1,512]{1,0:T(1,128)}, u32[]{:S(2)}) copy-start(s32[1,512]{1,0:T(1,128)} %cols_ref.1) | copy-start | bytes 6148

commit v3 on v2

--- a/solution.py
+++ b/solution.py
@@ -40,11 +40,6 @@
 
 def sum_at_owner(blocks, axis):
     return jnp.sum(lax.all_to_all(blocks, axis, 0, 0, tiled=True), axis=0)
-
-
-def sent_to_all(shard, axis):
-    copies = jnp.broadcast_to(shard, (lax.axis_size(axis), *shard.shape))
-    return lax.all_to_all(copies, axis, split_axis=0, concat_axis=0, tiled=True)
 
 
 def ring_sum(shard, axis):
@@ -114,7 +109,9 @@
     return lax.fori_loop(0, row_count, corners, out)
 
 
-def slots_kernel(lines, lanes, device_ref, rows_ref, cols_ref, row_slots_ref, col_slots_ref):
+def slots_kernel(
+    lines, lanes, device_ref, rows_ref, cols_ref, factor_ref, row_slots_ref, col_slots_ref, packed_ref
+):
     line = lax.broadcasted_iota(jnp.int32, (LINES, 1), 0)
     own = jnp.where(
         line < lines, device_ref[0] * lines + line, device_ref[1] * lines + line - lines
@@ -150,9 +147,19 @@
                 later = (line > other) & (line < (other // lines + 1) * lines)
                 before += jnp.where(later, held[other : other + 1], 0.0)
         out_ref[...] = jnp.where(found > 0.5, before, -1.0).astype(jnp.int32)
-
-
-def block_slots(col_block, ratio, panel_cols, row_lists):
+    copies, group, slots = packed_ref.shape
+    place = lax.broadcasted_iota(jnp.int32, (slots, lanes), 0)
+    packed = jnp.zeros((slots, group), jnp.float32)
+    for part in range(lines):
+        hot = (place == row_slots_ref[part : part + 1, :]).astype(jnp.float32)
+        held = factor_ref[part * lanes : (part + 1) * lanes, :]
+        packed += jnp.dot(hot, held, precision=HIGHEST, preferred_element_type=jnp.float32)
+    packed_ref[...] = jnp.broadcast_to(packed.T[None], packed_ref.shape)
+
+
+def block_slots(row_slots, ratio, factor, panel_cols, row_lists):
+    col_block, group = factor.shape
+    copies = lax.axis_size(ROW[:2])
     lanes = LANES if col_block % LANES == 0 else col_block
     lines = col_block // lanes
     device = jnp.stack([lax.axis_index("col"), lax.axis_index(ROW) * ratio]).astype(jnp.int32)
@@ -160,13 +167,13 @@
     whole = pl.BlockSpec(memory_space=pltpu.VMEM)
     found = pl.pallas_call(
         functools.partial(slots_kernel, lines, lanes),
-        out_shape=(shape, shape),
-        in_specs=[pl.BlockSpec(memory_space=pltpu.SMEM), whole, whole],
-        out_specs=(whole, whole),
+        out_shape=(shape, shape, jax.ShapeDtypeStruct((copies, group, row_slots), jnp.float32)),
+        in_specs=[pl.BlockSpec(memory_space=pltpu.SMEM), whole, whole, whole],
+        out_specs=(whole, whole, whole),
         name="block_slots",
-    )(device, row_lists[None], panel_cols[None])
+    )(device, row_lists[None], panel_cols[None], factor)
     used = (1 + ratio) * lines
-    return [slots[:used].reshape(used * lanes) for slots in found]
+    return [slots[:used].reshape(used * lanes) for slots in found[:2]] + [found[2]]
 
 
 def one_hot(slot, count, dtype=jnp.float32):
@@ -174,10 +181,42 @@
     return hot.astype(jnp.float32).astype(dtype)
 
 
-def fullest(listed, col_block, col_count):
-    home = listed // col_block
-    counts = jnp.sum((jnp.arange(col_count)[:, None] == home).astype(jnp.int32), axis=1)
-    return jnp.max(counts)
+def places_kernel(sizes, panel_ref, other_ref, rows_ref, out_ref):
+    col_block, ratio, col_slots, col_count = sizes
+    row_k = ratio * col_slots
+    wide = ratio * row_k
+    other = other_ref[...]
+    other_home = lax.div(other, jnp.int32(col_block))
+    for order in range(2):
+        panel = panel_ref[order : order + 1, :]
+        home = lax.div(panel, jnp.int32(col_block))
+        earlier = (other < panel) & (other_home == home)
+        rank = jnp.sum(earlier.astype(jnp.float32), axis=0, keepdims=True).astype(jnp.int32)
+        pair = lax.div(home, jnp.int32(ratio))
+        place = home - pair * ratio
+        out_ref[order : order + 1, :] = home * col_slots + rank
+    for part in range(ratio):
+        down = pair * wide + part * row_k + place * col_slots + rank
+        along = pair * wide + (1 - place) * row_k + part * col_slots + rank
+        out_ref[2 + part : 3 + part, :] = down
+        out_ref[2 + ratio + part : 3 + ratio + part, :] = along
+    out_ref[6:7, :] = rank
+    rows_home = lax.div(rows_ref[...], jnp.int32(col_block))
+    block = lax.broadcasted_iota(jnp.int32, (col_count, rows_ref.shape[1]), 0)
+    counts = jnp.sum((block == rows_home).astype(jnp.float32), axis=1, keepdims=True)
+    most = jnp.max(counts, axis=0, keepdims=True).astype(jnp.int32)
+    out_ref[7:8, :] = jnp.broadcast_to(most, (1, panel_ref.shape[1]))
+
+
+def panel_places(col_slots, col_block, ratio, col_count, group, panel_cols, row_lists):
+    width = panel_cols.shape[0]
+    by_core = jnp.moveaxis(panel_cols.reshape(-1, 2, group), 1, 0).reshape(2, width // 2)
+    local = jnp.where(lax.axis_index(ROW[2]) == 0, by_core, by_core[::-1]).reshape(width)
+    return pl.pallas_call(
+        functools.partial(places_kernel, (col_block, ratio, col_slots, col_count)),
+        out_shape=jax.ShapeDtypeStruct((8, width), jnp.int32),
+        name="panel_places",
+    )(jnp.stack([panel_cols, local]), panel_cols[:, None], row_lists[None])
 
 
 def panel_step(matrix, factor, dinv, panel_cols, row_lists):
@@ -194,7 +233,9 @@
     col_pos = lax.axis_index("col")
     side = col_pos % ratio
 
-    list_slot, panel_slot = block_slots(col_block, ratio, panel_cols, row_lists)
+    list_slot, panel_slot, packed = block_slots(
+        row_slots, ratio, factor, panel_cols, row_lists
+    )
     in_list, in_panel = list_slot >= 0, panel_slot >= 0
     col_in, row_in = in_list[:col_block], in_list[col_block:]
     col_panel, row_panel = in_panel[:col_block], in_panel[col_block:]
@@ -202,12 +243,10 @@
     pick_cols = pick[:col_block]
     pick_rows = pick[col_block:].reshape(ratio, col_block, row_slots)
     put = one_hot(panel_slot, col_slots)
-    put_cols = put[:col_block]
     put_rows = put[col_block:].reshape(ratio, col_block, col_slots)
 
-    narrow_pick = one_hot(list_slot[:col_block], row_slots, jnp.bfloat16)
-    packed = selected(thirds(factor, 1), narrow_pick, BY_FIRST)
-    own_half = sent_to_all(packed, ROW[:2]).reshape(width // 2, row_slots)
+    own_half = lax.all_to_all(packed, ROW[:2], 0, 0, tiled=True)
+    own_half = own_half.reshape(width // 2, row_slots)
     other_half = lax.ppermute(own_half, ROW[2], [(0, 1), (1, 0)])
     lower = jnp.concatenate([own_half, other_half])
 
@@ -220,26 +259,19 @@
     partial_value = -dot(dense, lower, BY_LAST)
     summed = sum_at_owner(partial_value.reshape(col_count, ratio * share, width), "col")
 
-    home = panel_cols // col_block
-    earlier = (panel_cols[None, :] < panel_cols[:, None]) & (home[None, :] == home[:, None])
-    rank = jnp.sum(earlier.astype(jnp.int32), axis=1)
-    slot = home * col_slots + rank
     wide = ratio * row_k
-    pair = home // ratio * wide
-    place = home % ratio
     half_slots = col_slots // 2
-
-    def this_core_first(values):
-        by_core = jnp.moveaxis(values.reshape(-1, 2, factor.shape[1]), 1, 0)
-        by_core = by_core.reshape(2, width // 2)
-        return jnp.where(lax.axis_index(ROW[2]) == 0, by_core, by_core[::-1]).reshape(width)
-
-    def route(first):
-        places = [this_core_first(first(part)) for part in range(ratio)]
-        return one_hot(jnp.concatenate(places), row_count * wide, jnp.bfloat16)
-
-    to_rows = route(lambda part: pair + part * row_k + place * col_slots + rank)
-    to_cols = route(lambda part: pair + (1 - place) * row_k + part * col_slots + rank)
+    slots = col_count * col_slots
+    found = panel_places(
+        col_slots, col_block, ratio, col_count, factor.shape[1], panel_cols, row_lists
+    )
+    slot, local_slot = found[0], found[1]
+
+    def route(places):
+        return one_hot(places.reshape(ratio * width), row_count * wide, jnp.bfloat16)
+
+    to_rows = route(found[2:4])
+    to_cols = route(found[4:6])
 
     halves_beside = jnp.concatenate([summed[:share], summed[share:]], axis=1)
     parts = thirds(halves_beside, 0)
@@ -261,8 +293,7 @@
         blocks = values.reshape(col_count, 2, half_slots, values.shape[1])
         return [blocks[:, part].reshape(col_count * half_slots, -1) for part in range(2)]
 
-    slots = col_count * col_slots
-    lower_slots = dot(one_hot(this_core_first(slot), slots), lower, BY_FIRST)
+    lower_slots = dot(one_hot(local_slot, slots), lower, BY_FIRST)
     mine = lax.dynamic_slice_in_dim(slot, col_pos * dinv_rows, dinv_rows)
     placed = dot(
         one_hot(mine, slots), dot(dinv, one_hot(slot - row_pos * row_k, row_k)), BY_FIRST
@@ -285,29 +316,29 @@
         ]
     )
     with_rows = jnp.where(row_panel[:, None] & col_in[None, :], at_rows, matrix)
+    corner = jnp.concatenate([corner[:, :row_k], corner[:, row_k:]])
     at_cols = jnp.concatenate(
         [
             below_rows[part]
-            + jnp.concatenate(
-                [
-                    dot(
-                        put_rows[part],
-                        corner[:, (half * ratio + part) * col_slots :][:, :col_slots],
-                        BY_LAST,
-                    )
-                    for half in range(2)
-                ],
-                axis=1,
+            + dot(
+                put_rows[part],
+                corner[:, part * col_slots : (part + 1) * col_slots],
+                BY_LAST,
             )
             for part in range(ratio)
         ]
     )
+    thrice = jnp.concatenate([one_hot(panel_slot[:col_block], col_slots, jnp.bfloat16)] * 3, axis=1)
+    at_cols = lax.dot_general(
+        thirds(at_cols, 1),
+        thrice,
+        (BY_LAST, ((), ())),
+        preferred_element_type=jnp.float32,
+    )
     taken_over = (row_panel | row_in)[:, None] & col_panel[None, :]
-    result = jnp.where(taken_over, dot(at_cols, put_cols, BY_LAST), with_rows)
-
-    fits = (fullest(row_lists, col_block, col_count) <= row_slots) & (
-        fullest(panel_cols, col_block, col_count) <= col_slots
-    )
+    result = jnp.where(taken_over, at_cols, with_rows)
+
+    fits = (jnp.max(found[6]) < col_slots) & (jnp.max(found[7]) <= row_slots)
 
     def again(carried):
         general = general_panel(matrix, factor, dinv, panel_cols, row_in, col_in)

time: 130 us -> 130 us (level)
  waiting for transfers between devices: 54.4 us -> 47.6 us
  Pallas kernels: 2.25 us -> 5.72 us
    all_to_all x2, waiting for transfers between devices: 31.8 us -> 26.1 us  [sum_at_owner(): return jnp.sum(lax.all_to_all(blocks, axis, 0, 0, tiled=True), axis=0)]
    unnamed x36 -> x33, local copies, waits for them, and re-layouts: 0.9 us -> 3.87 us
    pallas_call x0 -> x1, Pallas kernels: none -> 2.17 us  [panel_places(): pl.pallas_call(functools.partial(places_kernel, (col_block, ratio, col_sl...]
    slice x0 -> x1, other arithmetic: none -> 2.16 us  [panel_step(): slot, local_slot = (found[0], found[1])]
    dot_general x0 -> x1, matrix products: none -> 1.69 us  [panel_step(): lax.dot_general(thirds(at_cols, 1), thrice, (BY_LAST, ((), ())), preferre...]
    reduce_max x2 -> x0, other arithmetic: 1.34 us -> none  [fullest(): return jnp.max(counts)]
    pallas_call x1, Pallas kernels: 2.25 us -> 3.56 us  [block_slots(): pl.pallas_call(functools.partial(slots_kernel, lines, lanes), out_shape=(...]
    dot_general x18 -> x15, matrix products: 14.4 us -> 13.6 us  [dot(): lax.dot_general(a, b, (dims, ((), ())), precision=HIGHEST, preferred_elem...]
  transfers between devices with their start and end apart: 6 -> 6, of which waited for: 6 -> 6; matrix products, arithmetic and copies ran while one was open for 13% -> 17% of each run, Pallas kernels for 0% -> 2%
where the time goes in v3:
time: 130 us; the launch traced here: 129 us
  waiting for transfers between devices  47.6 us (37%)
  starting transfers between devices  41 us (32%)
  matrix products  16.9 us (13%)
  other arithmetic  8.49 us (7%)
  local copies, waits for them, and re-layouts  7.7 us (6%)
  Pallas kernels  5.72 us (4%)
  between operations  1.69 us (1%)
    all_to_all x2, waiting for transfers between devices, sum_at_owner(): return jnp.sum(lax.all_to_all(blocks, axis, 0, 0, tiled=True), axis=0)  26.1 us
    all_to_all x2, starting transfers between devices, sum_at_owner(): return jnp.sum(lax.all_to_all(blocks, axis, 0, 0, tiled=True), axis=0)  17.1 us
    dot_general x15, matrix products, dot(): lax.dot_general(a, b, (dims, ((), ())), precision=HIGHEST, preferred_elem...  13.6 us
    all_to_all x1, waiting for transfers between devices, panel_step(): received = lax.all_to_all(jnp.moveaxis(chosen, 1, 0), ROW, 0, 0, tiled=True)  9.28 us
    all_to_all x1, starting transfers between devices, panel_step(): own_half = lax.all_to_all(packed, ROW[:2], 0, 0, tiled=True)  8.66 us
    all_to_all x1, waiting for transfers between devices, panel_step(): lax.all_to_all(sent.reshape(col_count, share, wide), 'col', 0, 0, tiled=T...  8.07 us
    all_to_all x1, starting transfers between devices, panel_step(): lax.all_to_all(sent.reshape(col_count, share, wide), 'col', 0, 0, tiled=T...  6.84 us
    all_to_all x1, starting transfers between devices, panel_step(): received = lax.all_to_all(jnp.moveaxis(chosen, 1, 0), ROW, 0, 0, tiled=True)  6.46 us
  transfers between devices with their start and end apart: 6, of which 6 were waited for; matrix products, arithmetic and copies ran while one was open for 17% of the time, Pallas kernels for 2%

profile of v3, /device:TPU:8, one launch (start us, length us, event | category | flops | bytes accessed | tf_op | source)
XLA Modules:
  0.0 129.0 jit_solution(14405122075622252350)
XLA Ops:
  0.0 1.7 %copy.33 = f32[1,384,32]{2,1,0:T(8,128)} copy(f32[1,384,32]{1,2,0:T(8,128)} %param.22) | data formatting | bytes 98304 | tf_op args[1]
  1.7 0.6 pad_add_fusion.1.device_ref
  2.3 3.6 %block_slots.1 = (s32[16,128]{1,0:T(8,128)}, s32[16,128]{1,0:T(8,128)}, f32[8,32,256]{2,1,0:T(8,128)}) custom-call(s32[2]{0:T(128)} %pad_add_fusion.1.device_ref, s32[1,6144]{1,0:T(1,128)} %rows_ref.3, s32[1,512]{1,0:T(1,128)} %cols_ref.1, f32[384,32]{1,0:T(8,128)} %bitcast.5.factor_ref), custom_call_target="tpu_custom_call" | custom-call | tf_op jit(solution)/shard_map/block_slots/pallas_call | solution.py:168
  5.8 8.7 %all-to-all-start = ((f32[8,32,256]{2,1,0:T(8,128)}), f32[8,32,256]{2,1,0:T(8,128)S(1)}, u32[]{:S(2)}, u32[]{:S(2)}) async-start(f32[8,32,256]{2,1,0:T(8,128)} %get-tuple-element.856), calls=%async_computation | async-start | bytes 524288 | tf_op jit(solution)/shard_map/all_to_all | solution.py:248
  14.5 0.7 slice_bitcast_fusion
  15.4 0.9 convolution_bitcast_fusion.1
  16.4 0.5 convolution_bitcast_fusion.3
  16.9 0.5 convolution_bitcast_fusion.2
  17.3 0.5 broadcast.138
  17.8 0.6 reduce.5
  18.7 0.5 fusion.99
  19.2 0.6 pad_add_fusion.panel_ref
  19.8 0.9 copy.32.other_ref
  20.7 2.2 %panel_places.1 = s32[8,512]{1,0:T(8,128)} custom-call(s32[2,512]{1,0:T(2,128)} %pad_add_fusion.panel_ref, s32[512,1]{1,0:T(8,128)} %copy.32.other_ref, s32[1,6144]{1,0:T(1,128)} %rows_ref.3), custom_call_target="tpu_custom_call" | custom-call | tf_op jit(solution)/shard_map/panel_places/pallas_call | solution.py:215
  22.8 2.2 %fusion.97 = (s32[1,512]{1,0:T(1,128)S(1)}, s32[1,512]{1,0:T(1,128)}, s32[]{:T(128)}, s32[]{:T(128)}, s32[1,512]{1,0:T(1,128)S(1)}) fusion(s32[8,512]{1,0:T(8,128)} %panel_places.1, s32[]{:T(128)S(6)} %mul.82), kind=kLoop, calls=%fused_computation.185 | loop fusion | flops 1534 | bytes 14348 | tf_op jit(solution)/shard_map/slice | solution.py:268
  25.0 3.5 %all-to-all-done = f32[8,32,256]{2,1,0:T(8,128)S(1)} async-done(((f32[8,32,256]{2,1,0:T(8,128)}), f32[8,32,256]{2,1,0:T(8,128)S(1)}, u32[]{:S(2)}, u32[]{:S(2)}) %all-to-all-start) | async-done | bytes 262176 | tf_op jit(solution)/shard_map/all_to_all | solution.py:248
  28.5 1.9 %collective-permute-start.5 = (f32[256,256]{1,0:T(8,128)S(1)}, f32[256,256]{1,0:T(8,128)S(1)}, u32[]{:S(2)}, u32[]{:S(2)}) collective-permute-start(f32[256,256]{1,0:T(8,128)S(1)} %bitcast.121), channel_id=1, source_target_pairs={{0,32},{32,0},{1,33},{33,1},{2,34},{34,2},{3,35},{35,3},{4,36},{36... | collective-permute-start | bytes 786440 | tf_op jit(solution)/shard_map/ppermute | solution.py:250
  30.4 0.8 slice_bitcast_fusion.2
  31.2 0.7 collective-permute-done.5
  31.9 2.0 %convolution_negate_fusion.1 = f32[512,512]{1,0:T(8,128)} fusion(f32[512,256]{1,0:T(8,128)S(1)} %bitcast.114, f32[256,256]{1,0:T(8,128)S(1)} %collective-permute-done.5, f32[256,256]{1,0:T(8,128)S(1)} %bitcast.122), kind=kOutput, calls=%fused_computation.56 | convolution fusion | flops 805699584 | bytes 2097152 | tf_op jit(solution)/shard_map/dot_general | solution.py:20
  33.9 12.2 %all-to-all-start.1 = ((f32[32,16,512]{2,1,0:T(8,128)}), f32[32,16,512]{2,1,0:T(8,128)S(1)}, u32[]{:S(2)}, u32[]{:S(2)}) async-start(f32[32,16,512]{2,1,0:T(8,128)} %bitcast.16), calls=%async_computation.1 | async-start | bytes 2097152 | tf_op jit(solution)/shard_map/all_to_all | solution.py:42
  46.2 0.6 slice.190
  48.1 0.8 copy.37
  48.9 0.6 broadcast_compare_fusion.6
  49.5 0.3 fusion.47
  49.9 0.7 fusion.72
  50.6 0.9 iota_compare_fusion.5
  51.5 2.9 %fusion.31 = f32[1024,256]{1,0:T(8,128)} fusion(s32[512]{0:T(512)S(1)} %bitcast.132, f32[256,256]{1,0:T(8,128)S(1)} %copy-done.8, f32[256,256]{1,0:T(8,128)S(1)} %bitcast.123), kind=kOutput, calls=%fused_computation.54 | convolution fusion | flops 1611268096 | bytes 1574912 | tf_op jit(solution)/shard_map/dot_general | solution.py:20
  54.4 18.5 %all-to-all-done.1 = f32[32,16,512]{2,1,0:T(8,128)S(1)} async-done(((f32[32,16,512]{2,1,0:T(8,128)}), f32[32,16,512]{2,1,0:T(8,128)S(1)}, u32[]{:S(2)}, u32[]{:S(2)}) %all-to-all-start.1) | async-done | bytes 1048608 | tf_op jit(solution)/shard_map/all_to_all | solution.py:42
  73.0 0.8 fusion.27
  73.8 0.6 fusion.71
  74.4 6.5 %all-to-all-start.2 = ((f32[16,8,128]{2,1,0:T(8,128)}), f32[16,8,128]{2,1,0:T(8,128)S(1)}, u32[]{:S(2)}, u32[]{:S(2)}) async-start(f32[16,8,128]{2,1,0:T(8,128)} %fusion.71), calls=%async_computation.2 | async-start | bytes 131072 | tf_op jit(solution)/shard_map/all_to_all | solution.py:279
  80.9 0.8 fusion.28
  81.7 9.3 %all-to-all-done.2 = f32[16,8,128]{2,1,0:T(8,128)S(1)} async-done(((f32[16,8,128]{2,1,0:T(8,128)}), f32[16,8,128]{2,1,0:T(8,128)S(1)}, u32[]{:S(2)}, u32[]{:S(2)}) %all-to-all-start.2) | async-done | bytes 65568 | tf_op jit(solution)/shard_map/all_to_all | solution.py:279
  91.0 0.7 pad_maximum_fusion.4
  91.7 6.8 %all-to-all-start.3 = ((f32[32,8,128]{2,1,0:T(8,128)}), f32[32,8,128]{2,1,0:T(8,128)S(1)}, u32[]{:S(2)}, u32[]{:S(2)}) async-start(f32[32,8,128]{2,1,0:T(8,128)} %bitcast.25), calls=%async_computation.3 | async-start | bytes 262144 | tf_op jit(solution)/shard_map/all_to_all | solution.py:284
  98.5 1.3 fusion.94
  99.8 8.1 %all-to-all-done.3 = f32[32,8,128]{2,1,0:T(8,128)S(1)} async-done(((f32[32,8,128]{2,1,0:T(8,128)}), f32[32,8,128]{2,1,0:T(8,128)S(1)}, u32[]{:S(2)}, u32[]{:S(2)}) %all-to-all-start.3) | async-done | bytes 131104 | tf_op jit(solution)/shard_map/all_to_all | solution.py:284
  107.9 0.8 slice_select_fusion.1
  108.6 0.4 fusion.40
  109.0 1.7 %convolution_subtract_fusion = f32[512,128]{1,0:T(8,128)} fusion(f32[512,256]{1,0:T(8,128)S(1)} %bitcast.116, f32[512,256]{1,0:T(8,128)S(1)} %bitcast.115, f32[64,256]{0,1:T(8,128)S(1)} %get-tuple-element.1035, f32[512,64]{1,0:T(8,128)S(1)} %bitcast.120, f32[512,64]{1,0:T(8,128)S(1)} %bitcast.119), kind=kOutput, calls=%fused_computation.62 | convolution fusion | flops 403374080 | bytes 1638400 | tf_op jit(solution)/shard_map/dot_general | solution.py:20
  110.7 4.9 %all-to-all-start.4 = ((f32[32,16,128]{2,1,0:T(8,128)}), f32[32,16,128]{2,1,0:T(8,128)S(1)}, u32[]{:S(2)}, u32[]{:S(2)}) async-start(f32[32,16,128]{2,1,0:T(8,128)} %bitcast.39), calls=%async_computation.4 | async-start | bytes 524288 | tf_op jit(solution)/shard_map/all_to_all | solution.py:42
  115.7 1.2 fusion.42
  116.9 1.3 %fusion.38 = f32[384,32]{0,1:T(8,128)S(1)} fusion(pred[1152,256]{1,0:T(32,128)(4,1)S(1)} %iota_compare_fusion.4, f32[64,256]{0,1:T(8,128)} %get-tuple-element.1034), kind=kOutput, calls=%fused_computation.74 | convolution fusion | flops 37748736 | bytes 212992 | tf_op jit(solution)/shard_map/dot_general | solution.py:20
  118.3 0.4 fusion.51
  118.7 0.4 fusion.48
  119.0 7.6 %all-to-all-done.4 = f32[32,16,128]{2,1,0:T(8,128)S(1)} async-done(((f32[32,16,128]{2,1,0:T(8,128)}), f32[32,16,128]{2,1,0:T(8,128)S(1)}, u32[]{:S(2)}, u32[]{:S(2)}) %all-to-all-start.4) | async-done | bytes 262176 | tf_op jit(solution)/shard_map/all_to_all | solution.py:42
  127.3 1.7 %convolution_select_fusion.3 = f32[768,384]{1,0:T(8,128)} fusion(f32[768,384]{1,0:T(8,128)S(1)} %copy-done.1, f32[384,384]{1,0:T(8,128)S(1)} %fusion.48, f32[384,384]{1,0:T(8,128)S(1)} %fusion.51, pred[384]{0:T(512)(128)(4,1)S(1)} %slice.222, pred[384]{0:T(512)(128)(4,1)S(1)} %copy-done.17, pred[768]{0:T(1024)(128)(4,1)S(1)} %copy-done.13, ...), kind=kOutput, calls=%fused_computation.55 | convolution fusion | flops 58761216 | bytes 3713280 | tf_op jit(solution)/shard_map/dot_general | solution.py:332
  (53 shorter events, 1.5 us)
Async XLA Ops:
  0.0 15.4 %copy-start.1 = (f32[768,384]{1,0:T(8,128)S(1)}, f32[768,384]{1,0:T(8,128)}, u32[]{:S(2)}) copy-start(f32[768,384]{1,0:T(8,128)} %param.21) | copy-start | bytes 3538948
  5.8 22.7 %all-to-all-start = ((f32[8,32,256]{2,1,0:T(8,128)}), f32[8,32,256]{2,1,0:T(8,128)S(1)}, u32[]{:S(2)}, u32[]{:S(2)}) async-start(f32[8,32,256]{2,1,0:T(8,128)} %get-tuple-element.856), calls=%async_computation | async-start | bytes 524288 | tf_op jit(solution)/shard_map/all_to_all | solution.py:248
  16.4 1.4 %copy-start.9 = (s32[1,512]{1,0:T(1,128)S(1)}, s32[1,512]{1,0:T(1,128)}, u32[]{:S(2)}) copy-start(s32[1,512]{1,0:T(1,128)} %cols_ref.1) | copy-start | bytes 6148
  16.4 2.3 %copy-start.10 = (s32[16,128]{1,0:T(8,128)S(1)}, s32[16,128]{1,0:T(8,128)}, u32[]{:S(2)}) copy-start(s32[16,128]{1,0:T(8,128)} %get-tuple-element.854) | copy-start | bytes 24580
  16.4 2.3 %copy-start.12 = (s32[16,128]{1,0:T(8,128)S(1)}, s32[16,128]{1,0:T(8,128)}, u32[]{:S(2)}) copy-start(s32[16,128]{1,0:T(8,128)} %get-tuple-element.855) | copy-start | bytes 24580
  28.5 3.4 %collective-permute-start.5 = (f32[256,256]{1,0:T(8,128)S(1)}, f32[256,256]{1,0:T(8,128)S(1)}, u32[]{:S(2)}, u32[]{:S(2)}) collective-permute-start(f32[256,256]{1,0:T(8,128)S(1)} %bitcast.121), channel_id=1, source_target_pairs={{0,32},{32,0},{1,33},{33,1},{2,34},{34,2},{3,35},{35,3},{4,36},{36... | collective-permute-start | bytes 786440 | tf_op jit(solution)/shard_map/ppermute | solution.py:250
  31.9 2.0 %copy-start.7 = (f32[256,256]{1,0:T(8,128)}, f32[256,256]{1,0:T(8,128)S(1)}, u32[]{:S(2)}) copy-start(f32[256,256]{1,0:T(8,128)S(1)} %collective-permute-done.5) | copy-start | bytes 786436
  33.9 14.2 %copy-start.11 = (f32[1,16,512]{2,1,0:T(8,128)S(1)}, f32[1,16,512]{2,1,0:T(8,128)}, u32[]{:S(2)}) copy-start(f32[1,16,512]{2,1,0:T(8,128)} %param.23) | copy-start | bytes 98308
  33.9 39.0 %all-to-all-start.1 = ((f32[32,16,512]{2,1,0:T(8,128)}), f32[32,16,512]{2,1,0:T(8,128)S(1)}, u32[]{:S(2)}, u32[]{:S(2)}) async-start(f32[32,16,512]{2,1,0:T(8,128)} %bitcast.16), calls=%async_computation.1 | async-start | bytes 2097152 | tf_op jit(solution)/shard_map/all_to_all | solution.py:42
  46.1 5.4 %copy-start.14 = (s32[1,512]{1,0:T(1,128)S(1)}, s32[1,512]{1,0:T(1,128)}, u32[]{:S(2)}) copy-start(s32[1,512]{1,0:T(1,128)} %get-tuple-element.1045) | copy-start | bytes 6148
  48.9 2.6 %copy-start.8 = (f32[256,256]{1,0:T(8,128)S(1)}, f32[256,256]{1,0:T(8,128)}, u32[]{:S(2)}) copy-start(f32[256,256]{1,0:T(8,128)} %copy-done.7) | copy-start | bytes 786436
  74.4 16.5 %all-to-all-start.2 = ((f32[16,8,128]{2,1,0:T(8,128)}), f32[16,8,128]{2,1,0:T(8,128)S(1)}, u32[]{:S(2)}, u32[]{:S(2)}) async-start(f32[16,8,128]{2,1,0:T(8,128)} %fusion.71), calls=%async_computation.2 | async-start | bytes 131072 | tf_op jit(solution)/shard_map/all_to_all | solution.py:279
  80.9 10.1 %copy-start.15 = (pred[128]{0:T(512)(128)(4,1)S(1)}, pred[128]{0:T(512)(128)(4,1)}, u32[]{:S(2)}) copy-start(pred[128]{0:T(512)(128)(4,1)} %get-tuple-element.1058) | copy-start | bytes 388
  80.9 10.1 %copy-start.16 = (pred[128]{0:T(512)(128)(4,1)S(1)}, pred[128]{0:T(512)(128)(4,1)}, u32[]{:S(2)}) copy-start(pred[128]{0:T(512)(128)(4,1)} %get-tuple-element.1059) | copy-start | bytes 388
  91.7 16.2 %all-to-all-start.3 = ((f32[32,8,128]{2,1,0:T(8,128)}), f32[32,8,128]{2,1,0:T(8,128)S(1)}, u32[]{:S(2)}, u32[]{:S(2)}) async-start(f32[32,8,128]{2,1,0:T(8,128)} %bitcast.25), calls=%async_computation.3 | async-start | bytes 262144 | tf_op jit(solution)/shard_map/all_to_all | solution.py:284
  109.0 9.2 %copy-start.6 = (pred[1152,32]{1,0:T(32,128)(4,1)S(1)}, pred[1152,32]{1,0:T(32,128)(4,1)}, u32[]{:S(2)}) copy-start(pred[1152,32]{1,0:T(32,128)(4,1)} %iota_compare_fusion.5) | copy-start | bytes 110596
  110.7 15.9 %all-to-all-start.4 = ((f32[32,16,128]{2,1,0:T(8,128)}), f32[32,16,128]{2,1,0:T(8,128)S(1)}, u32[]{:S(2)}, u32[]{:S(2)}) async-start(f32[32,16,128]{2,1,0:T(8,128)} %bitcast.39), calls=%async_computation.4 | async-start | bytes 524288 | tf_op jit(solution)/shard_map/all_to_all | solution.py:42
  118.3 9.1 %copy-start.13 = (pred[768]{0:T(1024)(128)(4,1)S(1)}, pred[768]{0:T(1024)(128)(4,1)}, u32[]{:S(2)}) copy-start(pred[768]{0:T(1024)(128)(4,1)} %get-tuple-element.1055) | copy-start | bytes 2308
  118.3 9.1 %copy-start.17 = (pred[384]{0:T(512)(128)(4,1)S(1)}, pred[384]{0:T(512)(128)(4,1)}, u32[]{:S(2)}) copy-start(pred[384]{0:T(512)(128)(4,1)} %slice.190) | copy-start | bytes 1156

commit v4 on v3

--- a/solution.py
+++ b/solution.py
@@ -8,7 +8,9 @@
 from jax.sharding import Mesh
 from jax.sharding import PartitionSpec as P
 
+
 ROW = ("row_0", "row_1", "row_2")
+COL = ("col_0", "col_1")
 HIGHEST = lax.Precision.HIGHEST
 LANES = 128
 LINES = 16
@@ -56,12 +58,12 @@
 
 def general_panel(matrix, factor, dinv, panel_cols, row_in, col_in):
     row_count = lax.axis_size(ROW)
-    ratio = lax.axis_size("col") // row_count
+    ratio = lax.axis_size(COL) // row_count
     row_block, col_block = matrix.shape
     width = panel_cols.shape[0]
     group = factor.shape[1]
     row_pos = lax.axis_index(ROW)
-    col_pos = lax.axis_index("col")
+    col_pos = lax.axis_index(COL)
     row_ids = row_pos * row_block + jnp.arange(row_block, dtype=jnp.int32)
     col_ids = col_pos * col_block + jnp.arange(col_block, dtype=jnp.int32)
     masked = factor * col_in[:, None].astype(jnp.float32)
@@ -73,7 +75,7 @@
     def products(turn, carried):
         out, gram = carried
         lower = ring_sum(jnp.where(row_pos == turn, masked, jnp.zeros_like(masked)), ROW)
-        by_row = ring_sum(-dot(matrix, lower), "col")
+        by_row = ring_sum(-dot(matrix, lower), COL)
         mine = lax.dynamic_slice_in_dim(by_row, col_pos % ratio * col_block, col_block, 0)
         mine = jnp.where(row_pos == col_pos // ratio, mine, jnp.zeros_like(mine))
         by_col = ring_sum(mine, ROW)
@@ -95,7 +97,7 @@
     out, gram = lax.fori_loop(0, row_count, products, (matrix, none))
     placed = lax.dynamic_update_slice(none, dinv, (col_pos * dinv.shape[0], 0))
     placed = jnp.where(row_pos == 0, placed, none)
-    diagonal = ring_sum(ring_sum(placed - gram, ROW), "col")
+    diagonal = ring_sum(ring_sum(placed - gram, ROW), COL)
     put_rows = (row_ids[:, None] == panel_cols).astype(jnp.float32)
     there = jnp.sum(put_rows, axis=1) > 0.5
 
@@ -109,9 +111,7 @@
     return lax.fori_loop(0, row_count, corners, out)
 
 
-def slots_kernel(
-    lines, lanes, device_ref, rows_ref, cols_ref, factor_ref, row_slots_ref, col_slots_ref, packed_ref
-):
+def slots_kernel(lines, lanes, device_ref, rows_ref, cols_ref, row_slots_ref, col_slots_ref):
     line = lax.broadcasted_iota(jnp.int32, (LINES, 1), 0)
     own = jnp.where(
         line < lines, device_ref[0] * lines + line, device_ref[1] * lines + line - lines
@@ -147,33 +147,23 @@
                 later = (line > other) & (line < (other // lines + 1) * lines)
                 before += jnp.where(later, held[other : other + 1], 0.0)
         out_ref[...] = jnp.where(found > 0.5, before, -1.0).astype(jnp.int32)
-    copies, group, slots = packed_ref.shape
-    place = lax.broadcasted_iota(jnp.int32, (slots, lanes), 0)
-    packed = jnp.zeros((slots, group), jnp.float32)
-    for part in range(lines):
-        hot = (place == row_slots_ref[part : part + 1, :]).astype(jnp.float32)
-        held = factor_ref[part * lanes : (part + 1) * lanes, :]
-        packed += jnp.dot(hot, held, precision=HIGHEST, preferred_element_type=jnp.float32)
-    packed_ref[...] = jnp.broadcast_to(packed.T[None], packed_ref.shape)
-
-
-def block_slots(row_slots, ratio, factor, panel_cols, row_lists):
-    col_block, group = factor.shape
-    copies = lax.axis_size(ROW[:2])
+
+
+def block_slots(col_block, ratio, panel_cols, row_lists):
     lanes = LANES if col_block % LANES == 0 else col_block
     lines = col_block // lanes
-    device = jnp.stack([lax.axis_index("col"), lax.axis_index(ROW) * ratio]).astype(jnp.int32)
+    device = jnp.stack([lax.axis_index(COL), lax.axis_index(ROW) * ratio]).astype(jnp.int32)
     shape = jax.ShapeDtypeStruct((LINES, lanes), jnp.int32)
     whole = pl.BlockSpec(memory_space=pltpu.VMEM)
     found = pl.pallas_call(
         functools.partial(slots_kernel, lines, lanes),
-        out_shape=(shape, shape, jax.ShapeDtypeStruct((copies, group, row_slots), jnp.float32)),
-        in_specs=[pl.BlockSpec(memory_space=pltpu.SMEM), whole, whole, whole],
-        out_specs=(whole, whole, whole),
+        out_shape=(shape, shape),
+        in_specs=[pl.BlockSpec(memory_space=pltpu.SMEM), whole, whole],
+        out_specs=(whole, whole),
         name="block_slots",
-    )(device, row_lists[None], panel_cols[None], factor)
+    )(device, row_lists[None], panel_cols[None])
     used = (1 + ratio) * lines
-    return [slots[:used].reshape(used * lanes) for slots in found[:2]] + [found[2]]
+    return [slots[:used].reshape(used * lanes) for slots in found]
 
 
 def one_hot(slot, count, dtype=jnp.float32):
@@ -211,7 +201,7 @@
 def panel_places(col_slots, col_block, ratio, col_count, group, panel_cols, row_lists):
     width = panel_cols.shape[0]
     by_core = jnp.moveaxis(panel_cols.reshape(-1, 2, group), 1, 0).reshape(2, width // 2)
-    local = jnp.where(lax.axis_index(ROW[2]) == 0, by_core, by_core[::-1]).reshape(width)
+    local = jnp.where(lax.axis_index(COL[1]) == 0, by_core, by_core[::-1]).reshape(width)
     return pl.pallas_call(
         functools.partial(places_kernel, (col_block, ratio, col_slots, col_count)),
         out_shape=jax.ShapeDtypeStruct((8, width), jnp.int32),
@@ -221,21 +211,19 @@
 
 def panel_step(matrix, factor, dinv, panel_cols, row_lists):
     row_count = lax.axis_size(ROW)
-    col_count = lax.axis_size("col")
+    col_count = lax.axis_size(COL)
     ratio = col_count // row_count
-    row_block, col_block = matrix.shape
+    _, col_block = matrix.shape
     width = panel_cols.shape[0]
     dinv_rows = dinv.shape[0]
     row_slots = col_block * 2 // 3
     col_slots = 2 * (width // col_count)
     row_k = ratio * col_slots
     row_pos = lax.axis_index(ROW)
-    col_pos = lax.axis_index("col")
-    side = col_pos % ratio
-
-    list_slot, panel_slot, packed = block_slots(
-        row_slots, ratio, factor, panel_cols, row_lists
-    )
+    col_pos = lax.axis_index(COL)
+    side = lax.axis_index(COL[1])
+
+    list_slot, panel_slot = block_slots(col_block, ratio, panel_cols, row_lists)
     in_list, in_panel = list_slot >= 0, panel_slot >= 0
     col_in, row_in = in_list[:col_block], in_list[col_block:]
     col_panel, row_panel = in_panel[:col_block], in_panel[col_block:]
@@ -245,19 +233,36 @@
     put = one_hot(panel_slot, col_slots)
     put_rows = put[col_block:].reshape(ratio, col_block, col_slots)
 
-    own_half = lax.all_to_all(packed, ROW[:2], 0, 0, tiled=True)
-    own_half = own_half.reshape(width // 2, row_slots)
-    other_half = lax.ppermute(own_half, ROW[2], [(0, 1), (1, 0)])
-    lower = jnp.concatenate([own_half, other_half])
+    narrow_pick = one_hot(list_slot[:col_block], row_slots, jnp.bfloat16)
+    packed = selected(thirds(factor, 1), narrow_pick, BY_FIRST)
+
+    core = lax.axis_index(ROW[2])
+    packed = lax.ppermute(packed, (ROW[2], COL[1]), [(0, 0), (1, 2), (2, 1), (3, 3)])
+    swap = [(0, 1), (1, 0)]
+    copies = jnp.broadcast_to(packed, (lax.axis_size(ROW[:2]), *packed.shape))
+    this_block = lax.all_to_all(copies, ROW[:2], 0, 0, tiled=True)
+    this_block = this_block.reshape(width // 2, row_slots)
+    that_block = lax.ppermute(this_block, ROW[2], swap)
+    own_lower = jnp.where(core == side, this_block, that_block)
+    pair_lower = jnp.where(core == side, that_block, this_block)
 
     narrow = dot(matrix, pick_cols).reshape(ratio, col_block, row_slots)
     dense = jnp.stack([dot(pick_rows[part], narrow[part], BY_FIRST) for part in range(ratio)])
-    share = row_slots // col_count
-    dense = jnp.moveaxis(dense.reshape(ratio, col_count, share, row_slots), 0, 1)
+    owners = col_count // ratio
+    share = row_slots // owners
+    dense = jnp.moveaxis(dense.reshape(ratio, owners, share, row_slots), 0, 1)
     dense = dense.reshape(ratio * row_slots, row_slots)
-
-    partial_value = -dot(dense, lower, BY_LAST)
-    summed = sum_at_owner(partial_value.reshape(col_count, ratio * share, width), "col")
+    pair_dense = lax.ppermute(dense, COL[1], swap)
+
+    partial_value = -dot(
+        jnp.concatenate([dense, pair_dense], axis=1),
+        jnp.concatenate([own_lower, pair_lower], axis=1),
+        BY_LAST,
+    )
+    summed = sum_at_owner(partial_value.reshape(owners, ratio * share, width // 2), COL[0])
+
+    rest_lower = lax.ppermute(pair_lower, COL[1], swap)
+    lower = jnp.concatenate([own_lower, rest_lower])
 
     wide = ratio * row_k
     half_slots = col_slots // 2
@@ -268,7 +273,7 @@
     slot, local_slot = found[0], found[1]
 
     def route(places):
-        return one_hot(places.reshape(ratio * width), row_count * wide, jnp.bfloat16)
+        return one_hot(places[:, : width // 2].reshape(-1), row_count * wide, jnp.bfloat16)
 
     to_rows = route(found[2:4])
     to_cols = route(found[4:6])
@@ -282,8 +287,9 @@
     lane = jnp.arange(wide, dtype=jnp.int32) // row_k
     sent = jnp.stack([jnp.where(lane == part, received, own) for part in range(ratio)], axis=1)
     arrived = lax.all_to_all(
-        sent.reshape(col_count, share, wide), "col", 0, 0, tiled=True
-    )
+        sent.reshape(col_count, share, wide), COL, 0, 0, tiled=True
+    )
+    arrived = jnp.sum(arrived.reshape(owners, ratio, share, wide), axis=1)
     arrived = arrived.reshape(row_slots, wide).T
     upper, under = arrived[:row_k], arrived[row_k:]
     beside = jnp.where(side == 0, upper, under)
@@ -305,7 +311,7 @@
         [jnp.concatenate([beside, empty], axis=1), jnp.concatenate([empty, beside], axis=1)]
     )
     terms = placed_pair - dot(lower_pair, beside_pair, BY_LAST)
-    corner = sum_at_owner(terms.reshape(col_count, half_slots, 2 * row_k), "col")
+    corner = sum_at_owner(terms.reshape(col_count, half_slots, 2 * row_k), COL)
 
     below_rows = [dot(pick_rows[part], below[part * col_slots : (part + 1) * col_slots], BY_LAST) for part in range(ratio)]
     spread_out = dot(beside, pick_cols, BY_LAST)
@@ -350,20 +356,18 @@
 def on_device(resident, factor, dinv, panel_cols, row_lists):
     matrix = resident
     for panel in reversed(range(factor.shape[0])):
-        matrix = panel_step(
-            matrix, factor[panel], dinv[panel], panel_cols[panel], row_lists[panel]
-        )
+        matrix = panel_step(matrix, factor[panel], dinv[panel], panel_cols[panel], row_lists[panel])
     return matrix
 
 
 def solution(mesh):
     finer = Mesh(
-        mesh.devices.reshape(-1, 2, 2, mesh.shape["col"]), ("row_0", "row_1", "row_2", "col")
+        mesh.devices.reshape(-1, 2, 2, mesh.shape["col"] // 2, 2), ROW + COL
     )
     return jax.shard_map(
         on_device,
         mesh=finer,
-        in_specs=(P(ROW, "col"), P(None, "col", ROW), P(None, "col", None), P(), P()),
-        out_specs=P(ROW, "col"),
+        in_specs=(P(ROW, COL), P(None, COL, ROW), P(None, COL, None), P(), P()),
+        out_specs=P(ROW, COL),
         check_vma=False,
     )

time: 130 us -> 134 us (1.031)
  waiting for transfers between devices: 47.6 us -> 52.3 us
  starting transfers between devices: 41 us -> 45.5 us
  matrix products: 16.9 us -> 14.9 us
    all_to_all x2, waiting for transfers between devices: 11.5 us -> 20.9 us  [the longest x1 11.6 us: panel_step(): this_block = lax.all_to_all(copies, ROW[:2], 0, 0, tiled=True)]
    ppermute x1 -> x4, starting transfers between devices: 1.91 us -> 10.9 us  [the longest x1 5.54 us: panel_step(): pair_dense = lax.ppermute(dense, COL[1], swap)]
    all_to_all x1, waiting for transfers between devices: 9.28 us -> 5.67 us  [panel_step(): received = lax.all_to_all(jnp.moveaxis(chosen, 1, 0), ROW, 0, 0, tiled=True)]
    all_to_all x1, starting transfers between devices: 6.46 us -> 3.51 us  [panel_step(): received = lax.all_to_all(jnp.moveaxis(chosen, 1, 0), ROW, 0, 0, tiled=True)]
    dot_general x15, matrix products: 13.6 us -> 11.9 us  [dot(): lax.dot_general(a, b, (dims, ((), ())), precision=HIGHEST, preferred_elem...]
    unnamed x33 -> x20, local copies, waits for them, and re-layouts: 3.87 us -> 2.16 us
  transfers between devices with their start and end apart: 6 -> 9, of which waited for: 6 -> 6; matrix products, arithmetic and copies ran while one was open for 17% -> 14% of each run, Pallas kernels for 2% -> 2%
where the time goes in v4:
time: 134 us; the launch traced here: 133 us
  waiting for transfers between devices  52.3 us (39%)
  starting transfers between devices  45.5 us (34%)
  matrix products  14.9 us (11%)
  other arithmetic  7.29 us (5%)
  local copies, waits for them, and re-layouts  6.43 us (5%)
  Pallas kernels  4.42 us (3%)
  between operations  1.72 us (1%)
    all_to_all x2, waiting for transfers between devices, sum_at_owner(): return jnp.sum(lax.all_to_all(blocks, axis, 0, 0, tiled=True), axis=0)  24.9 us
    all_to_all x2, starting transfers between devices, sum_at_owner(): return jnp.sum(lax.all_to_all(blocks, axis, 0, 0, tiled=True), axis=0)  16.2 us
    dot_general x15, matrix products, dot(): lax.dot_general(a, b, (dims, ((), ())), precision=HIGHEST, preferred_elem...  11.9 us
    all_to_all x1, waiting for transfers between devices, panel_step(): this_block = lax.all_to_all(copies, ROW[:2], 0, 0, tiled=True)  11.6 us
    all_to_all x1, waiting for transfers between devices, panel_step(): lax.all_to_all(sent.reshape(col_count, share, wide), COL, 0, 0, tiled=True)  9.3 us
    all_to_all x1, starting transfers between devices, panel_step(): this_block = lax.all_to_all(copies, ROW[:2], 0, 0, tiled=True)  8.66 us
    all_to_all x1, starting transfers between devices, panel_step(): lax.all_to_all(sent.reshape(col_count, share, wide), COL, 0, 0, tiled=True)  6.18 us
    all_to_all x1, waiting for transfers between devices, panel_step(): received = lax.all_to_all(jnp.moveaxis(chosen, 1, 0), ROW, 0, 0, tiled=True)  5.67 us
  transfers between devices with their start and end apart: 9, of which 6 were waited for; matrix products, arithmetic and copies ran while one was open for 14% of the time, Pallas kernels for 2%

profile of v4, /device:TPU:8, one launch (start us, length us, event | category | flops | bytes accessed | tf_op | source)
XLA Modules:
  0.0 132.6 jit_solution(12604033738476714329)
XLA Ops:
  0.0 0.8 reduce-precision_convert_fusion.3
  0.8 0.7 pad_add_fusion.1.device_ref
  1.5 2.2 %block_slots.1 = (s32[16,128]{1,0:T(8,128)}, s32[16,128]{1,0:T(8,128)}) custom-call(s32[2]{0:T(128)} %pad_add_fusion.1.device_ref, s32[1,6144]{1,0:T(1,128)} %rows_ref.3, s32[1,512]{1,0:T(1,128)} %cols_ref.1), custom_call_target="tpu_custom_call" | custom-call | tf_op jit(solution)/shard_map/block_slots/pallas_call | solution.py:158
  3.7 0.7 slice_bitcast_fusion.4
  4.7 0.7 collective-permute-start.6
  5.4 0.7 slice_bitcast_fusion
  6.3 2.2 %convolution_bitcast_fusion.1 = f32[768,256]{0,1:T(8,128)S(1)} fusion(f32[768,384]{1,0:T(8,128)} %param.21, pred[1152,256]{1,0:T(32,128)(4,1)S(1)} %iota_compare_fusion.4), kind=kOutput, calls=%fused_computation.56 | convolution fusion | flops 906067968 | bytes 2064384 | tf_op jit(solution)/shard_map/dot_general | solution.py:22
  8.6 0.5 fusion.45
  9.0 0.5 fusion.47
  9.6 5.5 %collective-permute-start.5 = (f32[512,256]{1,0:T(8,128)S(1)}, f32[512,256]{1,0:T(8,128)S(1)}, u32[]{:S(2)}, u32[]{:S(2)}) collective-permute-start(f32[512,256]{1,0:T(8,128)S(1)} %bitcast.138), channel_id=1, source_target_pairs={{0,1},{1,0},{2,3},{3,2},{4,5},{5,4},{6,7},{7,6},{8,9},{9,8},{10,11... | collective-permute-start | bytes 1572872 | tf_op jit(solution)/shard_map/ppermute | solution.py:255
  15.2 0.5 broadcast.137
  15.7 0.7 reduce.5
  16.6 0.6 pad_add_fusion.panel_ref
  17.2 0.9 copy.48.other_ref
  18.0 2.2 %panel_places.1 = s32[8,512]{1,0:T(8,128)} custom-call(s32[2,512]{1,0:T(2,128)} %pad_add_fusion.panel_ref, s32[512,1]{1,0:T(8,128)} %copy.48.other_ref, s32[1,6144]{1,0:T(1,128)} %rows_ref.3), custom_call_target="tpu_custom_call" | custom-call | tf_op jit(solution)/shard_map/panel_places/pallas_call | solution.py:205
  20.2 0.7 broadcast_in_dim.42
  20.9 8.7 %all-to-all-start = ((f32[8,32,256]{2,1,0:T(8,128)}), f32[8,32,256]{2,1,0:T(8,128)S(1)}, u32[]{:S(2)}, u32[]{:S(2)}) async-start(f32[8,32,256]{2,1,0:T(8,128)} %broadcast_in_dim.42), calls=%async_computation | async-start | bytes 524288 | tf_op jit(solution)/shard_map/all_to_all | solution.py:243
  29.6 0.8 slice_bitcast_fusion.2
  30.4 1.6 %fusion.121 = (s32[1,512]{1,0:T(1,128)S(1)}, s32[1,512]{1,0:T(1,128)S(1)}, s32[]{:T(128)}, s32[]{:T(128)}, s32[1,512]{1,0:T(1,128)S(1)}) fusion(s32[8,512]{1,0:T(8,128)} %panel_places.1, s32[]{:T(128)S(6)} %mul.90), kind=kLoop, calls=%fused_computation.218 | loop fusion | flops 1534 | bytes 14348 | tf_op jit(solution)/shard_map/slice | solution.py:273
  32.2 11.6 %all-to-all-done = f32[8,32,256]{2,1,0:T(8,128)S(1)} async-done(((f32[8,32,256]{2,1,0:T(8,128)}), f32[8,32,256]{2,1,0:T(8,128)S(1)}, u32[]{:S(2)}, u32[]{:S(2)}) %all-to-all-start) | async-done | bytes 262176 | tf_op jit(solution)/shard_map/all_to_all | solution.py:243
  43.9 1.9 %collective-permute-start.7 = (f32[256,256]{1,0:T(8,128)S(1)}, f32[256,256]{1,0:T(8,128)S(1)}, u32[]{:S(2)}, u32[]{:S(2)}) collective-permute-start(f32[256,256]{1,0:T(8,128)S(1)} %bitcast.148), channel_id=1, source_target_pairs={{0,32},{32,0},{1,33},{33,1},{2,34},{34,2},{3,35},{35,3},{4,36},{36... | collective-permute-start | bytes 786440 | tf_op jit(solution)/shard_map/ppermute | solution.py:245
  45.8 0.7 convert_convert_fusion.6
  46.6 0.7 collective-permute-done.7
  47.4 1.8 %convolution_negate_fusion.1 = f32[512,256]{1,0:T(8,128)} fusion(f32[512,256]{1,0:T(8,128)S(1)} %collective-permute-done.5, f32[512,256]{1,0:T(8,128)S(1)} %bitcast.139, f32[256,256]{1,0:T(8,128)S(1)} %get-tuple-element.1046, f32[256,256]{1,0:T(8,128)S(1)} %get-tuple-element.1045), kind=kOutput, calls=%fused_computation.57 | convolution fusion | flops 805830656 | bytes 2097152 | tf_op jit(solution)/shard_map/dot_general | solution.py:22
  49.2 11.0 %all-to-all-start.1 = ((f32[16,32,256]{2,1,0:T(8,128)}), f32[16,32,256]{2,1,0:T(8,128)S(1)}, u32[]{:S(2)}, u32[]{:S(2)}) async-start(f32[16,32,256]{2,1,0:T(8,128)} %bitcast.18), calls=%async_computation.1 | async-start | bytes 1048576 | tf_op jit(solution)/shard_map/all_to_all | solution.py:44
  60.2 0.7 fusion.94
  61.2 15.0 %all-to-all-done.1 = f32[16,32,256]{2,1,0:T(8,128)S(1)} async-done(((f32[16,32,256]{2,1,0:T(8,128)}), f32[16,32,256]{2,1,0:T(8,128)S(1)}, u32[]{:S(2)}, u32[]{:S(2)}) %all-to-all-start.1) | async-done | bytes 524320 | tf_op jit(solution)/shard_map/all_to_all | solution.py:44
  76.3 0.5 fusion.27
  76.9 0.7 bitcast_bitcast_fusion.1
  77.5 3.5 %all-to-all-start.2 = ((f32[16,16,128]{2,1,0:T(8,128)}), f32[16,16,128]{2,1,0:T(8,128)S(1)}, u32[]{:S(2)}, u32[]{:S(2)}) async-start(f32[16,16,128]{2,1,0:T(8,128)} %bitcast_bitcast_fusion.1), calls=%async_computation.2 | async-start | bytes 262144 | tf_op jit(solution)/shard_map/all_to_all | solution.py:284
  81.1 0.8 copy.54
  83.2 0.8 copy.56
  84.0 2.8 %collective-permute-start.8 = (f32[256,256]{1,0:T(8,128)S(1)}, f32[256,256]{1,0:T(8,128)S(1)}, u32[]{:S(2)}, u32[]{:S(2)}) collective-permute-start(f32[256,256]{1,0:T(8,128)S(1)} %get-tuple-element.1046), channel_id=1, source_target_pairs={{0,1},{1,0},{2,3},{3,2},{4,5},{5,4},{6,7},{7,6},{8,9},{9,8},{10,11... | collective-permute-start | bytes 786440 | tf_op jit(solution)/shard_map/ppermute | solution.py:264
  86.8 0.5 fusion.28
  87.4 5.7 %all-to-all-done.2 = f32[16,16,128]{2,1,0:T(8,128)S(1)} async-done(((f32[16,16,128]{2,1,0:T(8,128)}), f32[16,16,128]{2,1,0:T(8,128)S(1)}, u32[]{:S(2)}, u32[]{:S(2)}) %all-to-all-start.2) | async-done | bytes 131104 | tf_op jit(solution)/shard_map/all_to_all | solution.py:284
  93.1 0.7 pad_maximum_fusion.1
  93.8 6.2 %all-to-all-start.3 = ((f32[32,16,128]{2,1,0:T(8,128)}), f32[32,16,128]{2,1,0:T(8,128)S(1)}, u32[]{:S(2)}, u32[]{:S(2)}) async-start(f32[32,16,128]{2,1,0:T(8,128)} %bitcast.24), calls=%async_computation.3 | async-start | bytes 524288 | tf_op jit(solution)/shard_map/all_to_all | solution.py:289
  100.0 1.9 %fusion.31 = f32[1024,256]{1,0:T(8,128)S(1)} fusion(s32[512]{0:T(512)S(1)} %bitcast.160, f32[256,256]{1,0:T(8,128)S(1)} %collective-permute-done.8, f32[256,256]{1,0:T(8,128)S(1)} %get-tuple-element.1045), kind=kOutput, calls=%fused_computation.54 | convolution fusion | flops 1611268096 | bytes 1574912 | tf_op jit(solution)/shard_map/dot_general | solution.py:22
  102.0 9.3 %all-to-all-done.3 = f32[32,16,128]{2,1,0:T(8,128)S(1)} async-done(((f32[32,16,128]{2,1,0:T(8,128)}), f32[32,16,128]{2,1,0:T(8,128)S(1)}, u32[]{:S(2)}, u32[]{:S(2)}) %all-to-all-start.3) | async-done | bytes 262176 | tf_op jit(solution)/shard_map/all_to_all | solution.py:289
  111.4 0.4 fusion.51
  111.8 1.7 %convolution_subtract_fusion = f32[512,128]{1,0:T(8,128)} fusion(f32[512,256]{1,0:T(8,128)S(1)} %bitcast.141, f32[512,256]{1,0:T(8,128)S(1)} %bitcast.140, f32[64,256]{0,1:T(8,128)S(1)} %get-tuple-element.1050, f32[512,64]{1,0:T(8,128)S(1)} %bitcast.145, f32[512,64]{1,0:T(8,128)S(1)} %bitcast.144), kind=kOutput, calls=%fused_computation.60 | convolution fusion | flops 403374080 | bytes 1638400 | tf_op jit(solution)/shard_map/dot_general | solution.py:22
  113.5 5.2 %all-to-all-start.4 = ((f32[32,16,128]{2,1,0:T(8,128)}), f32[32,16,128]{2,1,0:T(8,128)S(1)}, u32[]{:S(2)}, u32[]{:S(2)}) async-start(f32[32,16,128]{2,1,0:T(8,128)} %bitcast.39), calls=%async_computation.4 | async-start | bytes 524288 | tf_op jit(solution)/shard_map/all_to_all | solution.py:44
  118.8 0.3 fusion.53
  119.1 0.4 fusion.49
  119.5 0.4 fusion.64
  119.9 0.4 fusion.61
  120.3 9.9 %all-to-all-done.4 = f32[32,16,128]{2,1,0:T(8,128)S(1)} async-done(((f32[32,16,128]{2,1,0:T(8,128)}), f32[32,16,128]{2,1,0:T(8,128)S(1)}, u32[]{:S(2)}, u32[]{:S(2)}) %all-to-all-start.4) | async-done | bytes 262176 | tf_op jit(solution)/shard_map/all_to_all | solution.py:44
  130.9 1.7 %convolution_select_fusion.3 = f32[768,384]{1,0:T(8,128)} fusion(f32[768,384]{1,0:T(8,128)S(1)} %copy-done.1, f32[384,384]{1,0:T(8,128)S(1)} %fusion.61, f32[384,384]{1,0:T(8,128)S(1)} %fusion.64, pred[384]{0:T(512)(128)(4,1)S(1)} %slice.247, pred[384]{0:T(512)(128)(4,1)S(1)} %slice.212, pred[768]{0:T(1024)(128)(4,1)S(1)} %get-tuple-element.1073, ...), kind=kOutput, calls=%fused_computation.55 | convolution fusion | flops 58761216 | bytes 3713280 | tf_op jit(solution)/shard_map/dot_general | solution.py:338
  (53 shorter events, 2.4 us)
Async XLA Ops:
  4.7 15.5 %collective-permute-start.6 = (f32[32,256]{1,0:T(8,128)S(1)}, f32[32,256]{1,0:T(8,128)S(1)}, u32[]{:S(2)}, u32[]{:S(2)}) collective-permute-start(f32[32,256]{1,0:T(8,128)S(1)} %slice_add_fusion.4), channel_id=1, source_target_pairs={{0,0},{1,32},{32,1},{33,33},{2,2},{3,34},{34,3},{35,35},{4,4},{5,3... | collective-permute-start | bytes 98312 | tf_op jit(solution)/shard_map/ppermute | solution.py:240
  8.5 6.6 %copy-start.11 = (s32[16,128]{1,0:T(8,128)S(1)}, s32[16,128]{1,0:T(8,128)}, u32[]{:S(2)}) copy-start(s32[16,128]{1,0:T(8,128)} %get-tuple-element.853) | copy-start | bytes 24580
  8.6 6.6 %copy-start.10 = (s32[16,128]{1,0:T(8,128)S(1)}, s32[16,128]{1,0:T(8,128)}, u32[]{:S(2)}) copy-start(s32[16,128]{1,0:T(8,128)} %get-tuple-element.854) | copy-start | bytes 24580
  8.6 7.1 %copy-start.8 = (s32[1,512]{1,0:T(1,128)S(1)}, s32[1,512]{1,0:T(1,128)}, u32[]{:S(2)}) copy-start(s32[1,512]{1,0:T(1,128)} %cols_ref.1) | copy-start | bytes 6148
  9.5 22.5 %copy-start.12 = (f32[1,16,512]{2,1,0:T(8,128)S(1)}, f32[1,16,512]{2,1,0:T(8,128)}, u32[]{:S(2)}) copy-start(f32[1,16,512]{2,1,0:T(8,128)} %param.23) | copy-start | bytes 98308
  9.6 37.8 %collective-permute-start.5 = (f32[512,256]{1,0:T(8,128)S(1)}, f32[512,256]{1,0:T(8,128)S(1)}, u32[]{:S(2)}, u32[]{:S(2)}) collective-permute-start(f32[512,256]{1,0:T(8,128)S(1)} %bitcast.138), channel_id=1, source_target_pairs={{0,1},{1,0},{2,3},{3,2},{4,5},{5,4},{6,7},{7,6},{8,9},{9,8},{10,11... | collective-permute-start | bytes 1572872 | tf_op jit(solution)/shard_map/ppermute | solution.py:255
  20.9 22.9 %all-to-all-start = ((f32[8,32,256]{2,1,0:T(8,128)}), f32[8,32,256]{2,1,0:T(8,128)S(1)}, u32[]{:S(2)}, u32[]{:S(2)}) async-start(f32[8,32,256]{2,1,0:T(8,128)} %broadcast_in_dim.42), calls=%async_computation | async-start | bytes 524288 | tf_op jit(solution)/shard_map/all_to_all | solution.py:243
  43.9 3.4 %collective-permute-start.7 = (f32[256,256]{1,0:T(8,128)S(1)}, f32[256,256]{1,0:T(8,128)S(1)}, u32[]{:S(2)}, u32[]{:S(2)}) collective-permute-start(f32[256,256]{1,0:T(8,128)S(1)} %bitcast.148), channel_id=1, source_target_pairs={{0,32},{32,0},{1,33},{33,1},{2,34},{34,2},{3,35},{35,3},{4,36},{36... | collective-permute-start | bytes 786440 | tf_op jit(solution)/shard_map/ppermute | solution.py:245
  49.2 27.1 %all-to-all-start.1 = ((f32[16,32,256]{2,1,0:T(8,128)}), f32[16,32,256]{2,1,0:T(8,128)S(1)}, u32[]{:S(2)}, u32[]{:S(2)}) async-start(f32[16,32,256]{2,1,0:T(8,128)} %bitcast.18), calls=%async_computation.1 | async-start | bytes 1048576 | tf_op jit(solution)/shard_map/all_to_all | solution.py:44
  76.3 6.9 %copy-start.7 = (f32[1,384,32]{1,2,0:T(8,128)S(1)}, f32[1,384,32]{1,2,0:T(8,128)}, u32[]{:S(2)}) copy-start(f32[1,384,32]{1,2,0:T(8,128)} %param.22) | copy-start | bytes 147460
  77.5 15.5 %all-to-all-start.2 = ((f32[16,16,128]{2,1,0:T(8,128)}), f32[16,16,128]{2,1,0:T(8,128)S(1)}, u32[]{:S(2)}, u32[]{:S(2)}) async-start(f32[16,16,128]{2,1,0:T(8,128)} %bitcast_bitcast_fusion.1), calls=%async_computation.2 | async-start | bytes 262144 | tf_op jit(solution)/shard_map/all_to_all | solution.py:284
  84.0 16.0 %collective-permute-start.8 = (f32[256,256]{1,0:T(8,128)S(1)}, f32[256,256]{1,0:T(8,128)S(1)}, u32[]{:S(2)}, u32[]{:S(2)}) collective-permute-start(f32[256,256]{1,0:T(8,128)S(1)} %get-tuple-element.1046), channel_id=1, source_target_pairs={{0,1},{1,0},{2,3},{3,2},{4,5},{5,4},{6,7},{7,6},{8,9},{9,8},{10,11... | collective-permute-start | bytes 786440 | tf_op jit(solution)/shard_map/ppermute | solution.py:264
  93.8 17.5 %all-to-all-start.3 = ((f32[32,16,128]{2,1,0:T(8,128)}), f32[32,16,128]{2,1,0:T(8,128)S(1)}, u32[]{:S(2)}, u32[]{:S(2)}) async-start(f32[32,16,128]{2,1,0:T(8,128)} %bitcast.24), calls=%async_computation.3 | async-start | bytes 524288 | tf_op jit(solution)/shard_map/all_to_all | solution.py:289
  113.5 16.7 %all-to-all-start.4 = ((f32[32,16,128]{2,1,0:T(8,128)}), f32[32,16,128]{2,1,0:T(8,128)S(1)}, u32[]{:S(2)}, u32[]{:S(2)}) async-start(f32[32,16,128]{2,1,0:T(8,128)} %bitcast.39), calls=%async_computation.4 | async-start | bytes 524288 | tf_op jit(solution)/shard_map/all_to_all | solution.py:44
  119.5 11.3 %copy-start.1 = (f32[768,384]{1,0:T(8,128)S(1)}, f32[768,384]{1,0:T(8,128)}, u32[]{:S(2)}) copy-start(f32[768,384]{1,0:T(8,128)} %param.21) | copy-start | bytes 3538948
  119.5 11.3 %copy-start.6 = (bf16[384,32]{1,0:T(8,128)(2,1)S(1)}, bf16[384,32]{1,0:T(8,128)(2,1)}, u32[]{:S(2)}) copy-start(bf16[384,32]{1,0:T(8,128)(2,1)} %convert_convert_fusion.6) | copy-start | bytes 73732

commit v5 on v4

--- a/solution.py
+++ b/solution.py
@@ -237,14 +237,18 @@
     packed = selected(thirds(factor, 1), narrow_pick, BY_FIRST)
 
     core = lax.axis_index(ROW[2])
-    packed = lax.ppermute(packed, (ROW[2], COL[1]), [(0, 0), (1, 2), (2, 1), (3, 3)])
     swap = [(0, 1), (1, 0)]
     copies = jnp.broadcast_to(packed, (lax.axis_size(ROW[:2]), *packed.shape))
-    this_block = lax.all_to_all(copies, ROW[:2], 0, 0, tiled=True)
-    this_block = this_block.reshape(width // 2, row_slots)
-    that_block = lax.ppermute(this_block, ROW[2], swap)
-    own_lower = jnp.where(core == side, this_block, that_block)
-    pair_lower = jnp.where(core == side, that_block, this_block)
+    this_half = lax.all_to_all(copies, ROW[:2], 0, 0, tiled=True)
+    this_half = this_half.reshape(width // 2, row_slots)
+    pair_axes = (ROW[2], COL[1])
+    near = lax.ppermute(this_half, pair_axes, [(1, 0), (2, 3)])
+    across = lax.ppermute(this_half, pair_axes, [(1, 2), (2, 1)])
+    that_half = lax.ppermute(this_half, ROW[2], swap)
+    same = core == side
+    own_lower = jnp.where(same, this_half, that_half)
+    lower = jnp.concatenate([own_lower, jnp.where(same, that_half, this_half)])
+    pair_lower = jnp.where(same, near, across)
 
     narrow = dot(matrix, pick_cols).reshape(ratio, col_block, row_slots)
     dense = jnp.stack([dot(pick_rows[part], narrow[part], BY_FIRST) for part in range(ratio)])
@@ -260,9 +264,6 @@
         BY_LAST,
     )
     summed = sum_at_owner(partial_value.reshape(owners, ratio * share, width // 2), COL[0])
-
-    rest_lower = lax.ppermute(pair_lower, COL[1], swap)
-    lower = jnp.concatenate([own_lower, rest_lower])
 
     wide = ratio * row_k
     half_slots = col_slots // 2

time: 134 us -> 133 us (level)
  waiting for transfers between devices: 52.3 us -> 43.2 us
  starting transfers between devices: 45.5 us -> 53.1 us
  other arithmetic: 7.29 us -> 9.6 us
    all_to_all x1, waiting for transfers between devices: 11.6 us -> 0.01 us  [panel_step(): this_half = lax.all_to_all(copies, ROW[:2], 0, 0, tiled=True)]
    all_to_all x1, starting transfers between devices: 3.51 us -> 10.2 us  [panel_step(): received = lax.all_to_all(jnp.moveaxis(chosen, 1, 0), ROW, 0, 0, tiled=True)]
    all_to_all x1, waiting for transfers between devices: 5.67 us -> 8.41 us  [panel_step(): received = lax.all_to_all(jnp.moveaxis(chosen, 1, 0), ROW, 0, 0, tiled=True)]
    ppermute x3, starting transfers between devices: 5.4 us -> 7.87 us  [the longest x1 5.22 us: panel_step(): that_half = lax.ppermute(this_half, ROW[2], swap)]
    select_n x1 -> x2, other arithmetic: 0.04 us -> 1.73 us  [the longest x1 1.69 us: panel_step(): lower = jnp.concatenate([own_lower, jnp.where(same, that_half, this_half)])]
  transfers between devices with their start and end apart: 9 -> 9, of which waited for: 6 -> 5; matrix products, arithmetic and copies ran while one was open for 14% -> 14% of each run, Pallas kernels for 2% -> 2%
where the time goes in v5:
time: 133 us; the launch traced here: 132 us
  starting transfers between devices  53.1 us (40%)
  waiting for transfers between devices  43.2 us (32%)
  matrix products  14.6 us (11%)
  other arithmetic  9.6 us (7%)
  local copies, waits for them, and re-layouts  5.81 us (4%)
  Pallas kernels  4.4 us (3%)
  between operations  1.75 us (1%)
    all_to_all x2, waiting for transfers between devices, sum_at_owner(): return jnp.sum(lax.all_to_all(blocks, axis, 0, 0, tiled=True), axis=0)  25.2 us
    all_to_all x2, starting transfers between devices, sum_at_owner(): return jnp.sum(lax.all_to_all(blocks, axis, 0, 0, tiled=True), axis=0)  16.5 us
    dot_general x15, matrix products, dot(): lax.dot_general(a, b, (dims, ((), ())), precision=HIGHEST, preferred_elem...  11.6 us
    all_to_all x1, starting transfers between devices, panel_step(): received = lax.all_to_all(jnp.moveaxis(chosen, 1, 0), ROW, 0, 0, tiled=True)  10.2 us
    all_to_all x1, starting transfers between devices, panel_step(): this_half = lax.all_to_all(copies, ROW[:2], 0, 0, tiled=True)  8.66 us
    all_to_all x1, waiting for transfers between devices, panel_step(): lax.all_to_all(sent.reshape(col_count, share, wide), COL, 0, 0, tiled=True)  8.46 us
    all_to_all x1, waiting for transfers between devices, panel_step(): received = lax.all_to_all(jnp.moveaxis(chosen, 1, 0), ROW, 0, 0, tiled=True)  8.41 us
    all_to_all x1, starting transfers between devices, panel_step(): lax.all_to_all(sent.reshape(col_count, share, wide), COL, 0, 0, tiled=True)  5.54 us
  transfers between devices with their start and end apart: 9, of which 5 were waited for; matrix products, arithmetic and copies ran while one was open for 14% of the time, Pallas kernels for 2%

profile of v5, /device:TPU:8, one launch (start us, length us, event | category | flops | bytes accessed | tf_op | source)
XLA Modules:
  0.0 132.5 jit_solution(7224342187636289500)
XLA Ops:
  0.0 0.9 reduce-precision_convert_fusion.3
  0.9 0.6 pad_add_fusion.1.device_ref
  1.5 2.2 %block_slots.1 = (s32[16,128]{1,0:T(8,128)}, s32[16,128]{1,0:T(8,128)}) custom-call(s32[2]{0:T(128)} %pad_add_fusion.1.device_ref, s32[1,6144]{1,0:T(1,128)} %rows_ref.3, s32[1,512]{1,0:T(1,128)} %cols_ref.1), custom_call_target="tpu_custom_call" | custom-call | tf_op jit(solution)/shard_map/block_slots/pallas_call | solution.py:158
  3.8 0.8 slice_bitcast_fusion.4
  4.8 0.7 broadcast_in_dim.42
  5.5 8.7 %all-to-all-start = ((f32[8,32,256]{2,1,0:T(8,128)}), f32[8,32,256]{2,1,0:T(8,128)S(1)}, u32[]{:S(2)}, u32[]{:S(2)}) async-start(f32[8,32,256]{2,1,0:T(8,128)} %broadcast_in_dim.42), calls=%async_computation | async-start | bytes 524288 | tf_op jit(solution)/shard_map/all_to_all | solution.py:242
  14.5 0.9 convolution_bitcast_fusion.1
  15.4 0.5 fusion.45
  15.9 0.5 fusion.47
  16.4 4.3 %collective-permute-start.5 = (f32[512,256]{1,0:T(8,128)S(1)}, f32[512,256]{1,0:T(8,128)S(1)}, u32[]{:S(2)}, u32[]{:S(2)}) collective-permute-start(f32[512,256]{1,0:T(8,128)S(1)} %bitcast.138), channel_id=1, source_target_pairs={{0,1},{1,0},{2,3},{3,2},{4,5},{5,4},{6,7},{7,6},{8,9},{9,8},{10,11... | collective-permute-start | bytes 1572872 | tf_op jit(solution)/shard_map/ppermute | solution.py:259
  20.7 0.5 broadcast.137
  21.2 0.7 reduce.5
  22.2 0.6 pad_add_fusion.panel_ref
  22.8 0.9 copy.48.other_ref
  23.6 2.2 %panel_places.1 = s32[8,512]{1,0:T(8,128)} custom-call(s32[2,512]{1,0:T(2,128)} %pad_add_fusion.panel_ref, s32[512,1]{1,0:T(8,128)} %copy.48.other_ref, s32[1,6144]{1,0:T(1,128)} %rows_ref.3), custom_call_target="tpu_custom_call" | custom-call | tf_op jit(solution)/shard_map/panel_places/pallas_call | solution.py:205
  25.8 2.1 %fusion.121 = (s32[1,512]{1,0:T(1,128)S(1)}, s32[1,512]{1,0:T(1,128)}, s32[]{:T(128)}, s32[]{:T(128)}, s32[1,512]{1,0:T(1,128)S(1)}) fusion(s32[8,512]{1,0:T(8,128)} %panel_places.1, s32[]{:T(128)S(6)} %mul.90), kind=kLoop, calls=%fused_computation.219 | loop fusion | flops 1534 | bytes 14348 | tf_op jit(solution)/shard_map/slice | solution.py:274
  27.9 0.3 fusion.58
  28.2 0.8 convert_convert_fusion.6
  29.0 1.3 collective-permute-start.7
  30.3 1.4 %collective-permute-start.8 = (f32[256,256]{1,0:T(8,128)S(1)}, f32[256,256]{1,0:T(8,128)}, u32[]{:S(2)}, u32[]{:S(2)}) collective-permute-start(f32[256,256]{1,0:T(8,128)S(1)} %bitcast.149), channel_id=1, source_target_pairs={{1,32},{32,1},{3,34},{34,3},{5,36},{36,5},{7,38},{38,7},{9,40},{40... | collective-permute-start | bytes 786440 | tf_op jit(solution)/shard_map/ppermute | solution.py:246
  31.7 0.8 slice_bitcast_fusion.2
  32.4 5.2 %collective-permute-start.6 = (f32[256,256]{1,0:T(8,128)S(1)}, f32[256,256]{1,0:T(8,128)}, u32[]{:S(2)}, u32[]{:S(2)}) collective-permute-start(f32[256,256]{1,0:T(8,128)S(1)} %bitcast.150), channel_id=1, source_target_pairs={{0,32},{32,0},{1,33},{33,1},{2,34},{34,2},{3,35},{35,3},{4,36},{36... | collective-permute-start | bytes 786440 | tf_op jit(solution)/shard_map/ppermute | solution.py:247
  37.7 1.2 collective-permute-done.6
  38.9 1.7 %broadcast_select_fusion.2 = (f32[256,256]{1,0:T(8,128)}, f32[256,256]{1,0:T(8,128)S(1)}) fusion(f32[256,256]{1,0:T(8,128)} %collective-permute-done.6, pred[]{:T(512)S(6)} %eq.319, f32[8,32,256]{2,1,0:T(8,128)S(1)} %all-to-all-done), kind=kLoop, calls=%fused_computation.139 | loop fusion | flops 131072 | bytes 1048577 | tf_op jit(solution)/shard_map/jit(_where)/select_n | solution.py:250
  40.6 1.8 %convolution_negate_fusion.1 = f32[512,256]{1,0:T(8,128)} fusion(f32[512,256]{1,0:T(8,128)S(1)} %collective-permute-done.5, f32[512,256]{1,0:T(8,128)S(1)} %bitcast.139, f32[256,256]{1,0:T(8,128)S(1)} %broadcast_select_fusion.3, f32[256,256]{1,0:T(8,128)S(1)} %get-tuple-element.1046), kind=kOutput, calls=%fused_computation.57 | convolution fusion | flops 805830656 | bytes 2097152 | tf_op jit(solution)/shard_map/dot_general | solution.py:22
  42.4 11.1 %all-to-all-start.1 = ((f32[16,32,256]{2,1,0:T(8,128)}), f32[16,32,256]{2,1,0:T(8,128)S(1)}, u32[]{:S(2)}, u32[]{:S(2)}) async-start(f32[16,32,256]{2,1,0:T(8,128)} %bitcast.18), calls=%async_computation.1 | async-start | bytes 1048576 | tf_op jit(solution)/shard_map/all_to_all | solution.py:44
  53.6 0.7 fusion.94
  54.6 15.3 %all-to-all-done.1 = f32[16,32,256]{2,1,0:T(8,128)S(1)} async-done(((f32[16,32,256]{2,1,0:T(8,128)}), f32[16,32,256]{2,1,0:T(8,128)S(1)}, u32[]{:S(2)}, u32[]{:S(2)}) %all-to-all-start.1) | async-done | bytes 524320 | tf_op jit(solution)/shard_map/all_to_all | solution.py:44
  69.9 0.5 fusion.27
  70.5 0.7 bitcast_bitcast_fusion.1
  71.2 10.2 %all-to-all-start.2 = ((f32[16,16,128]{2,1,0:T(8,128)}), f32[16,16,128]{2,1,0:T(8,128)S(1)}, u32[]{:S(2)}, u32[]{:S(2)}) async-start(f32[16,16,128]{2,1,0:T(8,128)} %bitcast_bitcast_fusion.1), calls=%async_computation.2 | async-start | bytes 262144 | tf_op jit(solution)/shard_map/all_to_all | solution.py:285
  81.4 0.8 copy.54
  83.5 0.8 copy.56
  84.3 0.5 fusion.28
  84.9 8.4 %all-to-all-done.2 = f32[16,16,128]{2,1,0:T(8,128)S(1)} async-done(((f32[16,16,128]{2,1,0:T(8,128)}), f32[16,16,128]{2,1,0:T(8,128)S(1)}, u32[]{:S(2)}, u32[]{:S(2)}) %all-to-all-start.2) | async-done | bytes 131104 | tf_op jit(solution)/shard_map/all_to_all | solution.py:285
  93.3 0.7 pad_maximum_fusion.1
  94.0 5.5 %all-to-all-start.3 = ((f32[32,16,128]{2,1,0:T(8,128)}), f32[32,16,128]{2,1,0:T(8,128)S(1)}, u32[]{:S(2)}, u32[]{:S(2)}) async-start(f32[32,16,128]{2,1,0:T(8,128)} %bitcast.24), calls=%async_computation.3 | async-start | bytes 524288 | tf_op jit(solution)/shard_map/all_to_all | solution.py:290
  99.6 2.9 %fusion.31 = f32[1024,256]{1,0:T(8,128)S(1)} fusion(s32[512]{0:T(512)S(1)} %bitcast.162, f32[256,256]{1,0:T(8,128)} %get-tuple-element.1045, f32[256,256]{1,0:T(8,128)S(1)} %get-tuple-element.1046), kind=kOutput, calls=%fused_computation.54 | convolution fusion | flops 1611268096 | bytes 1574912 | tf_op jit(solution)/shard_map/dot_general | solution.py:22
  102.6 8.5 %all-to-all-done.3 = f32[32,16,128]{2,1,0:T(8,128)S(1)} async-done(((f32[32,16,128]{2,1,0:T(8,128)}), f32[32,16,128]{2,1,0:T(8,128)S(1)}, u32[]{:S(2)}, u32[]{:S(2)}) %all-to-all-start.3) | async-done | bytes 262176 | tf_op jit(solution)/shard_map/all_to_all | solution.py:290
  111.1 0.4 fusion.51
  111.5 1.7 %convolution_subtract_fusion = f32[512,128]{1,0:T(8,128)} fusion(f32[512,256]{1,0:T(8,128)S(1)} %bitcast.141, f32[512,256]{1,0:T(8,128)S(1)} %bitcast.140, f32[64,256]{0,1:T(8,128)S(1)} %get-tuple-element.1050, f32[512,64]{1,0:T(8,128)S(1)} %bitcast.145, f32[512,64]{1,0:T(8,128)S(1)} %bitcast.144), kind=kOutput, calls=%fused_computation.60 | convolution fusion | flops 403374080 | bytes 1638400 | tf_op jit(solution)/shard_map/dot_general | solution.py:22
  113.2 5.4 %all-to-all-start.4 = ((f32[32,16,128]{2,1,0:T(8,128)}), f32[32,16,128]{2,1,0:T(8,128)S(1)}, u32[]{:S(2)}, u32[]{:S(2)}) async-start(f32[32,16,128]{2,1,0:T(8,128)} %bitcast.39), calls=%async_computation.4 | async-start | bytes 524288 | tf_op jit(solution)/shard_map/all_to_all | solution.py:44
  118.7 0.3 fusion.53
  119.0 0.4 fusion.49
  119.4 0.4 fusion.64
  119.8 0.4 fusion.61
  120.2 9.9 %all-to-all-done.4 = f32[32,16,128]{2,1,0:T(8,128)S(1)} async-done(((f32[32,16,128]{2,1,0:T(8,128)}), f32[32,16,128]{2,1,0:T(8,128)S(1)}, u32[]{:S(2)}, u32[]{:S(2)}) %all-to-all-start.4) | async-done | bytes 262176 | tf_op jit(solution)/shard_map/all_to_all | solution.py:44
  130.8 1.7 %convolution_select_fusion.3 = f32[768,384]{1,0:T(8,128)} fusion(f32[768,384]{1,0:T(8,128)S(1)} %copy-done.1, f32[384,384]{1,0:T(8,128)S(1)} %fusion.61, f32[384,384]{1,0:T(8,128)S(1)} %fusion.64, pred[384]{0:T(512)(128)(4,1)S(1)} %slice.247, pred[384]{0:T(512)(128)(4,1)S(1)} %slice.212, pred[768]{0:T(1024)(128)(4,1)S(1)} %get-tuple-element.1073, ...), kind=kOutput, calls=%fused_computation.55 | convolution fusion | flops 58761216 | bytes 3713280 | tf_op jit(solution)/shard_map/dot_general | solution.py:339
  (58 shorter events, 2.1 us)
Async XLA Ops:
  0.0 14.5 %copy-start.1 = (f32[768,384]{1,0:T(8,128)S(1)}, f32[768,384]{1,0:T(8,128)}, u32[]{:S(2)}) copy-start(f32[768,384]{1,0:T(8,128)} %param.21) | copy-start | bytes 3538948
  3.8 10.4 %copy-start.11 = (s32[16,128]{1,0:T(8,128)S(1)}, s32[16,128]{1,0:T(8,128)}, u32[]{:S(2)}) copy-start(s32[16,128]{1,0:T(8,128)} %get-tuple-element.854) | copy-start | bytes 24580
  5.5 23.5 %all-to-all-start = ((f32[8,32,256]{2,1,0:T(8,128)}), f32[8,32,256]{2,1,0:T(8,128)S(1)}, u32[]{:S(2)}, u32[]{:S(2)}) async-start(f32[8,32,256]{2,1,0:T(8,128)} %broadcast_in_dim.42), calls=%async_computation | async-start | bytes 524288 | tf_op jit(solution)/shard_map/all_to_all | solution.py:242
  15.4 5.3 %copy-start.10 = (s32[16,128]{1,0:T(8,128)S(1)}, s32[16,128]{1,0:T(8,128)}, u32[]{:S(2)}) copy-start(s32[16,128]{1,0:T(8,128)} %get-tuple-element.853) | copy-start | bytes 24580
  15.4 5.8 %copy-start.8 = (s32[1,512]{1,0:T(1,128)S(1)}, s32[1,512]{1,0:T(1,128)}, u32[]{:S(2)}) copy-start(s32[1,512]{1,0:T(1,128)} %cols_ref.1) | copy-start | bytes 6148
  15.9 12.0 %copy-start.12 = (f32[1,16,512]{2,1,0:T(8,128)S(1)}, f32[1,16,512]{2,1,0:T(8,128)}, u32[]{:S(2)}) copy-start(f32[1,16,512]{2,1,0:T(8,128)} %param.23) | copy-start | bytes 98308
  16.4 24.2 %collective-permute-start.5 = (f32[512,256]{1,0:T(8,128)S(1)}, f32[512,256]{1,0:T(8,128)S(1)}, u32[]{:S(2)}, u32[]{:S(2)}) collective-permute-start(f32[512,256]{1,0:T(8,128)S(1)} %bitcast.138), channel_id=1, source_target_pairs={{0,1},{1,0},{2,3},{3,2},{4,5},{5,4},{6,7},{7,6},{8,9},{9,8},{10,11... | collective-permute-start | bytes 1572872 | tf_op jit(solution)/shard_map/ppermute | solution.py:259
  29.0 8.7 %collective-permute-start.7 = (f32[256,256]{1,0:T(8,128)S(1)}, f32[256,256]{1,0:T(8,128)S(1)}, u32[]{:S(2)}, u32[]{:S(2)}) collective-permute-start(f32[256,256]{1,0:T(8,128)S(1)} %bitcast.148), channel_id=1, source_target_pairs={{1,0},{32,33},{3,2},{34,35},{5,4},{36,37},{7,6},{38,39},{9,8},{40,... | collective-permute-start | bytes 786440 | tf_op jit(solution)/shard_map/ppermute | solution.py:245
  30.3 7.4 %collective-permute-start.8 = (f32[256,256]{1,0:T(8,128)S(1)}, f32[256,256]{1,0:T(8,128)}, u32[]{:S(2)}, u32[]{:S(2)}) collective-permute-start(f32[256,256]{1,0:T(8,128)S(1)} %bitcast.149), channel_id=1, source_target_pairs={{1,32},{32,1},{3,34},{34,3},{5,36},{36,5},{7,38},{38,7},{9,40},{40... | collective-permute-start | bytes 786440 | tf_op jit(solution)/shard_map/ppermute | solution.py:246
  32.4 6.5 %collective-permute-start.6 = (f32[256,256]{1,0:T(8,128)S(1)}, f32[256,256]{1,0:T(8,128)}, u32[]{:S(2)}, u32[]{:S(2)}) collective-permute-start(f32[256,256]{1,0:T(8,128)S(1)} %bitcast.150), channel_id=1, source_target_pairs={{0,32},{32,0},{1,33},{33,1},{2,34},{34,2},{3,35},{35,3},{4,36},{36... | collective-permute-start | bytes 786440 | tf_op jit(solution)/shard_map/ppermute | solution.py:247
  42.4 27.4 %all-to-all-start.1 = ((f32[16,32,256]{2,1,0:T(8,128)}), f32[16,32,256]{2,1,0:T(8,128)S(1)}, u32[]{:S(2)}, u32[]{:S(2)}) async-start(f32[16,32,256]{2,1,0:T(8,128)} %bitcast.18), calls=%async_computation.1 | async-start | bytes 1048576 | tf_op jit(solution)/shard_map/all_to_all | solution.py:44
  69.9 11.5 %copy-start.13 = (f32[1,16,512]{2,1,0:T(8,128)S(1)}, f32[1,16,512]{2,1,0:T(8,128)}, u32[]{:S(2)}) copy-start(f32[1,16,512]{2,1,0:T(8,128)} %param.23) | copy-start | bytes 98308
  69.9 13.6 %copy-start.7 = (f32[1,384,32]{1,2,0:T(8,128)S(1)}, f32[1,384,32]{1,2,0:T(8,128)}, u32[]{:S(2)}) copy-start(f32[1,384,32]{1,2,0:T(8,128)} %param.22) | copy-start | bytes 147460
  71.2 22.1 %all-to-all-start.2 = ((f32[16,16,128]{2,1,0:T(8,128)}), f32[16,16,128]{2,1,0:T(8,128)S(1)}, u32[]{:S(2)}, u32[]{:S(2)}) async-start(f32[16,16,128]{2,1,0:T(8,128)} %bitcast_bitcast_fusion.1), calls=%async_computation.2 | async-start | bytes 262144 | tf_op jit(solution)/shard_map/all_to_all | solution.py:285
  84.9 14.7 %copy-start.14 = (s32[1,512]{1,0:T(1,128)S(1)}, s32[1,512]{1,0:T(1,128)}, u32[]{:S(2)}) copy-start(s32[1,512]{1,0:T(1,128)} %get-tuple-element.1063) | copy-start | bytes 6148
  94.0 17.0 %all-to-all-start.3 = ((f32[32,16,128]{2,1,0:T(8,128)}), f32[32,16,128]{2,1,0:T(8,128)S(1)}, u32[]{:S(2)}, u32[]{:S(2)}) async-start(f32[32,16,128]{2,1,0:T(8,128)} %bitcast.24), calls=%async_computation.3 | async-start | bytes 524288 | tf_op jit(solution)/shard_map/all_to_all | solution.py:290
  113.2 16.9 %all-to-all-start.4 = ((f32[32,16,128]{2,1,0:T(8,128)}), f32[32,16,128]{2,1,0:T(8,128)S(1)}, u32[]{:S(2)}, u32[]{:S(2)}) async-start(f32[32,16,128]{2,1,0:T(8,128)} %bitcast.39), calls=%async_computation.4 | async-start | bytes 524288 | tf_op jit(solution)/shard_map/all_to_all | solution.py:44
  119.4 11.4 %copy-start.6 = (bf16[384,32]{1,0:T(8,128)(2,1)S(1)}, bf16[384,32]{1,0:T(8,128)(2,1)}, u32[]{:S(2)}) copy-start(bf16[384,32]{1,0:T(8,128)(2,1)} %convert_convert_fusion.6) | copy-start | bytes 73732

commit v6 on v5

--- a/solution.py
+++ b/solution.py
@@ -111,10 +111,12 @@
     return lax.fori_loop(0, row_count, corners, out)
 
 
-def slots_kernel(lines, lanes, device_ref, rows_ref, cols_ref, row_slots_ref, col_slots_ref):
+def slots_kernel(lines, lanes, ratio, rows_ref, cols_ref, row_slots_ref, col_slots_ref):
     line = lax.broadcasted_iota(jnp.int32, (LINES, 1), 0)
     own = jnp.where(
-        line < lines, device_ref[0] * lines + line, device_ref[1] * lines + line - lines
+        line < lines,
+        lax.axis_index(COL) * lines + line,
+        (lax.axis_index(ROW) * ratio - 1) * lines + line,
     )
     lower = lax.broadcasted_iota(jnp.int32, (lanes, lanes), 0)
     upper = lax.broadcasted_iota(jnp.int32, (lanes, lanes), 1)
@@ -152,16 +154,15 @@
 def block_slots(col_block, ratio, panel_cols, row_lists):
     lanes = LANES if col_block % LANES == 0 else col_block
     lines = col_block // lanes
-    device = jnp.stack([lax.axis_index(COL), lax.axis_index(ROW) * ratio]).astype(jnp.int32)
     shape = jax.ShapeDtypeStruct((LINES, lanes), jnp.int32)
     whole = pl.BlockSpec(memory_space=pltpu.VMEM)
     found = pl.pallas_call(
-        functools.partial(slots_kernel, lines, lanes),
+        functools.partial(slots_kernel, lines, lanes, ratio),
         out_shape=(shape, shape),
-        in_specs=[pl.BlockSpec(memory_space=pltpu.SMEM), whole, whole],
+        in_specs=[whole, whole],
         out_specs=(whole, whole),
         name="block_slots",
-    )(device, row_lists[None], panel_cols[None])
+    )(row_lists[None], panel_cols[None])
     used = (1 + ratio) * lines
     return [slots[:used].reshape(used * lanes) for slots in found]
 
@@ -171,14 +172,16 @@
     return hot.astype(jnp.float32).astype(dtype)
 
 
-def places_kernel(sizes, panel_ref, other_ref, rows_ref, out_ref):
+def places_kernel(sizes, own_ref, local_ref, rows_ref, out_ref):
     col_block, ratio, col_slots, col_count = sizes
     row_k = ratio * col_slots
     wide = ratio * row_k
-    other = other_ref[...]
+    width = own_ref.shape[1]
+    other = jnp.broadcast_to(own_ref[...].astype(jnp.float32), (8, width)).T[:, :1]
+    other = other.astype(jnp.int32)
     other_home = lax.div(other, jnp.int32(col_block))
-    for order in range(2):
-        panel = panel_ref[order : order + 1, :]
+    for order, panel_ref in enumerate((own_ref, local_ref)):
+        panel = panel_ref[...]
         home = lax.div(panel, jnp.int32(col_block))
         earlier = (other < panel) & (other_home == home)
         rank = jnp.sum(earlier.astype(jnp.float32), axis=0, keepdims=True).astype(jnp.int32)
@@ -195,7 +198,7 @@
     block = lax.broadcasted_iota(jnp.int32, (col_count, rows_ref.shape[1]), 0)
     counts = jnp.sum((block == rows_home).astype(jnp.float32), axis=1, keepdims=True)
     most = jnp.max(counts, axis=0, keepdims=True).astype(jnp.int32)
-    out_ref[7:8, :] = jnp.broadcast_to(most, (1, panel_ref.shape[1]))
+    out_ref[7:8, :] = jnp.broadcast_to(most, (1, width))
 
 
 def panel_places(col_slots, col_block, ratio, col_count, group, panel_cols, row_lists):
@@ -206,7 +209,7 @@
         functools.partial(places_kernel, (col_block, ratio, col_slots, col_count)),
         out_shape=jax.ShapeDtypeStruct((8, width), jnp.int32),
         name="panel_places",
-    )(jnp.stack([panel_cols, local]), panel_cols[:, None], row_lists[None])
+    )(panel_cols[None], local[None], row_lists[None])
 
 
 def panel_step(matrix, factor, dinv, panel_cols, row_lists):
@@ -347,8 +350,12 @@
 
     fits = (jnp.max(found[6]) < col_slots) & (jnp.max(found[7]) <= row_slots)
 
+    zero = lax.shift_right_logical((received[0, 0, 0] > 0.0).astype(jnp.int32), 1)
+    late_factor = factor + zero.astype(jnp.float32)
+    late_dinv = dinv + zero.astype(jnp.float32)
+
     def again(carried):
-        general = general_panel(matrix, factor, dinv, panel_cols, row_in, col_in)
+        general = general_panel(matrix, late_factor, late_dinv, panel_cols, row_in, col_in)
         return jnp.zeros((), jnp.bool_), general
 
     return lax.while_loop(lambda carried: carried[0], again, (~fits, result))[1]

time: 133 us -> 134 us (level)
  waiting for transfers between devices: 43.2 us -> 34.3 us
  local copies, waits for them, and re-layouts: 5.81 us -> 8.58 us
  matrix products: 14.6 us -> 17.1 us
  other arithmetic: 9.6 us -> 11.3 us
  starting transfers between devices: 53.1 us -> 54.5 us
    all_to_all x2, waiting for transfers between devices: 25.2 us -> 21.2 us  [sum_at_owner(): return jnp.sum(lax.all_to_all(blocks, axis, 0, 0, tiled=True), axis=0)]
    all_to_all x1, waiting for transfers between devices: 8.46 us -> 5.34 us  [panel_step(): lax.all_to_all(sent.reshape(col_count, share, wide), COL, 0, 0, tiled=True)]
    dot_general x15, matrix products: 11.6 us -> 14 us  [dot(): lax.dot_general(a, b, (dims, ((), ())), precision=HIGHEST, preferred_elem...]
    all_to_all x1, starting transfers between devices: 5.54 us -> 6.91 us  [panel_step(): lax.all_to_all(sent.reshape(col_count, share, wide), COL, 0, 0, tiled=True)]
    add x0 -> x2, other arithmetic: none -> 1.35 us  [the longest x1 0.72 us: panel_step(): late_dinv = dinv + zero.astype(jnp.float32)]
  transfers between devices with their start and end apart: 9 -> 9, of which waited for: 5 -> 5; matrix products, arithmetic and copies ran while one was open for 14% -> 18% of each run, Pallas kernels for 2% -> 2%
where the time goes in v6:
time: 134 us; the launch traced here: 132 us
  starting transfers between devices  54.5 us (41%)
  waiting for transfers between devices  34.3 us (26%)
  matrix products  17.1 us (13%)
  other arithmetic  11.3 us (8%)
  local copies, waits for them, and re-layouts  8.58 us (6%)
  Pallas kernels  4.34 us (3%)
  between operations  2.37 us (2%)
    all_to_all x2, waiting for transfers between devices, sum_at_owner(): return jnp.sum(lax.all_to_all(blocks, axis, 0, 0, tiled=True), axis=0)  21.2 us
    all_to_all x2, starting transfers between devices, sum_at_owner(): return jnp.sum(lax.all_to_all(blocks, axis, 0, 0, tiled=True), axis=0)  17.1 us
    dot_general x15, matrix products, dot(): lax.dot_general(a, b, (dims, ((), ())), precision=HIGHEST, preferred_elem...  14 us
    all_to_all x1, starting transfers between devices, panel_step(): received = lax.all_to_all(jnp.moveaxis(chosen, 1, 0), ROW, 0, 0, tiled=True)  9.59 us
    all_to_all x1, starting transfers between devices, panel_step(): this_half = lax.all_to_all(copies, ROW[:2], 0, 0, tiled=True)  8.66 us
    all_to_all x1, waiting for transfers between devices, panel_step(): received = lax.all_to_all(jnp.moveaxis(chosen, 1, 0), ROW, 0, 0, tiled=True)  7.13 us
    all_to_all x1, starting transfers between devices, panel_step(): lax.all_to_all(sent.reshape(col_count, share, wide), COL, 0, 0, tiled=True)  6.91 us
    all_to_all x1, waiting for transfers between devices, panel_step(): lax.all_to_all(sent.reshape(col_count, share, wide), COL, 0, 0, tiled=True)  5.34 us
  transfers between devices with their start and end apart: 9, of which 5 were waited for; matrix products, arithmetic and copies ran while one was open for 18% of the time, Pallas kernels for 2%

profile of v6, /device:TPU:8, one launch (start us, length us, event | category | flops | bytes accessed | tf_op | source)
XLA Modules:
  0.0 132.5 jit_solution(5829045405967314219)
XLA Ops:
  0.0 0.9 reduce-precision_convert_fusion.3
  0.9 2.2 %block_slots.1 = (s32[16,128]{1,0:T(8,128)}, s32[16,128]{1,0:T(8,128)}) custom-call(s32[1,6144]{1,0:T(1,128)} %rows_ref.3, s32[1,512]{1,0:T(1,128)} %cols_ref.1), custom_call_target="tpu_custom_call" | custom-call | tf_op jit(solution)/shard_map/block_slots/pallas_call | solution.py:159
  3.2 0.8 slice_bitcast_fusion.4
  4.2 0.7 broadcast_in_dim.42
  4.9 8.7 %all-to-all-start = ((f32[8,32,256]{2,1,0:T(8,128)}), f32[8,32,256]{2,1,0:T(8,128)S(1)}, u32[]{:S(2)}, u32[]{:S(2)}) async-start(f32[8,32,256]{2,1,0:T(8,128)} %broadcast_in_dim.42), calls=%async_computation | async-start | bytes 524288 | tf_op jit(solution)/shard_map/all_to_all | solution.py:245
  13.8 0.9 convolution_bitcast_fusion.1
  15.8 4.3 %collective-permute-start.5 = (f32[512,256]{1,0:T(8,128)S(1)}, f32[512,256]{1,0:T(8,128)S(1)}, u32[]{:S(2)}, u32[]{:S(2)}) collective-permute-start(f32[512,256]{1,0:T(8,128)S(1)} %bitcast.140), channel_id=1, source_target_pairs={{0,1},{1,0},{2,3},{3,2},{4,5},{5,4},{6,7},{7,6},{8,9},{9,8},{10,11... | collective-permute-start | bytes 1572872 | tf_op jit(solution)/shard_map/ppermute | solution.py:262
  20.1 0.6 broadcast.137
  20.7 0.7 reduce.5
  21.6 0.6 copy.57
  22.2 2.1 %panel_places.1 = s32[8,512]{1,0:T(8,128)} custom-call(s32[1,512]{1,0:T(1,128)S(1)} %copy-done.11, s32[1,512]{1,0:T(1,128)} %bitcast.159, s32[1,6144]{1,0:T(1,128)} %rows_ref.3), custom_call_target="tpu_custom_call" | custom-call | tf_op jit(solution)/shard_map/panel_places/pallas_call | solution.py:208
  24.3 1.6 %fusion.121 = (s32[1,512]{1,0:T(1,128)S(1)}, s32[1,512]{1,0:T(1,128)S(1)}, s32[]{:T(128)}, s32[]{:T(128)}, s32[1,512]{1,0:T(1,128)S(1)}) fusion(s32[8,512]{1,0:T(8,128)} %panel_places.1, s32[]{:T(128)S(6)} %mul.83), kind=kLoop, calls=%fused_computation.219 | loop fusion | flops 1534 | bytes 14348 | tf_op jit(solution)/shard_map/slice | solution.py:277
  25.9 0.8 slice_bitcast_fusion.2
  26.9 0.8 convert_convert_fusion.6
  27.7 1.3 collective-permute-start.7
  29.0 1.4 %collective-permute-start.8 = (f32[256,256]{1,0:T(8,128)S(1)}, f32[256,256]{1,0:T(8,128)}, u32[]{:S(2)}, u32[]{:S(2)}) collective-permute-start(f32[256,256]{1,0:T(8,128)S(1)} %bitcast.151), channel_id=1, source_target_pairs={{1,32},{32,1},{3,34},{34,3},{5,36},{36,5},{7,38},{38,7},{9,40},{40... | collective-permute-start | bytes 786440 | tf_op jit(solution)/shard_map/ppermute | solution.py:249
  30.3 5.2 %collective-permute-start.6 = (f32[256,256]{1,0:T(8,128)S(1)}, f32[256,256]{1,0:T(8,128)}, u32[]{:S(2)}, u32[]{:S(2)}) collective-permute-start(f32[256,256]{1,0:T(8,128)S(1)} %bitcast.152), channel_id=1, source_target_pairs={{0,32},{32,0},{1,33},{33,1},{2,34},{34,2},{3,35},{35,3},{4,36},{36... | collective-permute-start | bytes 786440 | tf_op jit(solution)/shard_map/ppermute | solution.py:250
  35.6 0.6 broadcast_compare_fusion.6
  36.2 0.7 collective-permute-done.6
  36.9 1.7 %broadcast_select_fusion.2 = (f32[256,256]{1,0:T(8,128)}, f32[256,256]{1,0:T(8,128)S(1)}) fusion(f32[256,256]{1,0:T(8,128)} %collective-permute-done.6, pred[]{:T(512)S(6)} %eq.319, f32[8,32,256]{2,1,0:T(8,128)S(1)} %all-to-all-done), kind=kLoop, calls=%fused_computation.140 | loop fusion | flops 131072 | bytes 1048577 | tf_op jit(solution)/shard_map/jit(_where)/select_n | solution.py:253
  38.6 1.8 %convolution_negate_fusion.1 = f32[512,256]{1,0:T(8,128)} fusion(f32[512,256]{1,0:T(8,128)S(1)} %collective-permute-done.5, f32[512,256]{1,0:T(8,128)S(1)} %bitcast.141, f32[256,256]{1,0:T(8,128)S(1)} %broadcast_select_fusion.3, f32[256,256]{1,0:T(8,128)S(1)} %get-tuple-element.1046), kind=kOutput, calls=%fused_computation.57 | convolution fusion | flops 805830656 | bytes 2097152 | tf_op jit(solution)/shard_map/dot_general | solution.py:22
  40.4 11.8 %all-to-all-start.1 = ((f32[16,32,256]{2,1,0:T(8,128)}), f32[16,32,256]{2,1,0:T(8,128)S(1)}, u32[]{:S(2)}, u32[]{:S(2)}) async-start(f32[16,32,256]{2,1,0:T(8,128)} %bitcast.15), calls=%async_computation.1 | async-start | bytes 1048576 | tf_op jit(solution)/shard_map/all_to_all | solution.py:44
  52.2 0.5 slice.216
  54.1 0.7 fusion.94
  55.1 13.3 %all-to-all-done.1 = f32[16,32,256]{2,1,0:T(8,128)S(1)} async-done(((f32[16,32,256]{2,1,0:T(8,128)}), f32[16,32,256]{2,1,0:T(8,128)S(1)}, u32[]{:S(2)}, u32[]{:S(2)}) %all-to-all-start.1) | async-done | bytes 524320 | tf_op jit(solution)/shard_map/all_to_all | solution.py:44
  68.5 0.5 fusion.27
  69.0 0.7 bitcast_bitcast_fusion.1
  69.7 9.6 %all-to-all-start.2 = ((f32[16,16,128]{2,1,0:T(8,128)}), f32[16,16,128]{2,1,0:T(8,128)S(1)}, u32[]{:S(2)}, u32[]{:S(2)}) async-start(f32[16,16,128]{2,1,0:T(8,128)} %bitcast_bitcast_fusion.1), calls=%async_computation.2 | async-start | bytes 262144 | tf_op jit(solution)/shard_map/all_to_all | solution.py:288
  79.3 2.9 %fusion.31 = f32[1024,256]{1,0:T(8,128)} fusion(s32[512]{0:T(512)S(1)} %bitcast.162, f32[256,256]{1,0:T(8,128)S(1)} %copy-done.9, f32[256,256]{1,0:T(8,128)S(1)} %get-tuple-element.1046), kind=kOutput, calls=%fused_computation.54 | convolution fusion | flops 1611268096 | bytes 1574912 | tf_op jit(solution)/shard_map/dot_general | solution.py:22
  82.2 0.5 fusion.28
  82.8 7.1 %all-to-all-done.2 = f32[16,16,128]{2,1,0:T(8,128)S(1)} async-done(((f32[16,16,128]{2,1,0:T(8,128)}), f32[16,16,128]{2,1,0:T(8,128)S(1)}, u32[]{:S(2)}, u32[]{:S(2)}) %all-to-all-start.2) | async-done | bytes 131104 | tf_op jit(solution)/shard_map/all_to_all | solution.py:288
  89.9 0.7 pad_maximum_fusion.1
  90.7 6.9 %all-to-all-start.3 = ((f32[32,16,128]{2,1,0:T(8,128)}), f32[32,16,128]{2,1,0:T(8,128)}, u32[]{:S(2)}, u32[]{:S(2)}) async-start(f32[32,16,128]{2,1,0:T(8,128)} %bitcast.21), calls=%async_computation.3 | async-start | bytes 524288 | tf_op jit(solution)/shard_map/all_to_all | solution.py:293
  97.6 1.3 fusion.118
  98.9 1.2 slice.254
  100.7 0.6 bitcast_add_fusion.1
  101.4 1.6 %copy.53 = f32[384,32]{1,0:T(8,128)} copy(f32[384,32]{0,1:T(8,128)} %bitcast_add_fusion.1) | data formatting | bytes 98304 | tf_op jit(solution)/shard_map/while | solution.py:361
  103.0 0.7 bitcast_add_fusion
  103.7 5.3 %all-to-all-done.3 = f32[32,16,128]{2,1,0:T(8,128)} async-done(((f32[32,16,128]{2,1,0:T(8,128)}), f32[32,16,128]{2,1,0:T(8,128)}, u32[]{:S(2)}, u32[]{:S(2)}) %all-to-all-start.3) | async-done | bytes 262176 | tf_op jit(solution)/shard_map/all_to_all | solution.py:293
  109.0 1.0 bitcast_reduce_fusion
  110.0 0.8 slice_select_fusion.1
  110.8 1.0 fusion.51
  111.8 1.7 %convolution_subtract_fusion = f32[512,128]{1,0:T(8,128)} fusion(f32[512,256]{1,0:T(8,128)S(1)} %bitcast.143, f32[512,256]{1,0:T(8,128)S(1)} %bitcast.142, f32[64,256]{0,1:T(8,128)S(1)} %get-tuple-element.1050, f32[512,64]{1,0:T(8,128)S(1)} %bitcast.147, f32[512,64]{1,0:T(8,128)S(1)} %bitcast.146), kind=kOutput, calls=%fused_computation.60 | convolution fusion | flops 403374080 | bytes 1638400 | tf_op jit(solution)/shard_map/dot_general | solution.py:22
  113.5 5.4 %all-to-all-start.4 = ((f32[32,16,128]{2,1,0:T(8,128)}), f32[32,16,128]{2,1,0:T(8,128)S(1)}, u32[]{:S(2)}, u32[]{:S(2)}) async-start(f32[32,16,128]{2,1,0:T(8,128)} %bitcast.36), calls=%async_computation.4 | async-start | bytes 524288 | tf_op jit(solution)/shard_map/all_to_all | solution.py:44
  118.9 1.2 fusion.53
  120.1 1.3 %fusion.49 = f32[384,32]{0,1:T(8,128)S(1)} fusion(pred[1152,256]{1,0:T(32,128)(4,1)S(1)} %iota_compare_fusion.4, f32[64,256]{0,1:T(8,128)} %get-tuple-element.1049), kind=kOutput, calls=%fused_computation.84 | convolution fusion | flops 37748736 | bytes 212992 | tf_op jit(solution)/shard_map/dot_general | solution.py:22
  122.2 7.9 %all-to-all-done.4 = f32[32,16,128]{2,1,0:T(8,128)S(1)} async-done(((f32[32,16,128]{2,1,0:T(8,128)}), f32[32,16,128]{2,1,0:T(8,128)S(1)}, u32[]{:S(2)}, u32[]{:S(2)}) %all-to-all-start.4) | async-done | bytes 262176 | tf_op jit(solution)/shard_map/all_to_all | solution.py:44
  130.8 1.7 %convolution_select_fusion.3 = f32[768,384]{1,0:T(8,128)} fusion(f32[768,384]{1,0:T(8,128)S(1)} %copy-done.1, f32[384,384]{1,0:T(8,128)S(1)} %fusion.61, f32[384,384]{1,0:T(8,128)S(1)} %fusion.64, pred[384]{0:T(512)(128)(4,1)S(1)} %slice.251, pred[384]{0:T(512)(128)(4,1)S(1)} %copy-done.18, pred[768]{0:T(1024)(128)(4,1)S(1)} %get-tuple-element.1073, ...), kind=kOutput, calls=%fused_computation.55 | convolution fusion | flops 58761216 | bytes 3713280 | tf_op jit(solution)/shard_map/dot_general | solution.py:342
  (66 shorter events, 4.0 us)
Async XLA Ops:
  0.0 13.8 %copy-start.1 = (f32[768,384]{1,0:T(8,128)S(1)}, f32[768,384]{1,0:T(8,128)}, u32[]{:S(2)}) copy-start(f32[768,384]{1,0:T(8,128)} %param.21) | copy-start | bytes 3538948
  3.2 10.4 %copy-start.13 = (s32[16,128]{1,0:T(8,128)S(1)}, s32[16,128]{1,0:T(8,128)}, u32[]{:S(2)}) copy-start(s32[16,128]{1,0:T(8,128)} %get-tuple-element.854) | copy-start | bytes 24580
  4.9 22.8 %all-to-all-start = ((f32[8,32,256]{2,1,0:T(8,128)}), f32[8,32,256]{2,1,0:T(8,128)S(1)}, u32[]{:S(2)}, u32[]{:S(2)}) async-start(f32[8,32,256]{2,1,0:T(8,128)} %broadcast_in_dim.42), calls=%async_computation | async-start | bytes 524288 | tf_op jit(solution)/shard_map/all_to_all | solution.py:245
  14.8 5.3 %copy-start.14 = (s32[16,128]{1,0:T(8,128)S(1)}, s32[16,128]{1,0:T(8,128)}, u32[]{:S(2)}) copy-start(s32[16,128]{1,0:T(8,128)} %get-tuple-element.853) | copy-start | bytes 24580
  14.8 5.9 %copy-start.11 = (s32[1,512]{1,0:T(1,128)S(1)}, s32[1,512]{1,0:T(1,128)}, u32[]{:S(2)}) copy-start(s32[1,512]{1,0:T(1,128)} %cols_ref.1) | copy-start | bytes 6148
  15.3 11.4 %copy-start.15 = (f32[1,16,512]{2,1,0:T(8,128)S(1)}, f32[1,16,512]{2,1,0:T(8,128)}, u32[]{:S(2)}) copy-start(f32[1,16,512]{2,1,0:T(8,128)} %param.23) | copy-start | bytes 98308
  15.8 22.8 %collective-permute-start.5 = (f32[512,256]{1,0:T(8,128)S(1)}, f32[512,256]{1,0:T(8,128)S(1)}, u32[]{:S(2)}, u32[]{:S(2)}) collective-permute-start(f32[512,256]{1,0:T(8,128)S(1)} %bitcast.140), channel_id=1, source_target_pairs={{0,1},{1,0},{2,3},{3,2},{4,5},{5,4},{6,7},{7,6},{8,9},{9,8},{10,11... | collective-permute-start | bytes 1572872 | tf_op jit(solution)/shard_map/ppermute | solution.py:262
  27.7 8.5 %collective-permute-start.7 = (f32[256,256]{1,0:T(8,128)S(1)}, f32[256,256]{1,0:T(8,128)S(1)}, u32[]{:S(2)}, u32[]{:S(2)}) collective-permute-start(f32[256,256]{1,0:T(8,128)S(1)} %bitcast.150), channel_id=1, source_target_pairs={{1,0},{32,33},{3,2},{34,35},{5,4},{36,37},{7,6},{38,39},{9,8},{40,... | collective-permute-start | bytes 786440 | tf_op jit(solution)/shard_map/ppermute | solution.py:248
  29.0 7.2 %collective-permute-start.8 = (f32[256,256]{1,0:T(8,128)S(1)}, f32[256,256]{1,0:T(8,128)}, u32[]{:S(2)}, u32[]{:S(2)}) collective-permute-start(f32[256,256]{1,0:T(8,128)S(1)} %bitcast.151), channel_id=1, source_target_pairs={{1,32},{32,1},{3,34},{34,3},{5,36},{36,5},{7,38},{38,7},{9,40},{40... | collective-permute-start | bytes 786440 | tf_op jit(solution)/shard_map/ppermute | solution.py:249
  30.3 6.5 %collective-permute-start.6 = (f32[256,256]{1,0:T(8,128)S(1)}, f32[256,256]{1,0:T(8,128)}, u32[]{:S(2)}, u32[]{:S(2)}) collective-permute-start(f32[256,256]{1,0:T(8,128)S(1)} %bitcast.152), channel_id=1, source_target_pairs={{0,32},{32,0},{1,33},{33,1},{2,34},{34,2},{3,35},{35,3},{4,36},{36... | collective-permute-start | bytes 786440 | tf_op jit(solution)/shard_map/ppermute | solution.py:250
  40.4 28.0 %all-to-all-start.1 = ((f32[16,32,256]{2,1,0:T(8,128)}), f32[16,32,256]{2,1,0:T(8,128)S(1)}, u32[]{:S(2)}, u32[]{:S(2)}) async-start(f32[16,32,256]{2,1,0:T(8,128)} %bitcast.15), calls=%async_computation.1 | async-start | bytes 1048576 | tf_op jit(solution)/shard_map/all_to_all | solution.py:44
  68.4 10.9 %copy-start.9 = (f32[256,256]{1,0:T(8,128)S(1)}, f32[256,256]{1,0:T(8,128)}, u32[]{:S(2)}) copy-start(f32[256,256]{1,0:T(8,128)} %get-tuple-element.1045) | copy-start | bytes 786436
  69.7 20.2 %all-to-all-start.2 = ((f32[16,16,128]{2,1,0:T(8,128)}), f32[16,16,128]{2,1,0:T(8,128)S(1)}, u32[]{:S(2)}, u32[]{:S(2)}) async-start(f32[16,16,128]{2,1,0:T(8,128)} %bitcast_bitcast_fusion.1), calls=%async_computation.2 | async-start | bytes 262144 | tf_op jit(solution)/shard_map/all_to_all | solution.py:288
  79.3 10.6 %copy-start.16 = (pred[128]{0:T(512)(128)(4,1)S(1)}, pred[128]{0:T(512)(128)(4,1)}, u32[]{:S(2)}) copy-start(pred[128]{0:T(512)(128)(4,1)} %get-tuple-element.1078) | copy-start | bytes 388
  79.3 10.6 %copy-start.17 = (pred[128]{0:T(512)(128)(4,1)S(1)}, pred[128]{0:T(512)(128)(4,1)}, u32[]{:S(2)}) copy-start(pred[128]{0:T(512)(128)(4,1)} %get-tuple-element.1079) | copy-start | bytes 388
  89.9 7.7 %copy-start.6 = (f32[16,16,128]{2,1,0:T(8,128)}, f32[16,16,128]{2,1,0:T(8,128)S(1)}, u32[]{:S(2)}) copy-start(f32[16,16,128]{2,1,0:T(8,128)S(1)} %all-to-all-done.2) | copy-start | bytes 393220
  90.7 18.4 %all-to-all-start.3 = ((f32[32,16,128]{2,1,0:T(8,128)}), f32[32,16,128]{2,1,0:T(8,128)}, u32[]{:S(2)}, u32[]{:S(2)}) async-start(f32[32,16,128]{2,1,0:T(8,128)} %bitcast.21), calls=%async_computation.3 | async-start | bytes 524288 | tf_op jit(solution)/shard_map/all_to_all | solution.py:293
  97.6 3.1 %copy-start.10 = (f32[1,384,32]{1,2,0:T(8,128)S(1)}, f32[1,384,32]{1,2,0:T(8,128)}, u32[]{:S(2)}) copy-start(f32[1,384,32]{1,2,0:T(8,128)} %param.22) | copy-start | bytes 147460
  113.5 8.0 %copy-start.8 = (f32[64,384]{1,0:T(8,128)S(1)}, f32[64,384]{1,0:T(8,128)}, u32[]{:S(2)}) copy-start(f32[64,384]{1,0:T(8,128)} %fusion.51) | copy-start | bytes 294916
  113.5 16.6 %all-to-all-start.4 = ((f32[32,16,128]{2,1,0:T(8,128)}), f32[32,16,128]{2,1,0:T(8,128)S(1)}, u32[]{:S(2)}, u32[]{:S(2)}) async-start(f32[32,16,128]{2,1,0:T(8,128)} %bitcast.36), calls=%async_computation.4 | async-start | bytes 524288 | tf_op jit(solution)/shard_map/all_to_all | solution.py:44
  121.4 9.3 %copy-start.7 = (bf16[384,32]{1,0:T(8,128)(2,1)S(1)}, bf16[384,32]{1,0:T(8,128)(2,1)}, u32[]{:S(2)}) copy-start(bf16[384,32]{1,0:T(8,128)(2,1)} %convert_convert_fusion.6) | copy-start | bytes 73732
  121.5 9.3 %copy-start.18 = (pred[384]{0:T(512)(128)(4,1)S(1)}, pred[384]{0:T(512)(128)(4,1)}, u32[]{:S(2)}) copy-start(pred[384]{0:T(512)(128)(4,1)} %slice.216) | copy-start | bytes 1156

commit v7 on v6

--- a/solution.py
+++ b/solution.py
@@ -204,7 +204,7 @@
 def panel_places(col_slots, col_block, ratio, col_count, group, panel_cols, row_lists):
     width = panel_cols.shape[0]
     by_core = jnp.moveaxis(panel_cols.reshape(-1, 2, group), 1, 0).reshape(2, width // 2)
-    local = jnp.where(lax.axis_index(COL[1]) == 0, by_core, by_core[::-1]).reshape(width)
+    local = jnp.where(lax.axis_index(ROW[2]) == 0, by_core, by_core[::-1]).reshape(width)
     return pl.pallas_call(
         functools.partial(places_kernel, (col_block, ratio, col_slots, col_count)),
         out_shape=jax.ShapeDtypeStruct((8, width), jnp.int32),
@@ -239,34 +239,20 @@
     narrow_pick = one_hot(list_slot[:col_block], row_slots, jnp.bfloat16)
     packed = selected(thirds(factor, 1), narrow_pick, BY_FIRST)
 
-    core = lax.axis_index(ROW[2])
-    swap = [(0, 1), (1, 0)]
     copies = jnp.broadcast_to(packed, (lax.axis_size(ROW[:2]), *packed.shape))
-    this_half = lax.all_to_all(copies, ROW[:2], 0, 0, tiled=True)
-    this_half = this_half.reshape(width // 2, row_slots)
-    pair_axes = (ROW[2], COL[1])
-    near = lax.ppermute(this_half, pair_axes, [(1, 0), (2, 3)])
-    across = lax.ppermute(this_half, pair_axes, [(1, 2), (2, 1)])
-    that_half = lax.ppermute(this_half, ROW[2], swap)
-    same = core == side
-    own_lower = jnp.where(same, this_half, that_half)
-    lower = jnp.concatenate([own_lower, jnp.where(same, that_half, this_half)])
-    pair_lower = jnp.where(same, near, across)
+    own_half = lax.all_to_all(copies, ROW[:2], 0, 0, tiled=True)
+    own_half = own_half.reshape(width // 2, row_slots)
+    other_half = lax.ppermute(own_half, ROW[2], [(0, 1), (1, 0)])
+    lower = jnp.concatenate([own_half, other_half])
 
     narrow = dot(matrix, pick_cols).reshape(ratio, col_block, row_slots)
     dense = jnp.stack([dot(pick_rows[part], narrow[part], BY_FIRST) for part in range(ratio)])
-    owners = col_count // ratio
-    share = row_slots // owners
-    dense = jnp.moveaxis(dense.reshape(ratio, owners, share, row_slots), 0, 1)
+    share = row_slots // col_count
+    dense = jnp.moveaxis(dense.reshape(ratio, col_count, share, row_slots), 0, 1)
     dense = dense.reshape(ratio * row_slots, row_slots)
-    pair_dense = lax.ppermute(dense, COL[1], swap)
-
-    partial_value = -dot(
-        jnp.concatenate([dense, pair_dense], axis=1),
-        jnp.concatenate([own_lower, pair_lower], axis=1),
-        BY_LAST,
-    )
-    summed = sum_at_owner(partial_value.reshape(owners, ratio * share, width // 2), COL[0])
+
+    partial_value = -dot(dense, lower, BY_LAST)
+    summed = sum_at_owner(partial_value.reshape(col_count, ratio * share, width), COL)
 
     wide = ratio * row_k
     half_slots = col_slots // 2
@@ -277,7 +263,7 @@
     slot, local_slot = found[0], found[1]
 
     def route(places):
-        return one_hot(places[:, : width // 2].reshape(-1), row_count * wide, jnp.bfloat16)
+        return one_hot(places.reshape(-1), row_count * wide, jnp.bfloat16)
 
     to_rows = route(found[2:4])
     to_cols = route(found[4:6])
@@ -293,7 +279,6 @@
     arrived = lax.all_to_all(
         sent.reshape(col_count, share, wide), COL, 0, 0, tiled=True
     )
-    arrived = jnp.sum(arrived.reshape(owners, ratio, share, wide), axis=1)
     arrived = arrived.reshape(row_slots, wide).T
     upper, under = arrived[:row_k], arrived[row_k:]
     beside = jnp.where(side == 0, upper, under)
@@ -350,12 +335,8 @@
 
     fits = (jnp.max(found[6]) < col_slots) & (jnp.max(found[7]) <= row_slots)
 
-    zero = lax.shift_right_logical((received[0, 0, 0] > 0.0).astype(jnp.int32), 1)
-    late_factor = factor + zero.astype(jnp.float32)
-    late_dinv = dinv + zero.astype(jnp.float32)
-
     def again(carried):
-        general = general_panel(matrix, late_factor, late_dinv, panel_cols, row_in, col_in)
+        general = general_panel(matrix, factor, dinv, panel_cols, row_in, col_in)
         return jnp.zeros((), jnp.bool_), general
 
     return lax.while_loop(lambda carried: carried[0], again, (~fits, result))[1]

time: 134 us -> 128 us (0.955)
  starting transfers between devices: 54.5 us -> 39.6 us
  waiting for transfers between devices: 34.3 us -> 47.3 us
  other arithmetic: 11.3 us -> 8.41 us
    ppermute x4 -> x1, starting transfers between devices: 12.2 us -> 1.91 us  [panel_step(): other_half = lax.ppermute(own_half, ROW[2], [(0, 1), (1, 0)])]
    all_to_all x1, waiting for transfers between devices: 0.01 us -> 4.88 us  [panel_step(): own_half = lax.all_to_all(copies, ROW[:2], 0, 0, tiled=True)]
    all_to_all x1, starting transfers between devices: 9.59 us -> 5.04 us  [panel_step(): received = lax.all_to_all(jnp.moveaxis(chosen, 1, 0), ROW, 0, 0, tiled=True)]
    all_to_all x2, waiting for transfers between devices: 21.2 us -> 24.4 us  [sum_at_owner(): return jnp.sum(lax.all_to_all(blocks, axis, 0, 0, tiled=True), axis=0)]
    all_to_all x1, waiting for transfers between devices: 5.34 us -> 8.07 us  [panel_step(): lax.all_to_all(sent.reshape(col_count, share, wide), COL, 0, 0, tiled=True)]
    all_to_all x1, waiting for transfers between devices: 7.13 us -> 9.28 us  [panel_step(): received = lax.all_to_all(jnp.moveaxis(chosen, 1, 0), ROW, 0, 0, tiled=True)]
    select_n x2 -> x0, other arithmetic: 1.71 us -> none  [the longest x1 1.67 us: panel_step(): lower = jnp.concatenate([own_lower, jnp.where(same, that_half, this_half)])]
    add x2 -> x0, other arithmetic: 1.35 us -> none  [the longest x1 0.72 us: panel_step(): late_dinv = dinv + zero.astype(jnp.float32)]
  transfers between devices with their start and end apart: 9 -> 6, of which waited for: 5 -> 6; matrix products, arithmetic and copies ran while one was open for 18% -> 17% of each run, Pallas kernels for 2% -> 2%
where the time goes in v7:
time: 128 us; the launch traced here: 127 us
  waiting for transfers between devices  47.3 us (37%)
  starting transfers between devices  39.6 us (31%)
  matrix products  18.1 us (14%)
  other arithmetic  8.41 us (7%)
  local copies, waits for them, and re-layouts  7.45 us (6%)
  Pallas kernels  4.33 us (3%)
  between operations  1.62 us (1%)
    all_to_all x2, waiting for transfers between devices, sum_at_owner(): return jnp.sum(lax.all_to_all(blocks, axis, 0, 0, tiled=True), axis=0)  24.4 us
    all_to_all x2, starting transfers between devices, sum_at_owner(): return jnp.sum(lax.all_to_all(blocks, axis, 0, 0, tiled=True), axis=0)  17.1 us
    dot_general x15, matrix products, dot(): lax.dot_general(a, b, (dims, ((), ())), precision=HIGHEST, preferred_elem...  14.6 us
    all_to_all x1, waiting for transfers between devices, panel_step(): received = lax.all_to_all(jnp.moveaxis(chosen, 1, 0), ROW, 0, 0, tiled=True)  9.28 us
    all_to_all x1, starting transfers between devices, panel_step(): own_half = lax.all_to_all(copies, ROW[:2], 0, 0, tiled=True)  8.66 us
    all_to_all x1, waiting for transfers between devices, panel_step(): lax.all_to_all(sent.reshape(col_count, share, wide), COL, 0, 0, tiled=True)  8.07 us
    all_to_all x1, starting transfers between devices, panel_step(): lax.all_to_all(sent.reshape(col_count, share, wide), COL, 0, 0, tiled=True)  6.83 us
    all_to_all x1, starting transfers between devices, panel_step(): received = lax.all_to_all(jnp.moveaxis(chosen, 1, 0), ROW, 0, 0, tiled=True)  5.04 us
  transfers between devices with their start and end apart: 6, of which 6 were waited for; matrix products, arithmetic and copies ran while one was open for 17% of the time, Pallas kernels for 2%

profile of v7, /device:TPU:8, one launch (start us, length us, event | category | flops | bytes accessed | tf_op | source)
XLA Modules:
  0.0 126.7 jit_solution(1682281014992577724)
XLA Ops:
  0.0 0.9 reduce-precision_convert_fusion.3
  0.9 2.2 %block_slots.1 = (s32[16,128]{1,0:T(8,128)}, s32[16,128]{1,0:T(8,128)}) custom-call(s32[1,6144]{1,0:T(1,128)} %rows_ref.3, s32[1,512]{1,0:T(1,128)} %cols_ref.1), custom_call_target="tpu_custom_call" | custom-call | tf_op jit(solution)/shard_map/block_slots/pallas_call | solution.py:159
  3.2 0.8 slice_bitcast_fusion.4
  4.2 0.7 broadcast_in_dim.42
  4.9 8.7 %all-to-all-start = ((f32[8,32,256]{2,1,0:T(8,128)}), f32[8,32,256]{2,1,0:T(8,128)S(1)}, u32[]{:S(2)}, u32[]{:S(2)}) async-start(f32[8,32,256]{2,1,0:T(8,128)} %broadcast_in_dim.42), calls=%async_computation | async-start | bytes 524288 | tf_op jit(solution)/shard_map/all_to_all | solution.py:243
  13.9 0.9 convolution_bitcast_fusion.1
  14.8 0.5 convolution_bitcast_fusion.3
  15.3 0.6 broadcast.137
  15.9 0.7 reduce.5
  16.9 0.5 convolution_bitcast_fusion.2
  17.3 0.6 copy.49
  17.9 2.1 %panel_places.1 = s32[8,512]{1,0:T(8,128)} custom-call(s32[1,512]{1,0:T(1,128)S(1)} %copy-done.9, s32[1,512]{1,0:T(1,128)} %bitcast.131, s32[1,6144]{1,0:T(1,128)} %rows_ref.3), custom_call_target="tpu_custom_call" | custom-call | tf_op jit(solution)/shard_map/panel_places/pallas_call | solution.py:208
  20.0 0.6 fusion.108
  20.6 2.1 %fusion.106 = (s32[1,512]{1,0:T(1,128)S(1)}, s32[1,512]{1,0:T(1,128)}, s32[]{:T(128)}, s32[]{:T(128)}, s32[1,512]{1,0:T(1,128)S(1)}) fusion(s32[8,512]{1,0:T(8,128)} %panel_places.1, s32[]{:T(128)S(6)} %mul.83), kind=kLoop, calls=%fused_computation.201 | loop fusion | flops 1534 | bytes 14348 | tf_op jit(solution)/shard_map/slice | solution.py:263
  22.7 4.9 %all-to-all-done = f32[8,32,256]{2,1,0:T(8,128)S(1)} async-done(((f32[8,32,256]{2,1,0:T(8,128)}), f32[8,32,256]{2,1,0:T(8,128)S(1)}, u32[]{:S(2)}, u32[]{:S(2)}) %all-to-all-start) | async-done | bytes 262176 | tf_op jit(solution)/shard_map/all_to_all | solution.py:243
  27.6 1.9 %collective-permute-start.5 = (f32[256,256]{1,0:T(8,128)S(1)}, f32[256,256]{1,0:T(8,128)S(1)}, u32[]{:S(2)}, u32[]{:S(2)}) collective-permute-start(f32[256,256]{1,0:T(8,128)S(1)} %bitcast.123), channel_id=1, source_target_pairs={{0,32},{32,0},{1,33},{33,1},{2,34},{34,2},{3,35},{35,3},{4,36},{36... | collective-permute-start | bytes 786440 | tf_op jit(solution)/shard_map/ppermute | solution.py:245
  29.5 0.8 slice_bitcast_fusion.2
  30.3 0.7 collective-permute-done.5
  31.0 2.0 %convolution_negate_fusion.1 = f32[512,512]{1,0:T(8,128)} fusion(f32[512,256]{1,0:T(8,128)S(1)} %bitcast.116, f32[256,256]{1,0:T(8,128)S(1)} %collective-permute-done.5, f32[256,256]{1,0:T(8,128)S(1)} %bitcast.124), kind=kOutput, calls=%fused_computation.56 | convolution fusion | flops 805699584 | bytes 2097152 | tf_op jit(solution)/shard_map/dot_general | solution.py:22
  33.0 12.2 %all-to-all-start.1 = ((f32[32,16,512]{2,1,0:T(8,128)}), f32[32,16,512]{2,1,0:T(8,128)S(1)}, u32[]{:S(2)}, u32[]{:S(2)}) async-start(f32[32,16,512]{2,1,0:T(8,128)} %bitcast.14), calls=%async_computation.1 | async-start | bytes 2097152 | tf_op jit(solution)/shard_map/all_to_all | solution.py:44
  45.3 0.6 slice.208
  47.1 0.8 copy.45
  48.0 0.8 copy.47
  48.8 0.6 broadcast_compare_fusion.6
  49.4 0.3 fusion.47
  49.8 0.7 fusion.79
  50.5 0.9 iota_compare_fusion.5
  51.4 3.9 %fusion.31 = f32[1024,256]{1,0:T(8,128)} fusion(s32[512]{0:T(512)S(1)} %bitcast.134, f32[256,256]{1,0:T(8,128)} %copy-done.7, f32[256,256]{1,0:T(8,128)S(1)} %bitcast.125), kind=kOutput, calls=%fused_computation.54 | convolution fusion | flops 1611268096 | bytes 1574912 | tf_op jit(solution)/shard_map/dot_general | solution.py:22
  55.3 16.8 %all-to-all-done.1 = f32[32,16,512]{2,1,0:T(8,128)S(1)} async-done(((f32[32,16,512]{2,1,0:T(8,128)}), f32[32,16,512]{2,1,0:T(8,128)S(1)}, u32[]{:S(2)}, u32[]{:S(2)}) %all-to-all-start.1) | async-done | bytes 1048608 | tf_op jit(solution)/shard_map/all_to_all | solution.py:44
  72.1 0.8 fusion.27
  72.9 0.6 fusion.78
  73.5 5.0 %all-to-all-start.2 = ((f32[16,8,128]{2,1,0:T(8,128)}), f32[16,8,128]{2,1,0:T(8,128)S(1)}, u32[]{:S(2)}, u32[]{:S(2)}) async-start(f32[16,8,128]{2,1,0:T(8,128)} %fusion.78), calls=%async_computation.2 | async-start | bytes 131072 | tf_op jit(solution)/shard_map/all_to_all | solution.py:274
  78.6 0.8 fusion.28
  79.4 9.3 %all-to-all-done.2 = f32[16,8,128]{2,1,0:T(8,128)S(1)} async-done(((f32[16,8,128]{2,1,0:T(8,128)}), f32[16,8,128]{2,1,0:T(8,128)S(1)}, u32[]{:S(2)}, u32[]{:S(2)}) %all-to-all-start.2) | async-done | bytes 65568 | tf_op jit(solution)/shard_map/all_to_all | solution.py:274
  88.7 0.7 pad_maximum_fusion.4
  89.4 6.8 %all-to-all-start.3 = ((f32[32,8,128]{2,1,0:T(8,128)}), f32[32,8,128]{2,1,0:T(8,128)S(1)}, u32[]{:S(2)}, u32[]{:S(2)}) async-start(f32[32,8,128]{2,1,0:T(8,128)} %bitcast.23), calls=%async_computation.3 | async-start | bytes 262144 | tf_op jit(solution)/shard_map/all_to_all | solution.py:279
  96.2 1.3 %fusion.103 = (f32[32,1,16,256]{3,2,1,0:T(8,128)S(1)}, f32[32,1,16,256]{3,2,1,0:T(8,128)S(1)}) fusion(f32[32,2,16,256]{3,2,1,0:T(8,128)} %bitcast.120), kind=kLoop, calls=%fused_computation.198 | loop fusion | bytes 2097152 | tf_op jit(solution)/shard_map/slice | solution.py:289
  97.5 8.1 %all-to-all-done.3 = f32[32,8,128]{2,1,0:T(8,128)S(1)} async-done(((f32[32,8,128]{2,1,0:T(8,128)}), f32[32,8,128]{2,1,0:T(8,128)S(1)}, u32[]{:S(2)}, u32[]{:S(2)}) %all-to-all-start.3) | async-done | bytes 131104 | tf_op jit(solution)/shard_map/all_to_all | solution.py:279
  105.6 0.7 slice_select_fusion.1
  106.3 0.4 fusion.40
  106.7 1.7 %convolution_subtract_fusion = f32[512,128]{1,0:T(8,128)} fusion(f32[512,256]{1,0:T(8,128)S(1)} %bitcast.118, f32[512,256]{1,0:T(8,128)S(1)} %bitcast.117, f32[64,256]{0,1:T(8,128)S(1)} %get-tuple-element.1048, f32[512,64]{1,0:T(8,128)S(1)} %bitcast.122, f32[512,64]{1,0:T(8,128)S(1)} %bitcast.121), kind=kOutput, calls=%fused_computation.62 | convolution fusion | flops 403374080 | bytes 1638400 | tf_op jit(solution)/shard_map/dot_general | solution.py:22
  108.4 4.9 %all-to-all-start.4 = ((f32[32,16,128]{2,1,0:T(8,128)}), f32[32,16,128]{2,1,0:T(8,128)S(1)}, u32[]{:S(2)}, u32[]{:S(2)}) async-start(f32[32,16,128]{2,1,0:T(8,128)} %bitcast.37), calls=%async_computation.4 | async-start | bytes 524288 | tf_op jit(solution)/shard_map/all_to_all | solution.py:44
  113.3 1.2 fusion.42
  114.6 1.3 %fusion.38 = f32[384,32]{0,1:T(8,128)S(1)} fusion(pred[1152,256]{1,0:T(32,128)(4,1)S(1)} %iota_compare_fusion.4, f32[64,256]{0,1:T(8,128)} %get-tuple-element.1047), kind=kOutput, calls=%fused_computation.76 | convolution fusion | flops 37748736 | bytes 212992 | tf_op jit(solution)/shard_map/dot_general | solution.py:22
  116.0 0.4 fusion.53
  116.3 0.4 fusion.50
  116.7 7.6 %all-to-all-done.4 = f32[32,16,128]{2,1,0:T(8,128)S(1)} async-done(((f32[32,16,128]{2,1,0:T(8,128)}), f32[32,16,128]{2,1,0:T(8,128)S(1)}, u32[]{:S(2)}, u32[]{:S(2)}) %all-to-all-start.4) | async-done | bytes 262176 | tf_op jit(solution)/shard_map/all_to_all | solution.py:44
  125.0 1.7 %convolution_select_fusion.3 = f32[768,384]{1,0:T(8,128)} fusion(f32[768,384]{1,0:T(8,128)S(1)} %copy-done.1, f32[384,384]{1,0:T(8,128)S(1)} %fusion.50, f32[384,384]{1,0:T(8,128)S(1)} %fusion.53, pred[384]{0:T(512)(128)(4,1)S(1)} %slice.243, pred[384]{0:T(512)(128)(4,1)S(1)} %copy-done.17, pred[768]{0:T(1024)(128)(4,1)S(1)} %copy-done.13, ...), kind=kOutput, calls=%fused_computation.55 | convolution fusion | flops 58761216 | bytes 3713280 | tf_op jit(solution)/shard_map/dot_general | solution.py:327
  (54 shorter events, 1.8 us)
Async XLA Ops:
  0.0 13.9 %copy-start.1 = (f32[768,384]{1,0:T(8,128)S(1)}, f32[768,384]{1,0:T(8,128)}, u32[]{:S(2)}) copy-start(f32[768,384]{1,0:T(8,128)} %param.21) | copy-start | bytes 3538948
  3.2 10.4 %copy-start.11 = (s32[16,128]{1,0:T(8,128)S(1)}, s32[16,128]{1,0:T(8,128)}, u32[]{:S(2)}) copy-start(s32[16,128]{1,0:T(8,128)} %get-tuple-element.854) | copy-start | bytes 24580
  3.2 10.5 %copy-start.10 = (s32[16,128]{1,0:T(8,128)S(1)}, s32[16,128]{1,0:T(8,128)}, u32[]{:S(2)}) copy-start(s32[16,128]{1,0:T(8,128)} %get-tuple-element.853) | copy-start | bytes 24580
  4.9 22.7 %all-to-all-start = ((f32[8,32,256]{2,1,0:T(8,128)}), f32[8,32,256]{2,1,0:T(8,128)S(1)}, u32[]{:S(2)}, u32[]{:S(2)}) async-start(f32[8,32,256]{2,1,0:T(8,128)} %broadcast_in_dim.42), calls=%async_computation | async-start | bytes 524288 | tf_op jit(solution)/shard_map/all_to_all | solution.py:243
  13.9 2.0 %copy-start.9 = (s32[1,512]{1,0:T(1,128)S(1)}, s32[1,512]{1,0:T(1,128)}, u32[]{:S(2)}) copy-start(s32[1,512]{1,0:T(1,128)} %cols_ref.1) | copy-start | bytes 6148
  27.6 3.4 %collective-permute-start.5 = (f32[256,256]{1,0:T(8,128)S(1)}, f32[256,256]{1,0:T(8,128)S(1)}, u32[]{:S(2)}, u32[]{:S(2)}) collective-permute-start(f32[256,256]{1,0:T(8,128)S(1)} %bitcast.123), channel_id=1, source_target_pairs={{0,32},{32,0},{1,33},{33,1},{2,34},{34,2},{3,35},{35,3},{4,36},{36... | collective-permute-start | bytes 786440 | tf_op jit(solution)/shard_map/ppermute | solution.py:245
  31.0 2.0 %copy-start.7 = (f32[256,256]{1,0:T(8,128)}, f32[256,256]{1,0:T(8,128)S(1)}, u32[]{:S(2)}) copy-start(f32[256,256]{1,0:T(8,128)S(1)} %collective-permute-done.5) | copy-start | bytes 786436
  33.0 14.1 %copy-start.12 = (f32[1,16,512]{2,1,0:T(8,128)S(1)}, f32[1,16,512]{2,1,0:T(8,128)}, u32[]{:S(2)}) copy-start(f32[1,16,512]{2,1,0:T(8,128)} %param.23) | copy-start | bytes 98308
  33.0 15.0 %copy-start.8 = (f32[1,384,32]{1,2,0:T(8,128)S(1)}, f32[1,384,32]{1,2,0:T(8,128)}, u32[]{:S(2)}) copy-start(f32[1,384,32]{1,2,0:T(8,128)} %param.22) | copy-start | bytes 147460
  33.0 39.0 %all-to-all-start.1 = ((f32[32,16,512]{2,1,0:T(8,128)}), f32[32,16,512]{2,1,0:T(8,128)S(1)}, u32[]{:S(2)}, u32[]{:S(2)}) async-start(f32[32,16,512]{2,1,0:T(8,128)} %bitcast.14), calls=%async_computation.1 | async-start | bytes 2097152 | tf_op jit(solution)/shard_map/all_to_all | solution.py:44
  47.1 4.3 %copy-start.14 = (s32[1,512]{1,0:T(1,128)S(1)}, s32[1,512]{1,0:T(1,128)}, u32[]{:S(2)}) copy-start(s32[1,512]{1,0:T(1,128)} %get-tuple-element.1061) | copy-start | bytes 6148
  73.5 15.1 %all-to-all-start.2 = ((f32[16,8,128]{2,1,0:T(8,128)}), f32[16,8,128]{2,1,0:T(8,128)S(1)}, u32[]{:S(2)}, u32[]{:S(2)}) async-start(f32[16,8,128]{2,1,0:T(8,128)} %fusion.78), calls=%async_computation.2 | async-start | bytes 131072 | tf_op jit(solution)/shard_map/all_to_all | solution.py:274
  78.6 10.1 %copy-start.15 = (pred[128]{0:T(512)(128)(4,1)S(1)}, pred[128]{0:T(512)(128)(4,1)}, u32[]{:S(2)}) copy-start(pred[128]{0:T(512)(128)(4,1)} %get-tuple-element.1076) | copy-start | bytes 388
  78.6 10.1 %copy-start.16 = (pred[128]{0:T(512)(128)(4,1)S(1)}, pred[128]{0:T(512)(128)(4,1)}, u32[]{:S(2)}) copy-start(pred[128]{0:T(512)(128)(4,1)} %get-tuple-element.1077) | copy-start | bytes 388
  89.4 16.2 %all-to-all-start.3 = ((f32[32,8,128]{2,1,0:T(8,128)}), f32[32,8,128]{2,1,0:T(8,128)S(1)}, u32[]{:S(2)}, u32[]{:S(2)}) async-start(f32[32,8,128]{2,1,0:T(8,128)} %bitcast.23), calls=%async_computation.3 | async-start | bytes 262144 | tf_op jit(solution)/shard_map/all_to_all | solution.py:279
  106.7 9.2 %copy-start.6 = (pred[1152,32]{1,0:T(32,128)(4,1)S(1)}, pred[1152,32]{1,0:T(32,128)(4,1)}, u32[]{:S(2)}) copy-start(pred[1152,32]{1,0:T(32,128)(4,1)} %iota_compare_fusion.5) | copy-start | bytes 110596
  108.4 15.9 %all-to-all-start.4 = ((f32[32,16,128]{2,1,0:T(8,128)}), f32[32,16,128]{2,1,0:T(8,128)S(1)}, u32[]{:S(2)}, u32[]{:S(2)}) async-start(f32[32,16,128]{2,1,0:T(8,128)} %bitcast.37), calls=%async_computation.4 | async-start | bytes 524288 | tf_op jit(solution)/shard_map/all_to_all | solution.py:44
  115.9 9.1 %copy-start.13 = (pred[768]{0:T(1024)(128)(4,1)S(1)}, pred[768]{0:T(1024)(128)(4,1)}, u32[]{:S(2)}) copy-start(pred[768]{0:T(1024)(128)(4,1)} %get-tuple-element.1071) | copy-start | bytes 2308
  116.0 9.1 %copy-start.17 = (pred[384]{0:T(512)(128)(4,1)S(1)}, pred[384]{0:T(512)(128)(4,1)}, u32[]{:S(2)}) copy-start(pred[384]{0:T(512)(128)(4,1)} %slice.208) | copy-start | bytes 1156
